TPU v7x, 16 devices: a whole 2x2x2 slice. The times are simulated.
16 devices in a mesh: data: 16 (over z, y, x, core).
Axes of the slice: x: 2, y: 2, z: 2, core: 2. Of those that a mesh axis runs over, the one named last changes fastest.
Arguments:
- x_act: bfloat16 [64, 256, 1024], P('data')
- y_tgt: bfloat16 [64, 256, 1024], P('data')
- w_in: float32 [4, 1024, 4096], P(None, 'data')
- w_out: float32 [4, 4096, 1024], P(None, 'data')
Outputs:
- output 1: float32 [4, 1024, 4096], P(None, 'data')
- output 2: float32 [4, 4096, 1024], P(None, 'data')
- output 3: float32 [], replicated
All inputs are finite; a program needn't handle non-finite values.
Results may differ from a plain program's by a relative error of at most 0.00156061.
Values are sent between devices in bfloat16 or wider.
A program may use at most 1 GiB of HBM per device.

v0:
```python
import math
import jax
import jax.numpy as jnp
from jax import lax
from jax.sharding import PartitionSpec as P

RHO_FRAC = 0.1
LEARN_RATE = 0.5


def gelu_exact(values):
    return jax.nn.gelu(values, approximate=False)


def layer_forward(h_prev, w_in_l, w_out_l):
    z_pre = jnp.dot(h_prev, w_in_l, preferred_element_type=jnp.float32).astype(jnp.bfloat16)
    gelu_out = gelu_exact(z_pre.astype(jnp.float32)).astype(jnp.bfloat16)
    branch = jnp.dot(gelu_out, w_out_l, preferred_element_type=jnp.float32)
    return (h_prev.astype(jnp.float32) + branch).astype(jnp.bfloat16), z_pre, gelu_out


def contract_rows(left, right):
    return lax.dot_general(left, right, (((0,), (0,)), ((), ())), preferred_element_type=jnp.float32)


def contract_cols(left, right):
    return lax.dot_general(left, right, (((1,), (1,)), ((), ())), preferred_element_type=jnp.float32)


def scatter_mean(grad_full, groups):
    rows, columns = grad_full.shape
    received = lax.all_to_all(grad_full.astype(jnp.bfloat16), 'data', 0, 0, tiled=True)
    return jnp.sum(received.reshape(groups, rows // groups, columns), axis=0, dtype=jnp.float32) / groups


def sam_pass(x_tok, y_tok, w_in_sh, w_out_sh, groups):
    layers = w_in_sh.shape[0]
    tokens = x_tok.shape[0]
    w_in_full = []
    w_out_full = []
    saved = []
    h_cur = x_tok
    for layer in range(layers):
        w_in_full.append(lax.all_gather(w_in_sh[layer], 'data', axis=0, tiled=True))
        w_out_full.append(lax.all_gather(w_out_sh[layer], 'data', axis=0, tiled=True))
        h_next, z_pre, gelu_out = layer_forward(h_cur, w_in_full[layer], w_out_full[layer])
        saved.append((h_cur, z_pre, gelu_out))
        h_cur = h_next
    residual = h_cur.astype(jnp.float32) - y_tok.astype(jnp.float32)
    local_loss = 0.5 * jnp.sum(residual * residual) / tokens
    d_res = residual / tokens
    rows_in = [None] * layers
    rows_out = [None] * layers
    for layer in reversed(range(layers)):
        h_prev, z_pre, gelu_out = saved[layer]
        d_bf = d_res.astype(jnp.bfloat16)
        rows_out[layer] = scatter_mean(contract_rows(gelu_out, d_bf), groups)
        d_gelu = contract_cols(d_bf, w_out_full[layer])
        _, gelu_vjp = jax.vjp(gelu_exact, z_pre.astype(jnp.float32))
        d_pre = gelu_vjp(d_gelu)[0].astype(jnp.bfloat16)
        rows_in[layer] = scatter_mean(contract_rows(h_prev, d_pre), groups)
        if layer > 0:
            d_res = d_res + contract_cols(d_pre, w_in_full[layer])
    return local_loss, jnp.stack(rows_in), jnp.stack(rows_out)


def solution(mesh):
    groups = mesh.shape['data']

    def device_step(x_blk, y_blk, w_in_sh, w_out_sh):
        layers = w_in_sh.shape[0]
        model_dim = w_out_sh.shape[2]
        radius = RHO_FRAC * math.sqrt(layers * model_dim)
        x_tok = x_blk.reshape(-1, model_dim)
        y_tok = y_blk.reshape(-1, model_dim)
        _, g_in, g_out = sam_pass(x_tok, y_tok, w_in_sh.astype(jnp.bfloat16), w_out_sh.astype(jnp.bfloat16), groups)
        part_sq = jnp.sum(g_in * g_in) + jnp.sum(g_out * g_out)
        grad_norm = jnp.sqrt(lax.psum(part_sq, 'data'))
        scale_eps = radius / grad_norm
        pert_in = (w_in_sh + scale_eps * g_in).astype(jnp.bfloat16)
        pert_out = (w_out_sh + scale_eps * g_out).astype(jnp.bfloat16)
        pert_loss, gp_in, gp_out = sam_pass(x_tok, y_tok, pert_in, pert_out, groups)
        mean_loss = lax.psum(pert_loss, 'data') / groups
        return w_in_sh - LEARN_RATE * gp_in, w_out_sh - LEARN_RATE * gp_out, mean_loss

    return jax.shard_map(device_step, mesh=mesh,
                         in_specs=(P('data', None, None), P('data', None, None), P(None, 'data', None), P(None, 'data', None)),
                         out_specs=(P(None, 'data', None), P(None, 'data', None), P()),
                         check_vma=False)
```

profile of v0, /device:TPU:0, one launch (start us, length us, event | category | flops | bytes accessed | tf_op | source)
XLA Modules:
  0.0 2824.4 jit_solution(17603430698170326677)
XLA Ops:
  19.2 43.7 %all-gather.33.cloned.1.call-done = bf16[1,1024,4096]{2,1,0:T(8,128)(2,1)} async-done(((bf16[1,64,4096]{2,1,0:T(8,128)(2,1)}), bf16[1,1024,4096]{2,1,0:T(8,128)(2,1)}) %all-gather.33.cloned.1.call-update) | async-done | bytes 8388624 | tf_op jit(solution)/shard_map/all_gather | solution.py:44
  62.9 45.2 %fusion.90 = (f32[1024,4096]{1,0:T(8,128)}, bf16[1024,4096]{1,0:T(8,128)(2,1)}) fusion(bf16[1024,1024]{1,0:T(8,128)(2,1)S(1)} %bitcast.385, bf16[1,1024,4096]{2,1,0:T(8,128)(2,1)} %all-gather.33.cloned.1.call-done), kind=kOutput, calls=%fused_computation.114 | convolution fusion | flops 8858370048 | bytes 35651584 | tf_op jit(solution)/shard_map/dot_general | solution.py:16
  114.4 16.9 fusion.412
  131.3 34.0 %all-gather.37.cloned.1.call-done = bf16[1,1024,4096]{2,1,0:T(8,128)(2,1)} async-done(((bf16[1,64,4096]{2,1,0:T(8,128)(2,1)}), bf16[1,1024,4096]{2,1,0:T(8,128)(2,1)}) %all-gather.37.cloned.1.call-update) | async-done | bytes 8388624 | tf_op jit(solution)/shard_map/all_gather | solution.py:44
  165.3 46.7 %fusion.118 = (f32[1024,4096]{1,0:T(8,128)}, bf16[1024,4096]{1,0:T(8,128)(2,1)}) fusion(bf16[1024,1024]{1,0:T(8,128)(2,1)} %fusion.412, bf16[1,1024,4096]{2,1,0:T(8,128)(2,1)} %all-gather.37.cloned.1.call-done), kind=kOutput, calls=%fused_computation.142 | convolution fusion | flops 8858370048 | bytes 35651584 | tf_op jit(solution)/shard_map/dot_general | solution.py:16
  216.1 16.9 add_convert_fusion.9
  233.1 33.8 %all-gather.41.cloned.1.call-done = bf16[1,1024,4096]{2,1,0:T(8,128)(2,1)} async-done(((bf16[1,64,4096]{2,1,0:T(8,128)(2,1)}), bf16[1,1024,4096]{2,1,0:T(8,128)(2,1)}) %all-gather.41.cloned.1.call-update) | async-done | bytes 8388624 | tf_op jit(solution)/shard_map/all_gather | solution.py:44
  266.9 46.9 %fusion.146 = (f32[1024,4096]{1,0:T(8,128)}, bf16[1024,4096]{1,0:T(8,128)(2,1)}) fusion(bf16[1024,1024]{1,0:T(8,128)(2,1)} %add_convert_fusion.9, bf16[1,1024,4096]{2,1,0:T(8,128)(2,1)} %all-gather.41.cloned.1.call-done), kind=kOutput, calls=%fused_computation.170 | convolution fusion | flops 8858370048 | bytes 35651584 | tf_op jit(solution)/shard_map/dot_general | solution.py:16
  318.3 16.9 add_convert_fusion.8
  335.2 34.0 %all-gather.45.cloned.1.call-done = bf16[1,1024,4096]{2,1,0:T(8,128)(2,1)} async-done(((bf16[1,64,4096]{2,1,0:T(8,128)(2,1)}), bf16[1,1024,4096]{2,1,0:T(8,128)(2,1)}) %all-gather.45.cloned.1.call-update) | async-done | bytes 8388624 | tf_op jit(solution)/shard_map/all_gather | solution.py:44
  369.2 46.6 %fusion.174 = (f32[1024,4096]{1,0:T(8,128)}, bf16[1024,4096]{1,0:T(8,128)(2,1)}) fusion(bf16[1024,1024]{1,0:T(8,128)(2,1)} %add_convert_fusion.8, bf16[1,1024,4096]{2,1,0:T(8,128)(2,1)} %all-gather.45.cloned.1.call-done), kind=kOutput, calls=%fused_computation.198 | convolution fusion | flops 8858370048 | bytes 35651584 | tf_op jit(solution)/shard_map/dot_general | solution.py:16
  420.1 18.2 fusion.421
  438.3 19.9 convolution_convert_fusion.7
  461.9 23.2 fusion.41
  485.1 14.8 convolution_convert_fusion.11
  500.0 69.2 %all-to-all-done.7 = bf16[16,256,1024]{2,1,0:T(8,128)(2,1)} async-done(((bf16[16,256,1024]{2,1,0:T(8,128)(2,1)}), bf16[16,256,1024]{2,1,0:T(8,128)(2,1)}, u32[]{:S(2)}, u32[]{:S(2)}) %all-to-all-start.7) | async-done | bytes 8388640 | tf_op jit(solution)/shard_map/all_to_all | solution.py:32
  573.2 15.5 fusion.420
  588.7 17.1 convolution_convert_fusion.8
  605.9 74.3 %all-to-all-done.3 = bf16[16,64,4096]{2,1,0:T(8,128)(2,1)} async-done(((bf16[16,64,4096]{2,1,0:T(8,128)(2,1)}), bf16[16,64,4096]{2,1,0:T(8,128)(2,1)}, u32[]{:S(2)}, u32[]{:S(2)}) %all-to-all-start.3) | async-done | bytes 8388640 | tf_op jit(solution)/shard_map/all_to_all | solution.py:32
  684.4 22.4 fusion.48
  721.4 69.9 %all-to-all-done.6 = bf16[16,256,1024]{2,1,0:T(8,128)(2,1)} async-done(((bf16[16,256,1024]{2,1,0:T(8,128)(2,1)}), bf16[16,256,1024]{2,1,0:T(8,128)(2,1)}, u32[]{:S(2)}, u32[]{:S(2)}) %all-to-all-start.6) | async-done | bytes 8388640 | tf_op jit(solution)/shard_map/all_to_all | solution.py:32
  795.5 15.7 fusion.428
  811.2 17.1 convolution_convert_fusion.9
  828.3 74.1 %all-to-all-done.2 = bf16[16,64,4096]{2,1,0:T(8,128)(2,1)} async-done(((bf16[16,64,4096]{2,1,0:T(8,128)(2,1)}), bf16[16,64,4096]{2,1,0:T(8,128)(2,1)}, u32[]{:S(2)}, u32[]{:S(2)}) %all-to-all-start.2) | async-done | bytes 8388640 | tf_op jit(solution)/shard_map/all_to_all | solution.py:32
  906.8 22.3 fusion.55
  929.1 15.5 add_convert_fusion.6
  944.6 26.9 fusion.362
  971.6 42.2 %all-to-all-done.5 = bf16[16,256,1024]{2,1,0:T(8,128)(2,1)} async-done(((bf16[16,256,1024]{2,1,0:T(8,128)(2,1)}), bf16[16,256,1024]{2,1,0:T(8,128)(2,1)}, u32[]{:S(2)}, u32[]{:S(2)}) %all-to-all-start.5) | async-done | bytes 8388640 | tf_op jit(solution)/shard_map/all_to_all | solution.py:32
  1017.8 19.7 convolution_convert_fusion.10
  1037.4 87.2 %all-to-all-done = bf16[16,64,4096]{2,1,0:T(8,128)(2,1)} async-done(((bf16[16,64,4096]{2,1,0:T(8,128)(2,1)}), bf16[16,64,4096]{2,1,0:T(8,128)(2,1)}, u32[]{:S(2)}, u32[]{:S(2)}) %all-to-all-start) | async-done | bytes 8388640 | tf_op jit(solution)/shard_map/all_to_all | solution.py:32
  1143.3 92.4 %all-to-all-done.4 = bf16[16,256,1024]{2,1,0:T(8,128)(2,1)} async-done(((bf16[16,256,1024]{2,1,0:T(8,128)(2,1)}), bf16[16,256,1024]{2,1,0:T(8,128)(2,1)}, u32[]{:S(2)}, u32[]{:S(2)}) %all-to-all-start.4) | async-done | bytes 8388640 | tf_op jit(solution)/shard_map/all_to_all | solution.py:32
  1282.1 64.4 %all-to-all-done.1 = bf16[16,64,4096]{2,1,0:T(8,128)(2,1)} async-done(((bf16[16,64,4096]{2,1,0:T(8,128)(2,1)}), bf16[16,64,4096]{2,1,0:T(8,128)(2,1)}, u32[]{:S(2)}, u32[]{:S(2)}) %all-to-all-start.1) | async-done | bytes 8388640 | tf_op jit(solution)/shard_map/all_to_all | solution.py:32
  1359.9 33.0 %psum.14 = f32[]{:T(128)} all-reduce(f32[]{:T(128)S(6)} %add.62), channel_id=1, replica_groups=mesh['data'=16] {'data'}, use_global_device_ids=true, to_apply=%region_10.0 | all-reduce | flops 1 | bytes 8 | tf_op jit(solution)/shard_map/psum | solution.py:78
  1407.9 41.2 %all-gather.49.cloned.1.call-done = bf16[1,1024,4096]{2,1,0:T(8,128)(2,1)} async-done(((bf16[1,64,4096]{2,1,0:T(8,128)(2,1)}), bf16[1,1024,4096]{2,1,0:T(8,128)(2,1)}) %all-gather.49.cloned.1.call-update) | async-done | bytes 8388624 | tf_op jit(solution)/shard_map/all_gather | solution.py:44
  1449.1 46.4 %fusion.213 = (f32[1024,4096]{1,0:T(8,128)}, bf16[4096,1024]{0,1:T(8,128)(2,1)}) fusion(bf16[1024,1024]{1,0:T(8,128)(2,1)} %bitcast.384, bf16[1,1024,4096]{2,1,0:T(8,128)(2,1)} %all-gather.49.cloned.1.call-done), kind=kOutput, calls=%fused_computation.237 | convolution fusion | flops 8858370048 | bytes 35651584 | tf_op jit(solution)/shard_map/dot_general | solution.py:16
  1500.4 16.9 fusion.413
  1517.4 34.0 %all-gather.53.cloned.1.call-done = bf16[1,1024,4096]{2,1,0:T(8,128)(2,1)} async-done(((bf16[1,64,4096]{2,1,0:T(8,128)(2,1)}), bf16[1,1024,4096]{2,1,0:T(8,128)(2,1)}) %all-gather.53.cloned.1.call-update) | async-done | bytes 8388624 | tf_op jit(solution)/shard_map/all_gather | solution.py:44
  1551.3 46.7 %fusion.241 = (f32[1024,4096]{1,0:T(8,128)}, bf16[1024,4096]{1,0:T(8,128)(2,1)}) fusion(bf16[1024,1024]{1,0:T(8,128)(2,1)} %fusion.413, bf16[1,1024,4096]{2,1,0:T(8,128)(2,1)} %all-gather.53.cloned.1.call-done), kind=kOutput, calls=%fused_computation.265 | convolution fusion | flops 8858370048 | bytes 35651584 | tf_op jit(solution)/shard_map/dot_general | solution.py:16
  1602.1 16.9 add_convert_fusion.3
  1619.1 34.0 %all-gather.57.cloned.1.call-done = bf16[1,1024,4096]{2,1,0:T(8,128)(2,1)} async-done(((bf16[1,64,4096]{2,1,0:T(8,128)(2,1)}), bf16[1,1024,4096]{2,1,0:T(8,128)(2,1)}) %all-gather.57.cloned.1.call-update) | async-done | bytes 8388624 | tf_op jit(solution)/shard_map/all_gather | solution.py:44
  1653.1 46.9 %fusion.269 = (f32[1024,4096]{1,0:T(8,128)}, bf16[1024,4096]{1,0:T(8,128)(2,1)}) fusion(bf16[1024,1024]{1,0:T(8,128)(2,1)} %add_convert_fusion.3, bf16[1,1024,4096]{2,1,0:T(8,128)(2,1)} %all-gather.57.cloned.1.call-done), kind=kOutput, calls=%fused_computation.293 | convolution fusion | flops 8858370048 | bytes 35651584 | tf_op jit(solution)/shard_map/dot_general | solution.py:16
  1704.5 16.9 add_convert_fusion.2
  1721.4 33.8 %all-gather.61.cloned.1.call-done = bf16[1,1024,4096]{2,1,0:T(8,128)(2,1)} async-done(((bf16[1,64,4096]{2,1,0:T(8,128)(2,1)}), bf16[1,1024,4096]{2,1,0:T(8,128)(2,1)}) %all-gather.61.cloned.1.call-update) | async-done | bytes 8388624 | tf_op jit(solution)/shard_map/all_gather | solution.py:44
  1755.2 46.6 %fusion.297 = (f32[1024,4096]{1,0:T(8,128)}, bf16[1024,4096]{1,0:T(8,128)(2,1)}) fusion(bf16[1024,1024]{1,0:T(8,128)(2,1)} %add_convert_fusion.2, bf16[1,1024,4096]{2,1,0:T(8,128)(2,1)} %all-gather.61.cloned.1.call-done), kind=kOutput, calls=%fused_computation.321 | convolution fusion | flops 8858370048 | bytes 35651584 | tf_op jit(solution)/shard_map/dot_general | solution.py:16
  1806.0 19.0 multiply_reduce_fusion
  1825.1 19.9 convolution_convert_fusion
  1848.7 23.2 fusion.20
  1886.7 69.2 %all-to-all-done.15 = bf16[16,256,1024]{2,1,0:T(8,128)(2,1)} async-done(((bf16[16,256,1024]{2,1,0:T(8,128)(2,1)}), bf16[16,256,1024]{2,1,0:T(8,128)(2,1)}, u32[]{:S(2)}, u32[]{:S(2)}) %all-to-all-start.15) | async-done | bytes 8388640 | tf_op jit(solution)/shard_map/all_to_all | solution.py:32
  1960.0 15.5 fusion.418
  1975.5 17.1 convolution_convert_fusion.1
  1992.6 74.3 %all-to-all-done.11 = bf16[16,64,4096]{2,1,0:T(8,128)(2,1)} async-done(((bf16[16,64,4096]{2,1,0:T(8,128)(2,1)}), bf16[16,64,4096]{2,1,0:T(8,128)(2,1)}, u32[]{:S(2)}, u32[]{:S(2)}) %all-to-all-start.11) | async-done | bytes 8388640 | tf_op jit(solution)/shard_map/all_to_all | solution.py:32
  2071.1 22.4 fusion.27
  2108.1 69.9 %all-to-all-done.14 = bf16[16,256,1024]{2,1,0:T(8,128)(2,1)} async-done(((bf16[16,256,1024]{2,1,0:T(8,128)(2,1)}), bf16[16,256,1024]{2,1,0:T(8,128)(2,1)}, u32[]{:S(2)}, u32[]{:S(2)}) %all-to-all-start.14) | async-done | bytes 8388640 | tf_op jit(solution)/shard_map/all_to_all | solution.py:32
  2182.3 15.7 fusion.443
  2197.9 17.1 convolution_convert_fusion.2
  2215.0 74.1 %all-to-all-done.10 = bf16[16,64,4096]{2,1,0:T(8,128)(2,1)} async-done(((bf16[16,64,4096]{2,1,0:T(8,128)(2,1)}), bf16[16,64,4096]{2,1,0:T(8,128)(2,1)}, u32[]{:S(2)}, u32[]{:S(2)}) %all-to-all-start.10) | async-done | bytes 8388640 | tf_op jit(solution)/shard_map/all_to_all | solution.py:32
  2293.6 22.3 fusion.34
  2315.9 15.5 add_convert_fusion
  2331.4 26.9 fusion.365
  2358.3 42.2 %all-to-all-done.13 = bf16[16,256,1024]{2,1,0:T(8,128)(2,1)} async-done(((bf16[16,256,1024]{2,1,0:T(8,128)(2,1)}), bf16[16,256,1024]{2,1,0:T(8,128)(2,1)}, u32[]{:S(2)}, u32[]{:S(2)}) %all-to-all-start.13) | async-done | bytes 8388640 | tf_op jit(solution)/shard_map/all_to_all | solution.py:32
  2404.5 19.7 convolution_convert_fusion.3
  2424.2 87.2 %all-to-all-done.8 = bf16[16,64,4096]{2,1,0:T(8,128)(2,1)} async-done(((bf16[16,64,4096]{2,1,0:T(8,128)(2,1)}), bf16[16,64,4096]{2,1,0:T(8,128)(2,1)}, u32[]{:S(2)}, u32[]{:S(2)}) %all-to-all-start.8) | async-done | bytes 8388640 | tf_op jit(solution)/shard_map/all_to_all | solution.py:32
  2530.0 92.4 %all-to-all-done.12 = bf16[16,256,1024]{2,1,0:T(8,128)(2,1)} async-done(((bf16[16,256,1024]{2,1,0:T(8,128)(2,1)}), bf16[16,256,1024]{2,1,0:T(8,128)(2,1)}, u32[]{:S(2)}, u32[]{:S(2)}) %all-to-all-start.12) | async-done | bytes 8388640 | tf_op jit(solution)/shard_map/all_to_all | solution.py:32
  2627.0 133.0 %psum.15 = f32[]{:T(128)} all-reduce(f32[]{:T(128)S(6)} %div.130), channel_id=1, replica_groups=mesh['data'=16] {'data'}, use_global_device_ids=true, to_apply=%region_20.0 | all-reduce | flops 1 | bytes 8 | tf_op jit(solution)/shard_map/psum | solution.py:83
  (148 shorter events, 311.5 us)
Async XLA Ops:
  7.2 55.7 %copy-start.7 = (bf16[4,256,1024]{2,1,0:T(8,128)(2,1)S(1)}, bf16[4,256,1024]{2,1,0:T(8,128)(2,1)}, u32[]{:S(2)}) copy-start(bf16[4,256,1024]{2,1,0:T(8,128)(2,1)} %param.4) | copy-start | bytes 6291460
  7.2 55.7 %all-gather.33.cloned.1.call-start = ((), (), s32[]{:S(2)}) async-start(), calls=%async_computation.16 | async-start | bytes 8912896 | tf_op jit(solution)/shard_map/all_gather | solution.py:44
  11.2 103.1 %all-gather.35.cloned.1.call-start = ((), (), s32[]{:S(2)}) async-start(), calls=%async_computation.17 | async-start | bytes 8912896 | tf_op jit(solution)/shard_map/all_gather | solution.py:45
  15.2 150.1 %all-gather.37.cloned.1.call-start = ((), (), s32[]{:S(2)}) async-start(), calls=%async_computation.18 | async-start | bytes 8912896 | tf_op jit(solution)/shard_map/all_gather | solution.py:44
  15.9 200.2 %all-gather.39.cloned.1.call-start = ((), (), s32[]{:S(2)}) async-start(), calls=%async_computation.19 | async-start | bytes 8912896 | tf_op jit(solution)/shard_map/all_gather | solution.py:45
  16.5 250.4 %all-gather.41.cloned.1.call-start = ((), (), s32[]{:S(2)}) async-start(), calls=%async_computation.20 | async-start | bytes 8912896 | tf_op jit(solution)/shard_map/all_gather | solution.py:44
  17.1 301.2 %all-gather.43.cloned.1.call-start = ((), (), s32[]{:S(2)}) async-start(), calls=%async_computation.21 | async-start | bytes 8912896 | tf_op jit(solution)/shard_map/all_gather | solution.py:45
  17.7 351.5 %all-gather.45.cloned.1.call-start = ((), (), s32[]{:S(2)}) async-start(), calls=%async_computation.22 | async-start | bytes 8912896 | tf_op jit(solution)/shard_map/all_gather | solution.py:44
  18.4 401.7 %all-gather.47.cloned.1.call-start = ((), (), s32[]{:S(2)}) async-start(), calls=%async_computation.23 | async-start | bytes 8912896 | tf_op jit(solution)/shard_map/all_gather | solution.py:45
  165.3 50.8 %copy-start.11 = (bf16[1024,1024]{1,0:T(8,128)(2,1)S(1)}, bf16[1024,1024]{1,0:T(8,128)(2,1)}, u32[]{:S(2)}) copy-start(bf16[1024,1024]{1,0:T(8,128)(2,1)} %fusion.412) | copy-start | bytes 6291460
  266.9 51.4 %copy-start.15 = (bf16[1024,1024]{1,0:T(8,128)(2,1)S(1)}, bf16[1024,1024]{1,0:T(8,128)(2,1)}, u32[]{:S(2)}) copy-start(bf16[1024,1024]{1,0:T(8,128)(2,1)} %add_convert_fusion.9) | copy-start | bytes 6291460
  369.2 50.9 %copy-start.5 = (bf16[4,256,1024]{2,1,0:T(8,128)(2,1)S(1)}, bf16[4,256,1024]{2,1,0:T(8,128)(2,1)}, u32[]{:S(2)}) copy-start(bf16[4,256,1024]{2,1,0:T(8,128)(2,1)} %param.5) | copy-start | bytes 6291460
  458.2 111.0 %all-to-all-start.7 = ((bf16[16,256,1024]{2,1,0:T(8,128)(2,1)}), bf16[16,256,1024]{2,1,0:T(8,128)(2,1)}, u32[]{:S(2)}, u32[]{:S(2)}) async-start(bf16[16,256,1024]{2,1,0:T(8,128)(2,1)} %bitcast.380), calls=%async_computation.7 | async-start | bytes 16777216 | tf_op jit(solution)/shard_map/all_to_all | solution.py:32
  569.2 111.0 %all-to-all-start.3 = ((bf16[16,64,4096]{2,1,0:T(8,128)(2,1)}), bf16[16,64,4096]{2,1,0:T(8,128)(2,1)}, u32[]{:S(2)}, u32[]{:S(2)}) async-start(bf16[16,64,4096]{2,1,0:T(8,128)(2,1)} %bitcast.370), calls=%async_computation.3 | async-start | bytes 16777216 | tf_op jit(solution)/shard_map/all_to_all | solution.py:32
  680.2 111.1 %all-to-all-start.6 = ((bf16[16,256,1024]{2,1,0:T(8,128)(2,1)}), bf16[16,256,1024]{2,1,0:T(8,128)(2,1)}, u32[]{:S(2)}, u32[]{:S(2)}) async-start(bf16[16,256,1024]{2,1,0:T(8,128)(2,1)} %bitcast.371), calls=%async_computation.6 | async-start | bytes 16777216 | tf_op jit(solution)/shard_map/all_to_all | solution.py:32
  684.4 22.5 copy-start.16
  791.3 111.1 %all-to-all-start.2 = ((bf16[16,64,4096]{2,1,0:T(8,128)(2,1)}), bf16[16,64,4096]{2,1,0:T(8,128)(2,1)}, u32[]{:S(2)}, u32[]{:S(2)}) async-start(bf16[16,64,4096]{2,1,0:T(8,128)(2,1)} %bitcast.372), calls=%async_computation.2 | async-start | bytes 16777216 | tf_op jit(solution)/shard_map/all_to_all | solution.py:32
  902.4 111.3 %all-to-all-start.5 = ((bf16[16,256,1024]{2,1,0:T(8,128)(2,1)}), bf16[16,256,1024]{2,1,0:T(8,128)(2,1)}, u32[]{:S(2)}, u32[]{:S(2)}) async-start(bf16[16,256,1024]{2,1,0:T(8,128)(2,1)} %bitcast.368), calls=%async_computation.5 | async-start | bytes 16777216 | tf_op jit(solution)/shard_map/all_to_all | solution.py:32
  929.1 15.5 copy-start.8
  971.6 46.2 %copy-start.19 = (bf16[1024,1024]{1,0:T(8,128)(2,1)S(1)}, bf16[1024,1024]{1,0:T(8,128)(2,1)}, u32[]{:S(2)}) copy-start(bf16[1024,1024]{1,0:T(8,128)(2,1)} %add_convert_fusion.6) | copy-start | bytes 6291460
  1013.7 110.9 %all-to-all-start = ((bf16[16,64,4096]{2,1,0:T(8,128)(2,1)}), bf16[16,64,4096]{2,1,0:T(8,128)(2,1)}, u32[]{:S(2)}, u32[]{:S(2)}) async-start(bf16[16,64,4096]{2,1,0:T(8,128)(2,1)} %bitcast.378), calls=%async_computation | async-start | bytes 16777216 | tf_op jit(solution)/shard_map/all_to_all | solution.py:32
  1037.4 91.3 %copy-start.12 = (bf16[1024,1024]{1,0:T(8,128)(2,1)S(1)}, bf16[1024,1024]{1,0:T(8,128)(2,1)}, u32[]{:S(2)}) copy-start(bf16[1024,1024]{1,0:T(8,128)(2,1)} %fusion.412) | copy-start | bytes 6291460
  1124.7 110.9 %all-to-all-start.4 = ((bf16[16,256,1024]{2,1,0:T(8,128)(2,1)}), bf16[16,256,1024]{2,1,0:T(8,128)(2,1)}, u32[]{:S(2)}, u32[]{:S(2)}) async-start(bf16[16,256,1024]{2,1,0:T(8,128)(2,1)} %bitcast.373), calls=%async_computation.4 | async-start | bytes 16777216 | tf_op jit(solution)/shard_map/all_to_all | solution.py:32
  1235.6 110.9 %all-to-all-start.1 = ((bf16[16,64,4096]{2,1,0:T(8,128)(2,1)}), bf16[16,64,4096]{2,1,0:T(8,128)(2,1)}, u32[]{:S(2)}, u32[]{:S(2)}) async-start(bf16[16,64,4096]{2,1,0:T(8,128)(2,1)} %bitcast.367), calls=%async_computation.1 | async-start | bytes 16777216 | tf_op jit(solution)/shard_map/all_to_all | solution.py:32
  1239.6 209.4 %all-gather.49.cloned.1.call-start = ((), (), s32[]{:S(2)}) async-start(), calls=%async_computation.24 | async-start | bytes 8912896 | tf_op jit(solution)/shard_map/all_gather | solution.py:44
  1351.7 3.4 copy-start.1
  1399.1 101.3 %all-gather.51.cloned.1.call-start = ((), (), s32[]{:S(2)}) async-start(), calls=%async_computation.25 | async-start | bytes 8912896 | tf_op jit(solution)/shard_map/all_gather | solution.py:45
  1404.1 147.3 %all-gather.53.cloned.1.call-start = ((), (), s32[]{:S(2)}) async-start(), calls=%async_computation.26 | async-start | bytes 8912896 | tf_op jit(solution)/shard_map/all_gather | solution.py:44
  1404.8 197.3 %all-gather.55.cloned.1.call-start = ((), (), s32[]{:S(2)}) async-start(), calls=%async_computation.27 | async-start | bytes 8912896 | tf_op jit(solution)/shard_map/all_gather | solution.py:45
  1405.4 247.7 %all-gather.57.cloned.1.call-start = ((), (), s32[]{:S(2)}) async-start(), calls=%async_computation.28 | async-start | bytes 8912896 | tf_op jit(solution)/shard_map/all_gather | solution.py:44
  1406.1 298.3 %all-gather.59.cloned.1.call-start = ((), (), s32[]{:S(2)}) async-start(), calls=%async_computation.29 | async-start | bytes 8912896 | tf_op jit(solution)/shard_map/all_gather | solution.py:45
  1406.7 348.5 %all-gather.61.cloned.1.call-start = ((), (), s32[]{:S(2)}) async-start(), calls=%async_computation.30 | async-start | bytes 8912896 | tf_op jit(solution)/shard_map/all_gather | solution.py:44
  1407.3 398.7 %all-gather.63.cloned.1.call-start = ((), (), s32[]{:S(2)}) async-start(), calls=%async_computation.31 | async-start | bytes 8912896 | tf_op jit(solution)/shard_map/all_gather | solution.py:45
  1449.1 51.4 %copy-start.9 = (bf16[4,256,1024]{2,1,0:T(8,128)(2,1)S(1)}, bf16[4,256,1024]{2,1,0:T(8,128)(2,1)}, u32[]{:S(2)}) copy-start(bf16[4,256,1024]{2,1,0:T(8,128)(2,1)} %param.4) | copy-start | bytes 6291460
  1551.3 50.8 %copy-start.13 = (bf16[1024,1024]{1,0:T(8,128)(2,1)S(1)}, bf16[1024,1024]{1,0:T(8,128)(2,1)}, u32[]{:S(2)}) copy-start(bf16[1024,1024]{1,0:T(8,128)(2,1)} %fusion.413) | copy-start | bytes 6291460
  1653.1 51.4 %copy-start.17 = (bf16[1024,1024]{1,0:T(8,128)(2,1)S(1)}, bf16[1024,1024]{1,0:T(8,128)(2,1)}, u32[]{:S(2)}) copy-start(bf16[1024,1024]{1,0:T(8,128)(2,1)} %add_convert_fusion.3) | copy-start | bytes 6291460
  1755.2 50.8 %copy-start.6 = (bf16[4,256,1024]{2,1,0:T(8,128)(2,1)S(1)}, bf16[4,256,1024]{2,1,0:T(8,128)(2,1)}, u32[]{:S(2)}) copy-start(bf16[4,256,1024]{2,1,0:T(8,128)(2,1)} %param.5) | copy-start | bytes 6291460
  1844.9 111.0 %all-to-all-start.15 = ((bf16[16,256,1024]{2,1,0:T(8,128)(2,1)}), bf16[16,256,1024]{2,1,0:T(8,128)(2,1)}, u32[]{:S(2)}, u32[]{:S(2)}) async-start(bf16[16,256,1024]{2,1,0:T(8,128)(2,1)} %bitcast.381), calls=%async_computation.15 | async-start | bytes 16777216 | tf_op jit(solution)/shard_map/all_to_all | solution.py:32
  1955.9 111.0 %all-to-all-start.11 = ((bf16[16,64,4096]{2,1,0:T(8,128)(2,1)}), bf16[16,64,4096]{2,1,0:T(8,128)(2,1)}, u32[]{:S(2)}, u32[]{:S(2)}) async-start(bf16[16,64,4096]{2,1,0:T(8,128)(2,1)} %bitcast.374), calls=%async_computation.11 | async-start | bytes 16777216 | tf_op jit(solution)/shard_map/all_to_all | solution.py:32
  2066.9 111.1 %all-to-all-start.14 = ((bf16[16,256,1024]{2,1,0:T(8,128)(2,1)}), bf16[16,256,1024]{2,1,0:T(8,128)(2,1)}, u32[]{:S(2)}, u32[]{:S(2)}) async-start(bf16[16,256,1024]{2,1,0:T(8,128)(2,1)} %bitcast.375), calls=%async_computation.14 | async-start | bytes 16777216 | tf_op jit(solution)/shard_map/all_to_all | solution.py:32
  2071.1 22.5 copy-start.18
  2178.0 111.1 %all-to-all-start.10 = ((bf16[16,64,4096]{2,1,0:T(8,128)(2,1)}), bf16[16,64,4096]{2,1,0:T(8,128)(2,1)}, u32[]{:S(2)}, u32[]{:S(2)}) async-start(bf16[16,64,4096]{2,1,0:T(8,128)(2,1)} %bitcast.376), calls=%async_computation.10 | async-start | bytes 16777216 | tf_op jit(solution)/shard_map/all_to_all | solution.py:32
  2289.2 111.3 %all-to-all-start.13 = ((bf16[16,256,1024]{2,1,0:T(8,128)(2,1)}), bf16[16,256,1024]{2,1,0:T(8,128)(2,1)}, u32[]{:S(2)}, u32[]{:S(2)}) async-start(bf16[16,256,1024]{2,1,0:T(8,128)(2,1)} %bitcast.369), calls=%async_computation.13 | async-start | bytes 16777216 | tf_op jit(solution)/shard_map/all_to_all | solution.py:32
  2315.9 15.5 copy-start.10
  2358.3 46.2 %copy-start.20 = (bf16[1024,1024]{1,0:T(8,128)(2,1)S(1)}, bf16[1024,1024]{1,0:T(8,128)(2,1)}, u32[]{:S(2)}) copy-start(bf16[1024,1024]{1,0:T(8,128)(2,1)} %add_convert_fusion) | copy-start | bytes 6291460
  2400.5 110.9 %all-to-all-start.8 = ((bf16[16,64,4096]{2,1,0:T(8,128)(2,1)}), bf16[16,64,4096]{2,1,0:T(8,128)(2,1)}, u32[]{:S(2)}, u32[]{:S(2)}) async-start(bf16[16,64,4096]{2,1,0:T(8,128)(2,1)} %bitcast.379), calls=%async_computation.8 | async-start | bytes 16777216 | tf_op jit(solution)/shard_map/all_to_all | solution.py:32
  2424.2 91.2 %copy-start.14 = (bf16[1024,1024]{1,0:T(8,128)(2,1)S(1)}, bf16[1024,1024]{1,0:T(8,128)(2,1)}, u32[]{:S(2)}) copy-start(bf16[1024,1024]{1,0:T(8,128)(2,1)} %fusion.413) | copy-start | bytes 6291460
  2511.4 110.9 %all-to-all-start.12 = ((bf16[16,256,1024]{2,1,0:T(8,128)(2,1)}), bf16[16,256,1024]{2,1,0:T(8,128)(2,1)}, u32[]{:S(2)}, u32[]{:S(2)}) async-start(bf16[16,256,1024]{2,1,0:T(8,128)(2,1)} %bitcast.377), calls=%async_computation.12 | async-start | bytes 16777216 | tf_op jit(solution)/shard_map/all_to_all | solution.py:32
  2622.4 180.4 %all-to-all-start.9 = ((bf16[16,64,4096]{2,1,0:T(8,128)(2,1)}), bf16[16,64,4096]{2,1,0:T(8,128)(2,1)}, u32[]{:S(2)}, u32[]{:S(2)}) async-start(bf16[16,64,4096]{2,1,0:T(8,128)(2,1)} %bitcast.366), calls=%async_computation.9 | async-start | bytes 16777216 | tf_op jit(solution)/shard_map/all_to_all | solution.py:32
  2802.8 10.9 copy-start
  2802.8 10.9 copy-start.2
  2802.8 10.9 copy-start.3
  2802.8 10.9 copy-start.4
Sparse Core Ops, SparseCore 0:
  11.4 51.4 all-gather.32
  65.7 48.6 all-gather.34
  116.6 48.6 all-gather.36
  167.4 48.6 all-gather.38
  218.2 48.6 all-gather.40
  269.6 48.6 all-gather.42
  320.5 48.6 all-gather.44
  371.4 48.6 all-gather.46
  1399.2 49.8 all-gather.48
  1451.7 48.6 all-gather.50
  1502.7 48.6 all-gather.52
  1553.4 48.6 all-gather.54
  1604.4 48.6 all-gather.56
  1655.7 48.6 all-gather.58
  1706.5 48.6 all-gather.60
  1757.3 48.6 all-gather.62
where the time goes:
time: 2830 us; the launch traced here: 2820 us
  waiting for transfers between devices  1420 us (50%)
  matrix products  1030 us (36%)
  blocking collectives  166 us (6%)
  other arithmetic  122 us (4%)
  starting transfers between devices  66.4 us (2%)
    all_to_all x16, waiting for transfers between devices, scatter_mean(): lax.all_to_all(grad_full.astype(jnp.bfloat16), 'data', 0, 0, tiled=True)  1080 us
    dot_general x8, matrix products, layer_forward(): jnp.dot(h_prev, w_in_l, preferred_element_type=jnp.float32)  372 us
    dot_general x16, matrix products, contract_rows(): lax.dot_general(left, right, (((0,), (0,)), ((), ())), preferred_element_...  289 us
    all_gather x8, waiting for transfers between devices, sam_pass(): w_in_full.append(lax.all_gather(w_in_sh[layer], 'data', axis=0, tiled=True))  289 us
    dot_general x12, matrix products, contract_cols(): lax.dot_general(left, right, (((1,), (1,)), ((), ())), preferred_element_...  229 us
    dot_general x8, matrix products, layer_forward(): branch = jnp.dot(gelu_out, w_out_l, preferred_element_type=jnp.float32)  139 us
    psum x1, blocking collectives, device_step(): mean_loss = lax.psum(pert_loss, 'data') / groups  133 us
    reduce_sum x16, other arithmetic, scatter_mean(): jnp.sum(received.reshape(groups, rows // groups, columns), axis=0, dtype=...  85.5 us
  transfers between devices with their start and end apart: 32, of which 31 were waited for; matrix products, arithmetic and copies ran while one was open for 37% of the time, Pallas kernels for 0%

commit v1 on v0

v1 whole, which is shorter than its diff:
```python
import functools
import math
import jax
import jax.numpy as jnp
from jax import lax
from jax.experimental import pallas as pl
from jax.experimental.pallas import tpu as pltpu
from jax.sharding import PartitionSpec as P

RHO_FRAC = 0.1
LEARN_RATE = 0.5
BF = jnp.bfloat16
F32 = jnp.float32
MESH = pl.DeviceIdType.MESH
SQRT_HALF = math.sqrt(0.5)
DENSITY = 1.0 / math.sqrt(2.0 * math.pi)
VMEM_LIMIT = 63 * 2 ** 20
NT = (((1,), (1,)), ((), ()))
CORE, AX_X, AX_Y, AX_Z = 1, 2, 4, 8
COLOR_ORDERS = ((AX_X, AX_Y, AX_Z), (AX_Y, AX_Z, AX_X), (AX_Z, AX_X, AX_Y))
ANY = pl.BlockSpec(memory_space=pl.ANY)


def flip(dev, bit):
    return dev + bit * (1 - 2 * ((dev // bit) % 2))


def flips(dev, mask):
    for bit in (1, 2, 4, 8):
        if mask & bit:
            dev = flip(dev, bit)
    return dev


def greet_neighbours():
    me = lax.axis_index('data')
    barrier = pltpu.get_barrier_semaphore()
    for bit in (CORE, AX_X, AX_Y, AX_Z):
        pl.semaphore_signal(barrier, inc=1, device_id=(flip(me, bit),), device_id_type=MESH)
    pl.semaphore_wait(barrier, 4)


class Gather:
    def __init__(self, shard, full, pieces, recv, send, own_vmem, own_sem):
        self.shard, self.full, self.pieces = shard, full, pieces
        self.recv, self.send = recv, send
        self.own_vmem, self.own_sem = own_vmem, own_sem
        self.me = lax.axis_index('data')

    def piece(self, origin_mask, color):
        rows, cols = self.pieces[color]
        if origin_mask == 0:
            return self.shard.at[rows, cols]
        return self.full.at[flips(self.me, origin_mask), rows, cols]

    def push(self, origin_mask, color, bit, sem_index, send_index):
        rows, cols = self.pieces[color]
        pltpu.make_async_remote_copy(
            src_ref=self.piece(origin_mask, color),
            dst_ref=self.full.at[flips(self.me, origin_mask), rows, cols],
            send_sem=self.send.at[send_index], recv_sem=self.recv.at[sem_index],
            device_id=(flip(self.me, bit),), device_id_type=MESH).start()

    def masks(self, color, stage):
        d1, d2, d3 = COLOR_ORDERS[color]
        return ((0,), (0, d1), (0, d1, d2, d1 | d2))[stage]

    def start(self, stage):
        for color in range(3):
            for mask in self.masks(color, stage):
                self.push(mask, color, COLOR_ORDERS[color][stage], 3 * color + stage, 0)

    def wait(self, stage):
        for color in range(3):
            rows, cols = self.pieces[color]
            landed = self.full.at[pl.ds(0, 2 ** stage), rows, cols]
            pltpu.make_async_copy(landed, landed, self.recv.at[3 * color + stage]).wait()

    def share(self, stage):
        for color in range(3):
            if stage < 0:
                self.push(0, color, CORE, 9, 1)
            else:
                bit = COLOR_ORDERS[color][stage]
                for mask in self.masks(color, stage):
                    self.push(mask | bit, color, CORE, 9, 1)

    def own_load(self):
        pltpu.make_async_copy(self.shard, self.own_vmem, self.own_sem).start()

    def own_store(self):
        pltpu.make_async_copy(self.shard, self.own_vmem, self.own_sem).wait()
        pltpu.make_async_copy(self.own_vmem, self.full.at[self.me], self.own_sem).start()

    def finish(self):
        half = self.full.at[pl.ds(0, 8)]
        pltpu.make_async_copy(half, half, self.recv.at[9]).wait()
        pltpu.make_async_copy(half, half, self.send.at[1]).wait()
        sent = self.full.at[pl.ds(0, 7)]
        pltpu.make_async_copy(sent, sent, self.send.at[0]).wait()
        pltpu.make_async_copy(self.own_vmem, self.full.at[self.me], self.own_sem).wait()


def gather_scratch(sh_in, sh_out):
    return [pltpu.SemaphoreType.DMA((10,)), pltpu.SemaphoreType.DMA((2,)),
            pltpu.SemaphoreType.DMA((10,)), pltpu.SemaphoreType.DMA((2,)),
            pltpu.VMEM(sh_in, BF), pltpu.SemaphoreType.DMA,
            pltpu.VMEM(sh_out, BF), pltpu.SemaphoreType.DMA]


def make_gathers(shard_in, shard_out, full_in, full_out, scratch):
    rin, sin, rout, sout, vin, semin, vout, semout = scratch
    every = slice(None)
    cols = full_in.shape[2]
    tiles = cols // 128
    a = 128 * ((tiles + 2) // 3)
    pieces_in = [(every, pl.ds(0, a)), (every, pl.ds(a, a)), (every, pl.ds(2 * a, cols - 2 * a))]
    rows = full_out.shape[1]
    b = 16 * (rows // 48)
    pieces_out = [(pl.ds(0, b), every), (pl.ds(b, b), every), (pl.ds(2 * b, rows - 2 * b), every)]
    return (Gather(shard_in, full_in, pieces_in, rin, sin, vin, semin),
            Gather(shard_out, full_out, pieces_out, rout, sout, vout, semout))


def gather_kernel(shard_in, shard_out, full_in, full_out, *scratch):
    g_in, g_out = make_gathers(shard_in, shard_out, full_in, full_out, scratch)
    greet_neighbours()
    g_in.start(0)
    g_out.start(0)
    g_in.own_load()
    g_out.own_load()
    g_in.share(-1)
    g_out.share(-1)
    g_in.own_store()
    g_out.own_store()
    for stage in (0, 1, 2):
        for g in (g_in, g_out):
            g.wait(stage)
            if stage < 2:
                g.start(stage + 1)
            g.share(stage)
    g_in.finish()
    g_out.finish()


def gather_layer(shard_in, shard_out):
    return pl.pallas_call(
        gather_kernel,
        out_shape=[jax.ShapeDtypeStruct((16,) + shard_in.shape, BF), jax.ShapeDtypeStruct((16,) + shard_out.shape, BF)],
        in_specs=[ANY, ANY], out_specs=[ANY, ANY],
        scratch_shapes=gather_scratch(shard_in.shape, shard_out.shape),
        compiler_params=pltpu.CompilerParams(collective_id=0, has_side_effects=True, vmem_limit_bytes=VMEM_LIMIT),
        name='gather_first')(shard_in, shard_out)


HB = 512
MT = 512


def gelu_and_slope(z):
    phi = 0.5 + 0.5 * lax.erf(z * SQRT_HALF)
    density = jnp.exp(z * z * -0.5) * DENSITY
    return z * phi, phi + z * density


def forward_compute(step, n_up, h_ref, wi_ref, wo_vmem, d_ref, hn_ref, a_vmem, a_hbm, a_sem):
    tokens = h_ref.shape[0]

    @pl.when(step < n_up)
    def _():
        base = pl.multiple_of(jnp.minimum(step, n_up - 1) * HB, HB)
        for m in range(tokens // MT):
            rows = pl.ds(m * MT, MT)
            z = jnp.dot(h_ref[rows, :], wi_ref[...], preferred_element_type=F32)
            act, slope = gelu_and_slope(z.astype(BF).astype(F32))
            a_vmem[rows, pl.ds(base, HB)] = act.astype(BF)
            d_ref[rows, :] = slope
        pltpu.make_async_copy(a_vmem.at[:, pl.ds(base, HB)], a_hbm.at[:, pl.ds(base, HB)], a_sem).start()

    @pl.when(step >= n_up)
    def _():
        base = pl.multiple_of(jnp.maximum(step - n_up, 0) * MT, MT)
        branch = jnp.dot(a_vmem[pl.ds(base, MT), :], wo_vmem[...], preferred_element_type=F32)
        hn_ref[...] = (h_ref[pl.ds(base, MT), :].astype(F32) + branch).astype(BF)


def forward_kernel(gathering, n_up, n_down, h_ref, wi_ref, wo_hbm, *refs):
    if gathering:
        shard_in, shard_out, a_hbm, d_ref, hn_ref, full_in, full_out, a_vmem, wo_vmem, a_sem, wo_sem, *scratch = refs
        g_in, g_out = make_gathers(shard_in, shard_out, full_in, full_out, scratch)
    else:
        a_hbm, d_ref, hn_ref, a_vmem, wo_vmem, a_sem, wo_sem = refs
    step = pl.program_id(0)

    def at(s, fn):
        pl.when(step == s)(fn)

    def begin():
        pltpu.make_async_copy(wo_hbm, wo_vmem, wo_sem).start()
        if gathering:
            greet_neighbours()
            g_in.start(0)
            g_out.start(0)
            g_in.own_load()
            g_out.own_load()
            g_in.share(-1)
            g_out.share(-1)

    def advance(g, stage):
        def fn():
            g.wait(stage)
            if stage < 2:
                g.start(stage + 1)
            g.share(stage)
        return fn

    at(0, begin)
    if gathering:
        def stores():
            g_in.own_store()
            g_out.own_store()
        at(1, stores)
        at(3, advance(g_in, 0))
        at(4, advance(g_out, 0))
        at(6, advance(g_in, 1))
        at(8, advance(g_out, 1))
        at(11, advance(g_in, 2))
    at(n_up, lambda: pltpu.make_async_copy(wo_hbm, wo_vmem, wo_sem).wait())
    forward_compute(step, n_up, h_ref, wi_ref, wo_vmem, d_ref, hn_ref, a_vmem, a_hbm, a_sem)

    def end():
        pltpu.make_async_copy(a_vmem, a_hbm, a_sem).wait()
        if gathering:
            advance(g_out, 2)()
            g_in.finish()
            g_out.finish()
    at(n_up + n_down - 1, end)


def forward_layer(h, w_in_full, w_out_full, next_shards):
    tokens, width = h.shape
    hidden = w_in_full.shape[1]
    n_up, n_down = hidden // HB, tokens // MT
    gathering = next_shards is not None
    up = lambda s: jnp.minimum(s, n_up - 1)
    down = lambda s: jnp.maximum(s - n_up, 0)
    in_specs = [pl.BlockSpec((tokens, width), lambda s: (0, 0), pipeline_mode=pl.Buffered(1)),
                pl.BlockSpec((width, HB), lambda s: (0, up(s))), ANY]
    out_specs = [ANY, pl.BlockSpec((tokens, HB), lambda s: (0, up(s))), pl.BlockSpec((MT, width), lambda s: (down(s), 0))]
    out_shape = [jax.ShapeDtypeStruct((tokens, hidden), BF), jax.ShapeDtypeStruct((tokens, hidden), F32),
                 jax.ShapeDtypeStruct((tokens, width), BF)]
    scratch = [pltpu.VMEM((tokens, hidden), BF), pltpu.VMEM((hidden, width), BF),
               pltpu.SemaphoreType.DMA, pltpu.SemaphoreType.DMA]
    args = [h, w_in_full, w_out_full]
    params = dict(vmem_limit_bytes=VMEM_LIMIT)
    if gathering:
        sh_in, sh_out = next_shards
        args += [sh_in, sh_out]
        in_specs += [ANY, ANY]
        out_specs += [ANY, ANY]
        out_shape += [jax.ShapeDtypeStruct((16,) + sh_in.shape, BF), jax.ShapeDtypeStruct((16,) + sh_out.shape, BF)]
        scratch += gather_scratch(sh_in.shape, sh_out.shape)
        params.update(collective_id=1, has_side_effects=True)
    return pl.pallas_call(
        functools.partial(forward_kernel, gathering, n_up, n_down), grid=(n_up + n_down,),
        in_specs=in_specs, out_specs=out_specs, out_shape=out_shape, scratch_shapes=scratch,
        compiler_params=pltpu.CompilerParams(**params),
        cost_estimate=pl.CostEstimate(flops=4 * tokens * width * hidden, bytes_accessed=70 * 2 ** 20, transcendentals=0),
        name='forward_gather' if gathering else 'forward_last')(*args)


NB = 256
CHIP_ORDER = (1, 2, 4, 0, 3, 5, 6, 7)
OWNERS = (1, 2, 4, 0)


def pick(index, values):
    out = values[0]
    for i in range(1, len(values)):
        out = jnp.where(index == i, values[i], out)
    return out


def chip_at(turn):
    chip = lax.axis_index('data') // 2
    mask = pick(turn, CHIP_ORDER)
    for bit in (1, 2, 4):
        chip = jnp.where((mask // bit) % 2 == 1, flip(chip, bit), chip)
    return chip


def block_at(step):
    core = lax.axis_index('data') % 2
    return 2 * chip_at(step // 2) + jnp.where(step % 2 == 0, 1 - core, core)


def rounded_sum(lhs_t, rhs, half):
    first = jnp.dot(lhs_t[:, :half], rhs[:half, :], preferred_element_type=F32).astype(BF).astype(F32)
    second = jnp.dot(lhs_t[:, half:], rhs[half:, :], preferred_element_type=F32).astype(BF).astype(F32)
    return first + second


def backward_kernel(with_input_grad, n_in, n_rows, rb_ref, wo_ref, a_ref, d_ref, h_hbm, *refs):
    if with_input_grad:
        wi_ref, r_ref, rn_ref, rbn_ref, gi_out, go_out, *scratch = refs
    else:
        gi_out, go_out, *scratch = refs
    (rbt, ht, hraw, e_ref, gi_x, gi_send, gi_recv, go_x, go_send, go_recv,
     h_sem, dsend, drecv, xsend, xrecv, own_sem) = scratch
    step = pl.program_id(0)
    me = lax.axis_index('data')
    core = me % 2
    tokens, width = rb_ref.shape
    half = tokens // 2
    rows_dev = ht.shape[0] // 8
    mine = 4 * rows_dev
    n_steps = 16
    partner = (flip(me, CORE),)

    def at(s, fn):
        pl.when(step == s)(fn)

    def h_copy(i):
        chip = me // 2
        if OWNERS[i]:
            chip = flip(chip, OWNERS[i])
        cols = pl.multiple_of(chip * 2 * rows_dev, 2 * rows_dev)
        return pltpu.make_async_copy(h_hbm.at[:, pl.ds(cols, 2 * rows_dev)], hraw.at[:, pl.ds(i * 2 * rows_dev, 2 * rows_dev)], h_sem)

    def begin():
        for i in range(4):
            h_copy(i).start()
        greet_neighbours()
        for m in range(tokens // 256):
            rbt[:, pl.ds(m * 256, 256)] = rb_ref[pl.ds(m * 256, 256), :].T

    def turn_h():
        pltpu.make_async_copy(hraw, hraw, h_sem).wait()
        for m in range(tokens // 256):
            cols = pl.ds(m * 256, 256)
            for i in range(4):
                flipped = hraw[pl.ds(m * 256, 256), pl.ds(i * 2 * rows_dev, 2 * rows_dev)].T
                ht[pl.ds(pl.multiple_of(i * rows_dev + core * mine, rows_dev), rows_dev), cols] = flipped[:rows_dev]
                ht[pl.ds(pl.multiple_of(i * rows_dev + (1 - core) * mine, rows_dev), rows_dev), cols] = flipped[rows_dev:]

    def core_copy(src, dst, index):
        return pltpu.make_async_remote_copy(src_ref=src, dst_ref=dst, send_sem=dsend.at[index], recv_sem=drecv.at[index],
                                            device_id=partner, device_id_type=MESH)

    def gi_core(turn):
        return core_copy(gi_send.at[turn % 2], gi_recv.at[turn % 2], turn % 2)

    def go_core(turn):
        return core_copy(go_send.at[turn % 2], go_recv.at[turn % 2], 2 + turn % 2)

    def ship(src, dst, i, kind):
        bit = 2 * OWNERS[i]
        if bit:
            pltpu.make_async_remote_copy(src_ref=src, dst_ref=dst(1 + i), send_sem=xsend.at[3 * kind + i],
                                         recv_sem=xrecv.at[3 * kind + i], device_id=(flip(me, bit),), device_id_type=MESH).start()
        else:
            pltpu.make_async_copy(src, dst(0), own_sem.at[kind]).start()

    def go_merge(turn):
        go_core(turn).wait_recv()
        go_x[turn] = go_x[turn] + go_recv[turn % 2]
        ship(go_x.at[turn], lambda slot: go_out.at[slot], turn, 1)

    def gi_merge(turn):
        gi_core(turn).wait_recv()
        gi_x[turn] = gi_x[turn] + gi_recv[turn % 2]
        cols = pl.ds(pl.multiple_of(chip_at(turn) * 2 * NB, 2 * NB), 2 * NB)
        for i in range(4):
            ship(gi_x.at[turn, pl.ds(i * rows_dev, rows_dev)], lambda slot: gi_out.at[slot, :, cols], i, 0)

    def in_grad(s):
        base = pl.multiple_of(block_at(s) * NB, NB)
        lane = pl.multiple_of(jnp.where(s % 2 == 0, 1 - core, core) * NB, NB)
        turn = s // 2
        total = rounded_sum(ht[...], e_ref[:, pl.ds(base, NB)], half)
        gi_x[turn, :, pl.ds(lane, NB)] = total[:mine]
        gi_send[turn % 2, :, pl.ds(lane, NB)] = total[mine:]

    even = step % 2 == 0
    at(0, begin)
    at(1, turn_h)
    for turn in range(4):
        at(2 * turn + 2, functools.partial(go_merge, turn))
    last_merge = n_steps + 2 if with_input_grad else n_steps
    pl.when(even & (step >= 4) & (step <= last_merge))(lambda: gi_merge(jnp.clip(step // 2 - 2, 0, 7)))
    pl.when((step % 2 == 1) & (step >= 5) & (step < n_steps))(lambda: gi_core(step // 2).wait_send())
    pl.when(even & (step >= 4) & (step < 8))(lambda: go_core(step // 2).wait_send())

    @pl.when(step < n_steps)
    def _():
        base = pl.multiple_of(block_at(jnp.minimum(step, n_steps - 1)) * NB, NB)
        for m in range(tokens // 512):
            rows = pl.ds(m * 512, 512)
            u = lax.dot_general(rb_ref[rows, :], wo_ref[...], NT, preferred_element_type=F32)
            e_ref[rows, pl.ds(base, NB)] = (d_ref[rows, :] * u).astype(BF)

    @pl.when((step >= 1) & (step <= n_steps))
    def _():
        in_grad(jnp.clip(step - 1, 0, n_steps - 1))

    pl.when(even & (step >= 2) & (step <= n_steps))(lambda: gi_core(jnp.maximum(step // 2 - 1, 0)).start())

    @pl.when(step < 8)
    def _():
        turn = jnp.minimum(step // 2, 3)
        for m in range(width // 512):
            rows = pl.ds(m * 512, 512)
            total = rounded_sum(rbt[rows, :], a_ref[...], half)

            @pl.when(even)
            def _():
                go_send[turn % 2, rows, :] = total

            @pl.when(jnp.logical_not(even))
            def _():
                go_x[turn, rows, :] = total

        @pl.when(even)
        def _():
            go_core(turn).start()

    if with_input_grad:
        @pl.when(step >= n_steps)
        def _():
            base = pl.multiple_of((jnp.maximum(step - n_steps, 0) % 2) * half, half)
            for m in range(half // 512):
                rows = pl.ds(m * 512, 512)
                u = lax.dot_general(e_ref[pl.ds(base + m * 512, 512), :], wi_ref[...], NT, preferred_element_type=F32) + r_ref[rows, :]
                rn_ref[rows, :] = u
                rbn_ref[rows, :] = u.astype(BF)

    def end():
        if not with_input_grad:
            gi_merge(7)
        for turn in (6, 7):
            gi_core(turn).wait_send()
        for turn in (2, 3):
            go_core(turn).wait_send()
        for i in range(3):
            for kind, whole in ((0, gi_out.at[0]), (1, go_out.at[0])):
                pltpu.make_async_copy(whole, whole, xsend.at[3 * kind + i]).wait()
                pltpu.make_async_copy(whole, whole, xrecv.at[3 * kind + i]).wait()
        pltpu.make_async_copy(gi_out.at[0], gi_out.at[0], own_sem.at[0]).wait()
        pltpu.make_async_copy(go_out.at[0], go_out.at[0], own_sem.at[1]).wait()
    at(n_steps + (8 if with_input_grad else 1) - 1, end)


def backward_layer(rb, r, h, w_in_full, w_out_full, a, d, with_input_grad):
    tokens, width = rb.shape
    hidden = a.shape[1]
    half = tokens // 2
    rows_dev = width // 16
    cap = lambda s: jnp.minimum(s, 15)
    tail = lambda s: jnp.maximum(s - 16, 0)
    in_specs = [pl.BlockSpec((tokens, width), lambda s: (0, 0), pipeline_mode=pl.Buffered(1)),
                pl.BlockSpec((NB, width), lambda s: (block_at(cap(s)), 0)),
                pl.BlockSpec((tokens, NB), lambda s: (0, block_at(jnp.minimum(s, 7)))),
                pl.BlockSpec((tokens, NB), lambda s: (0, block_at(cap(s)))),
                ANY]
    args = [rb, w_out_full, a, d, h]
    out_specs, out_shape = [], []
    if with_input_grad:
        in_specs += [pl.BlockSpec((NB, hidden), lambda s: (tail(s) // 2, 0)),
                     pl.BlockSpec((half, NB), lambda s: (tail(s) % 2, tail(s) // 2))]
        args += [w_in_full, r]
        out_specs += [pl.BlockSpec((half, NB), lambda s: (tail(s) % 2, tail(s) // 2))] * 2
        out_shape += [jax.ShapeDtypeStruct((tokens, width), F32), jax.ShapeDtypeStruct((tokens, width), BF)]
    out_specs += [ANY, ANY]
    out_shape += [jax.ShapeDtypeStruct((4, rows_dev, hidden), F32), jax.ShapeDtypeStruct((4, width, hidden // 16), F32)]
    scratch = [pltpu.VMEM((width, tokens), BF), pltpu.VMEM((8 * rows_dev, tokens), BF), pltpu.VMEM((tokens, 8 * rows_dev), BF),
               pltpu.VMEM((tokens, hidden), BF),
               pltpu.VMEM((8, 4 * rows_dev, 2 * NB), F32), pltpu.VMEM((2, 4 * rows_dev, 2 * NB), F32), pltpu.VMEM((2, 4 * rows_dev, 2 * NB), F32),
               pltpu.VMEM((4, width, NB), F32), pltpu.VMEM((2, width, NB), F32), pltpu.VMEM((2, width, NB), F32),
               pltpu.SemaphoreType.DMA, pltpu.SemaphoreType.DMA((4,)), pltpu.SemaphoreType.DMA((4,)),
               pltpu.SemaphoreType.DMA((6,)), pltpu.SemaphoreType.DMA((6,)), pltpu.SemaphoreType.DMA((2,))]
    return pl.pallas_call(
        functools.partial(backward_kernel, with_input_grad, 0, rows_dev), grid=(24 if with_input_grad else 17,),
        in_specs=in_specs, out_specs=out_specs, out_shape=out_shape, scratch_shapes=scratch,
        compiler_params=pltpu.CompilerParams(collective_id=2 if with_input_grad else 3, has_side_effects=True, vmem_limit_bytes=VMEM_LIMIT),
        cost_estimate=pl.CostEstimate(flops=6 * tokens * width * hidden, bytes_accessed=100 * 2 ** 20, transcendentals=0),
        name='backward' if with_input_grad else 'backward_first')(*args)


def antipodal(values):
    return lax.ppermute(values, 'data', [(i, i ^ 14) for i in range(16)])


def sam_pass(x_pair, y_pair, shards_in, shards_out):
    layers = len(shards_in)
    own = x_pair.shape[0] // 2
    h_cur = x_pair
    saved = []
    full = gather_layer(shards_in[0], shards_out[0])
    for layer in range(layers):
        w_in_full = full[0].reshape(-1, full[0].shape[-1])
        w_out_full = full[1].reshape(-1, full[1].shape[-1])
        nxt = (shards_in[layer + 1], shards_out[layer + 1]) if layer + 1 < layers else None
        act, slope, h_next, *full = forward_layer(h_cur, w_in_full, w_out_full, nxt)
        saved.append((h_cur, act, slope, w_in_full, w_out_full))
        h_cur = h_next
    residual = h_cur.astype(F32) - y_pair.astype(F32)
    local_loss = 0.5 * jnp.sum(residual[:own] * residual[:own]) / own
    r = residual / own
    rb = r.astype(BF)
    g_in = [None] * layers
    g_out = [None] * layers
    for layer in reversed(range(layers)):
        h_prev, act, slope, w_in_full, w_out_full = saved[layer]
        res = backward_layer(rb, r, h_prev, w_in_full, w_out_full, act, slope, layer > 0)
        if layer > 0:
            r, rb = res[0], res[1]
        g_in[layer] = jnp.sum(res[-2], axis=0) / 16
        g_out[layer] = (jnp.sum(res[-1], axis=0) / 16).T
    return local_loss, g_in, g_out


def solution(mesh):
    groups = mesh.shape['data']

    def device_step(x_blk, y_blk, w_in_sh, w_out_sh):
        layers = w_in_sh.shape[0]
        model_dim = w_out_sh.shape[2]
        radius = RHO_FRAC * math.sqrt(layers * model_dim)
        x_tok = x_blk.reshape(-1, model_dim)
        y_tok = y_blk.reshape(-1, model_dim)
        x_pair = jnp.concatenate([x_tok, antipodal(x_tok)])
        y_pair = jnp.concatenate([y_tok, antipodal(y_tok)])
        span = range(layers)
        _, g_in, g_out = sam_pass(x_pair, y_pair, [w_in_sh[l].astype(BF) for l in span], [w_out_sh[l].astype(BF) for l in span])
        part_sq = sum(jnp.sum(g * g) for g in g_in) + sum(jnp.sum(g * g) for g in g_out)
        grad_norm = jnp.sqrt(lax.psum(part_sq, 'data'))
        scale_eps = radius / grad_norm
        pert_in = [(w_in_sh[l] + scale_eps * g_in[l]).astype(BF) for l in span]
        pert_out = [(w_out_sh[l] + scale_eps * g_out[l]).astype(BF) for l in span]
        pert_loss, gp_in, gp_out = sam_pass(x_pair, y_pair, pert_in, pert_out)
        mean_loss = lax.psum(pert_loss, 'data') / groups
        return w_in_sh - LEARN_RATE * jnp.stack(gp_in), w_out_sh - LEARN_RATE * jnp.stack(gp_out), mean_loss

    return jax.shard_map(device_step, mesh=mesh,
                         in_specs=(P('data', None, None), P('data', None, None), P(None, 'data', None), P(None, 'data', None)),
                         out_specs=(P(None, 'data', None), P(None, 'data', None), P()),
                         check_vma=False)
```

time: 2830 us -> 1620 us (0.57)
  waiting for transfers between devices: 1420 us -> 0.01 us
  Pallas kernels: 0 us -> 1400 us
  matrix products: 1030 us -> 0 us
  blocking collectives: 166 us -> 62.8 us
  starting transfers between devices: 66.4 us -> 5.28 us
    pallas_call x0 -> x18, Pallas kernels: none -> 1400 us  [the longest x8 677 us: backward_layer(): pl.pallas_call(functools.partial(backward_kernel, with_input_grad, 0, row...]
    all_to_all x16 -> x0, waiting for transfers between devices: 1080 us -> none  [scatter_mean(): lax.all_to_all(grad_full.astype(jnp.bfloat16), 'data', 0, 0, tiled=True)]
    dot_general x44 -> x0, matrix products: 1030 us -> none  [the longest x8 372 us: layer_forward(): jnp.dot(h_prev, w_in_l, preferred_element_type=jnp.float32)]
    all_gather x16 -> x0, waiting for transfers between devices: 326 us -> none  [the longest x8 289 us: sam_pass(): w_in_full.append(lax.all_gather(w_in_sh[layer], 'data', axis=0, tiled=True))]
    psum x1, blocking collectives: 133 us -> 31.4 us  [device_step(): mean_loss = lax.psum(pert_loss, 'data') / groups]
    all_to_all x16 -> x0, starting transfers between devices: 65.4 us -> none  [scatter_mean(): lax.all_to_all(grad_full.astype(jnp.bfloat16), 'data', 0, 0, tiled=True)]
    reduce_sum x18 -> x23, other arithmetic: 92.4 us -> 57.7 us  [the longest x8 26.1 us: sam_pass(): g_in[layer] = jnp.sum(res[-2], axis=0) / 16]
  transfers between devices with their start and end apart: 32 -> 2, of which waited for: 31 -> 0; matrix products, arithmetic and copies ran while one was open for 37% -> 1% of each run, Pallas kernels for 0% -> 25%
where the time goes in v1:
time: 1620 us; the launch traced here: 1610 us
  Pallas kernels  1400 us (86%)
  other arithmetic  108 us (7%)
  blocking collectives  62.8 us (4%)
  local copies, waits for them, and re-layouts  22.9 us (1%)
    pallas_call x8, Pallas kernels, backward_layer(): pl.pallas_call(functools.partial(backward_kernel, with_input_grad, 0, row...  677 us
    pallas_call x8, Pallas kernels, forward_layer(): pl.pallas_call(functools.partial(forward_kernel, gathering, n_up, n_down)...  526 us
    pallas_call x2, Pallas kernels, gather_layer(): pl.pallas_call(gather_kernel, out_shape=[jax.ShapeDtypeStruct((16,) + sha...  198 us
  transfers between devices with their start and end apart: 2, of which 0 were waited for; matrix products, arithmetic and copies ran while one was open for 1% of the time, Pallas kernels for 25%

profile of v1, /device:TPU:0, one launch (start us, length us, event | category | flops | bytes accessed | tf_op | source)
XLA Modules:
  0.0 1609.2 jit_solution(3459689533164039173)
XLA Ops:
  0.6 5.2 collective-permute-start
  5.9 5.4 copy.11
  11.3 3.8 bitcast_convert_fusion
  15.1 1.4 bitcast_convert_fusion.1
  16.5 137.2 %gather_first.2 = (bf16[16,64,4096]{2,1,0:T(8,128)(2,1)}, bf16[16,256,1024]{2,1,0:T(8,128)(2,1)}) custom-call(bf16[64,4096]{1,0:T(8,128)(2,1)} %get-tuple-element.158.shard_in, bf16[256,1024]{1,0:T(8,128)(2,1)} %get-tuple-element.154.shard_out), custom_call_target="tpu_custom_call" | custom-call | tf_op jit(solution)/shard_map/gather_first/pallas_call | solution.py:147
  153.7 4.7 pad_maximum_fusion.h_ref.h_hbm
  158.4 70.2 %forward_gather.6 = (bf16[2048,4096]{1,0:T(8,128)(2,1)}, f32[2048,4096]{1,0:T(8,128)}, bf16[2048,1024]{1,0:T(8,128)(2,1)}, bf16[16,64,4096]{2,1,0:T(8,128)(2,1)}, bf16[16,256,1024]{2,1,0:T(8,128)(2,1)}) custom-call(bf16[2048,1024]{1,0:T(8,128)(2,1)} %pad_maximum_fusion.h_ref.h_hbm, bf16[1024,4096]{1,0:T(8,128)(2,1)} %bitcast.99, ...), custom_call_target="tpu_custom_call" | custom-call | flops 34359738368 | bytes 73400320 | tf_op jit(solution)/shard_map/forward_gather/pallas_call | solution.py:264
  228.6 69.5 %forward_gather.7 = (bf16[2048,4096]{1,0:T(8,128)(2,1)}, f32[2048,4096]{1,0:T(8,128)}, bf16[2048,1024]{1,0:T(8,128)(2,1)}, bf16[16,64,4096]{2,1,0:T(8,128)(2,1)}, bf16[16,256,1024]{2,1,0:T(8,128)(2,1)}) custom-call(bf16[2048,1024]{1,0:T(8,128)(2,1)} %get-tuple-element.71.h_ref.h_hbm, bf16[1024,4096]{1,0:T(8,128)(2,1)} %bitcast.101, ...), custom_call_target="tpu_custom_call" | custom-call | flops 34359738368 | bytes 73400320 | tf_op jit(solution)/shard_map/forward_gather/pallas_call | solution.py:264
  298.1 69.8 %forward_gather.8 = (bf16[2048,4096]{1,0:T(8,128)(2,1)}, f32[2048,4096]{1,0:T(8,128)}, bf16[2048,1024]{1,0:T(8,128)(2,1)}, bf16[16,64,4096]{2,1,0:T(8,128)(2,1)}, bf16[16,256,1024]{2,1,0:T(8,128)(2,1)}) custom-call(bf16[2048,1024]{1,0:T(8,128)(2,1)} %get-tuple-element.74.h_ref.h_hbm, bf16[1024,4096]{1,0:T(8,128)(2,1)} %bitcast.109, ...), custom_call_target="tpu_custom_call" | custom-call | flops 34359738368 | bytes 73400320 | tf_op jit(solution)/shard_map/forward_gather/pallas_call | solution.py:264
  367.8 54.1 %forward_last.2 = (bf16[2048,4096]{1,0:T(8,128)(2,1)}, f32[2048,4096]{1,0:T(8,128)}, bf16[2048,1024]{1,0:T(8,128)(2,1)}) custom-call(bf16[2048,1024]{1,0:T(8,128)(2,1)} %get-tuple-element.77.h_ref.h_hbm, bf16[1024,4096]{1,0:T(8,128)(2,1)} %bitcast.117, bf16[4096,1024]{1,0:T(8,128)(2,1)} %bitcast.119), custom_call_target="tpu_custom_call" | custom-call | flops 34359738368 | bytes 73400320 | tf_op jit(solution)/shard_map/forward_last/pallas_call | solution.py:264
  421.9 7.7 fusion
  429.6 87.3 %backward.6 = (f32[2048,1024]{1,0:T(8,128)}, bf16[2048,1024]{1,0:T(8,128)(2,1)}, f32[4,64,4096]{2,1,0:T(8,128)}, f32[4,1024,256]{2,1,0:T(8,128)}) custom-call(bf16[2048,1024]{1,0:T(8,128)(2,1)} %get-tuple-element.142.rb_ref, bf16[4096,1024]{1,0:T(8,128)(2,1)} %bitcast.120, bf16[2048,4096]{1,0:T(8,128)(2,1)} %get-tuple-element.81.a_ref, ...), custom_call_target="tpu_custom_call" | custom-call | flops 51539607552 | bytes 104857600 | tf_op jit(solution)/shard_map/backward/pallas_call | solution.py:481
  516.9 88.3 %backward.7 = (f32[2048,1024]{1,0:T(8,128)}, bf16[2048,1024]{1,0:T(8,128)(2,1)}, f32[4,64,4096]{2,1,0:T(8,128)}, f32[4,1024,256]{2,1,0:T(8,128)}) custom-call(bf16[2048,1024]{1,0:T(8,128)(2,1)} %get-tuple-element.83.rb_ref, bf16[4096,1024]{1,0:T(8,128)(2,1)} %bitcast.112, bf16[2048,4096]{1,0:T(8,128)(2,1)} %get-tuple-element.84.a_ref, ...), custom_call_target="tpu_custom_call" | custom-call | flops 51539607552 | bytes 104857600 | tf_op jit(solution)/shard_map/backward/pallas_call | solution.py:481
  605.3 87.6 %backward.8 = (f32[2048,1024]{1,0:T(8,128)}, bf16[2048,1024]{1,0:T(8,128)(2,1)}, f32[4,64,4096]{2,1,0:T(8,128)}, f32[4,1024,256]{2,1,0:T(8,128)}) custom-call(bf16[2048,1024]{1,0:T(8,128)(2,1)} %get-tuple-element.87.rb_ref, bf16[4096,1024]{1,0:T(8,128)(2,1)} %bitcast.104, bf16[2048,4096]{1,0:T(8,128)(2,1)} %get-tuple-element.88.a_ref, ...), custom_call_target="tpu_custom_call" | custom-call | flops 51539607552 | bytes 104857600 | tf_op jit(solution)/shard_map/backward/pallas_call | solution.py:481
  692.9 75.0 %backward_first.2 = (f32[4,64,4096]{2,1,0:T(8,128)}, f32[4,1024,256]{2,1,0:T(8,128)}) custom-call(bf16[2048,1024]{1,0:T(8,128)(2,1)} %get-tuple-element.91.rb_ref, bf16[4096,1024]{1,0:T(8,128)(2,1)} %bitcast.96, bf16[2048,4096]{1,0:T(8,128)(2,1)} %get-tuple-element.92.a_ref, f32[2048,4096]{1,0:T(8,128)} %get-tuple-element.93.d_ref, ...), custom_call_target="tpu_custom_call" | custom-call | flops 51539607552 | bytes 104857600 | tf_op jit(solution)/shard_map/backward_first/pallas_call | solution.py:481
  767.9 2.6 reduce_sum.233
  770.5 2.6 reduce_sum.235
  773.1 1.4 copy.7
  774.5 1.0 multiply_reduce_fusion.2
  775.4 1.3 copy.8
  776.8 2.6 reduce_sum.237
  780.2 1.3 copy.9
  781.5 2.6 reduce_sum.239
  784.1 0.9 multiply_reduce_fusion
  785.0 3.5 reduce_sum.225
  788.5 3.5 reduce_sum.227
  792.0 2.5 reduce_sum.229
  794.6 0.9 multiply_reduce_fusion.5
  795.5 2.5 reduce_sum.231
  798.0 1.0 multiply_reduce_fusion.4
  801.5 2.4 multiply_reduce_fusion.6
  806.6 1.4 copy.10
  807.9 31.4 %psum.14 = f32[]{:T(128)} all-reduce(f32[]{:T(128)S(6)} %add.55), channel_id=1, replica_groups=mesh['data'=16] {'data'}, use_global_device_ids=true, to_apply=%region_16.0 | all-reduce | flops 1 | bytes 8 | tf_op jit(solution)/shard_map/psum | solution.py:536
  840.1 4.6 fusion.8
  846.1 2.2 fusion.4
  848.3 60.7 %gather_first.3 = (bf16[16,64,4096]{2,1,0:T(8,128)(2,1)}, bf16[16,256,1024]{2,1,0:T(8,128)(2,1)}) custom-call(bf16[64,4096]{1,0:T(8,128)(2,1)} %get-tuple-element.148.shard_in, bf16[256,1024]{1,0:T(8,128)(2,1)} %get-tuple-element.144.shard_out), custom_call_target="tpu_custom_call" | custom-call | tf_op jit(solution)/shard_map/gather_first/pallas_call | solution.py:147
  909.0 69.3 %forward_gather.9 = (bf16[2048,4096]{1,0:T(8,128)(2,1)}, f32[2048,4096]{1,0:T(8,128)}, bf16[2048,1024]{1,0:T(8,128)(2,1)}, bf16[16,64,4096]{2,1,0:T(8,128)(2,1)}, bf16[16,256,1024]{2,1,0:T(8,128)(2,1)}) custom-call(bf16[2048,1024]{1,0:T(8,128)(2,1)} %pad_maximum_fusion.h_ref.h_hbm, bf16[1024,4096]{1,0:T(8,128)(2,1)} %bitcast.100, ...), custom_call_target="tpu_custom_call" | custom-call | flops 34359738368 | bytes 73400320 | tf_op jit(solution)/shard_map/forward_gather/pallas_call | solution.py:264
  978.2 69.5 %forward_gather.10 = (bf16[2048,4096]{1,0:T(8,128)(2,1)}, f32[2048,4096]{1,0:T(8,128)}, bf16[2048,1024]{1,0:T(8,128)(2,1)}, bf16[16,64,4096]{2,1,0:T(8,128)(2,1)}, bf16[16,256,1024]{2,1,0:T(8,128)(2,1)}) custom-call(bf16[2048,1024]{1,0:T(8,128)(2,1)} %get-tuple-element.104.h_ref.h_hbm, bf16[1024,4096]{1,0:T(8,128)(2,1)} %bitcast.105, ...), custom_call_target="tpu_custom_call" | custom-call | flops 34359738368 | bytes 73400320 | tf_op jit(solution)/shard_map/forward_gather/pallas_call | solution.py:264
  1047.8 69.7 %forward_gather.11 = (bf16[2048,4096]{1,0:T(8,128)(2,1)}, f32[2048,4096]{1,0:T(8,128)}, bf16[2048,1024]{1,0:T(8,128)(2,1)}, bf16[16,64,4096]{2,1,0:T(8,128)(2,1)}, bf16[16,256,1024]{2,1,0:T(8,128)(2,1)}) custom-call(bf16[2048,1024]{1,0:T(8,128)(2,1)} %get-tuple-element.107.h_ref.h_hbm, bf16[1024,4096]{1,0:T(8,128)(2,1)} %bitcast.113, ...), custom_call_target="tpu_custom_call" | custom-call | flops 34359738368 | bytes 73400320 | tf_op jit(solution)/shard_map/forward_gather/pallas_call | solution.py:264
  1117.4 54.1 %forward_last.3 = (bf16[2048,4096]{1,0:T(8,128)(2,1)}, f32[2048,4096]{1,0:T(8,128)}, bf16[2048,1024]{1,0:T(8,128)(2,1)}) custom-call(bf16[2048,1024]{1,0:T(8,128)(2,1)} %get-tuple-element.110.h_ref.h_hbm, bf16[1024,4096]{1,0:T(8,128)(2,1)} %bitcast.121, bf16[4096,1024]{1,0:T(8,128)(2,1)} %bitcast.123), custom_call_target="tpu_custom_call" | custom-call | flops 34359738368 | bytes 73400320 | tf_op jit(solution)/shard_map/forward_last/pallas_call | solution.py:264
  1171.5 10.6 convert_subtract_fusion
  1182.1 87.9 %backward.9 = (f32[2048,1024]{1,0:T(8,128)}, bf16[2048,1024]{1,0:T(8,128)(2,1)}, f32[4,64,4096]{2,1,0:T(8,128)}, f32[4,1024,256]{2,1,0:T(8,128)}) custom-call(bf16[2048,1024]{1,0:T(8,128)(2,1)} %get-tuple-element.140.rb_ref, bf16[4096,1024]{1,0:T(8,128)(2,1)} %bitcast.124, bf16[2048,4096]{1,0:T(8,128)(2,1)} %get-tuple-element.114.a_ref, ...), custom_call_target="tpu_custom_call" | custom-call | flops 51539607552 | bytes 104857600 | tf_op jit(solution)/shard_map/backward/pallas_call | solution.py:481
  1270.0 87.8 %backward.10 = (f32[2048,1024]{1,0:T(8,128)}, bf16[2048,1024]{1,0:T(8,128)(2,1)}, f32[4,64,4096]{2,1,0:T(8,128)}, f32[4,1024,256]{2,1,0:T(8,128)}) custom-call(bf16[2048,1024]{1,0:T(8,128)(2,1)} %get-tuple-element.116.rb_ref, bf16[4096,1024]{1,0:T(8,128)(2,1)} %bitcast.116, bf16[2048,4096]{1,0:T(8,128)(2,1)} %get-tuple-element.117.a_ref, ...), custom_call_target="tpu_custom_call" | custom-call | flops 51539607552 | bytes 104857600 | tf_op jit(solution)/shard_map/backward/pallas_call | solution.py:481
  1357.8 88.1 %backward.11 = (f32[2048,1024]{1,0:T(8,128)}, bf16[2048,1024]{1,0:T(8,128)(2,1)}, f32[4,64,4096]{2,1,0:T(8,128)}, f32[4,1024,256]{2,1,0:T(8,128)}) custom-call(bf16[2048,1024]{1,0:T(8,128)(2,1)} %get-tuple-element.120.rb_ref, bf16[4096,1024]{1,0:T(8,128)(2,1)} %bitcast.108, bf16[2048,4096]{1,0:T(8,128)(2,1)} %get-tuple-element.121.a_ref, ...), custom_call_target="tpu_custom_call" | custom-call | flops 51539607552 | bytes 104857600 | tf_op jit(solution)/shard_map/backward/pallas_call | solution.py:481
  1446.0 74.4 %backward_first.3 = (f32[4,64,4096]{2,1,0:T(8,128)}, f32[4,1024,256]{2,1,0:T(8,128)}) custom-call(bf16[2048,1024]{1,0:T(8,128)(2,1)} %get-tuple-element.124.rb_ref, bf16[4096,1024]{1,0:T(8,128)(2,1)} %bitcast.98, bf16[2048,4096]{1,0:T(8,128)(2,1)} %get-tuple-element.125.a_ref, f32[2048,4096]{1,0:T(8,128)} %get-tuple-element.126.d_ref, ...), custom_call_target="tpu_custom_call" | custom-call | flops 51539607552 | bytes 104857600 | tf_op jit(solution)/shard_map/backward_first/pallas_call | solution.py:481
  1520.4 2.6 reduce_sum.245
  1523.1 2.6 reduce_sum.246
  1525.8 2.6 reduce_sum.247
  1528.4 1.1 multiply_bitcast_fusion.1
  1529.4 2.6 reduce_sum.248
  1532.0 1.1 multiply_bitcast_fusion
  1533.1 3.5 reduce_sum.241
  1536.6 1.3 multiply_bitcast_fusion.7
  1537.9 3.5 reduce_sum.242
  1541.4 2.3 multiply_bitcast_fusion.6
  1543.7 3.5 reduce_sum.243
  1547.2 2.3 multiply_bitcast_fusion.5
  1549.5 3.5 reduce_sum.244
  1553.0 2.3 multiply_bitcast_fusion.4
  1555.3 3.9 fusion.1
  1559.8 5.4 fusion.3
  1565.2 5.5 copy.12
  1570.7 31.4 %psum.15 = f32[]{:T(128)} all-reduce(f32[]{:T(128)S(6)} %div.103), channel_id=1, replica_groups=mesh['data'=16] {'data'}, use_global_device_ids=true, to_apply=%region_26.0 | all-reduce | flops 1 | bytes 8 | tf_op jit(solution)/shard_map/psum | solution.py:541
  1602.8 5.1 fusion.2
  (22 shorter events, 2.5 us)
Async XLA Ops:
  0.6 153.1 %collective-permute-start = (bf16[1024,1024]{1,0:T(8,128)(2,1)}, bf16[1024,1024]{1,0:T(8,128)(2,1)}, u32[]{:S(2)}, u32[]{:S(2)}) collective-permute-start(bf16[1024,1024]{1,0:T(8,128)(2,1)} %bitcast.93), channel_id=1, source_target_pairs={{0,14},{1,15},{2,12},{3,13},{4,10},{5,11},{6,8},{7,9},{8,6},{9,7},... | collective-permute-start | bytes 6291464 | tf_op jit(solution)/shard_map/ppermute | solution.py:490
  5.9 416.1 %collective-permute-start.1 = (bf16[1024,1024]{1,0:T(8,128)(2,1)}, bf16[1024,1024]{1,0:T(8,128)(2,1)}, u32[]{:S(2)}, u32[]{:S(2)}) collective-permute-start(bf16[1024,1024]{1,0:T(8,128)(2,1)} %bitcast.90), channel_id=1, source_target_pairs={{0,14},{1,15},{2,12},{3,13},{4,10},{5,11},{6,8},{7,9},{8,6},{9,7},... | collective-permute-start | bytes 6291464 | tf_op jit(solution)/shard_map/ppermute | solution.py:490
  11.3 3.8 copy-start.1
  840.0 4.7 copy-start
  840.1 4.8 copy-start.4
  840.1 5.4 copy-start.5
  840.1 5.7 copy-start.6
  840.1 6.0 copy-start.7
  1565.2 37.5 %copy-start.2 = (f32[1,64,4096]{2,1,0:T(8,128)S(1)}, f32[1,64,4096]{2,1,0:T(8,128)}, u32[]{:S(2)}) copy-start(f32[1,64,4096]{2,1,0:T(8,128)} %multiply_bitcast_fusion.6) | copy-start | bytes 3145732
  1565.2 37.5 %copy-start.3 = (f32[1,64,4096]{2,1,0:T(8,128)S(1)}, f32[1,64,4096]{2,1,0:T(8,128)}, u32[]{:S(2)}) copy-start(f32[1,64,4096]{2,1,0:T(8,128)} %multiply_bitcast_fusion.5) | copy-start | bytes 3145732

commit v2 on v0

v2 whole, which is shorter than its diff:
```python
import functools
import math
import jax
import jax.numpy as jnp
from jax import lax
from jax.experimental import pallas as pl
from jax.experimental.pallas import tpu as pltpu
from jax.sharding import PartitionSpec as P

RHO_FRAC = 0.1
LEARN_RATE = 0.5
BF = jnp.bfloat16
F32 = jnp.float32
MESH = pl.DeviceIdType.MESH
DEVICES = 16
LANES = 128
SUM_TILE = (8, LANES)
SQRT_HALF = math.sqrt(0.5)
LOG2_E = math.log2(math.e)
LOG_DENSITY = -0.5 * math.log2(2.0 * math.pi)
VMEM_LIMIT = 63 * 2 ** 20
NT = (((1,), (1,)), ((), ()))
CORE, AX_X, AX_Y, AX_Z = 1, 2, 4, 8
ANTIPODE = AX_X | AX_Y | AX_Z
COLOR_ORDERS = ((AX_X, AX_Y, AX_Z), (AX_Y, AX_Z, AX_X), (AX_Z, AX_X, AX_Y))
ANY = pl.BlockSpec(memory_space=pl.ANY)


def span(index, size):
    return pl.ds(index * size, size)


def flip(dev, bit):
    return dev ^ bit


def flips(dev, mask):
    return dev ^ mask


def greet_neighbours(*more):
    me = lax.axis_index('data')
    barrier = pltpu.get_barrier_semaphore()
    masks = (CORE, AX_X, AX_Y, AX_Z) + more
    for mask in masks:
        pl.semaphore_signal(barrier, inc=1, device_id=(flips(me, mask),), device_id_type=MESH)
    pl.semaphore_wait(barrier, len(masks))


def greet_all():
    me = lax.axis_index('data')
    barrier = pltpu.get_barrier_semaphore()
    for other in range(1, DEVICES):
        pl.semaphore_signal(barrier, inc=1, device_id=((me + other) % DEVICES,), device_id_type=MESH)


def send_to_all(tiles, send, recv):
    me = lax.axis_index('data')
    pl.semaphore_wait(pltpu.get_barrier_semaphore(), DEVICES - 1)
    for other in range(1, DEVICES):
        pltpu.make_async_remote_copy(src_ref=tiles.at[me], dst_ref=tiles.at[me], send_sem=send, recv_sem=recv,
                                     device_id=((me + other) % DEVICES,), device_id_type=MESH).start()


def sum_of_all(tiles, send, recv):
    others = tiles.at[pl.ds(0, DEVICES - 1)]
    pltpu.make_async_copy(others, others, recv).wait()
    pltpu.make_async_copy(others, others, send).wait()
    return jnp.sum(tiles[...], axis=0)


TILE_SCRATCH = [pltpu.VMEM((DEVICES,) + SUM_TILE, F32), pltpu.SemaphoreType.DMA, pltpu.SemaphoreType.DMA]


class Gather:
    def __init__(self, full, pieces, sems, shard=None, own_vmem=None, own_sem=None):
        self.shard, self.full, self.pieces = shard, full, pieces
        self.recv, self.send = sems
        self.own_vmem, self.own_sem = own_vmem, own_sem
        self.me = lax.axis_index('data')

    def piece(self, origin_mask, color):
        rows, cols = self.pieces[color]
        if origin_mask == 0 and self.shard is not None:
            return self.shard.at[rows, cols]
        return self.full.at[flips(self.me, origin_mask), rows, cols]

    def push(self, origin_mask, color, bit, sem_index, send_index):
        rows, cols = self.pieces[color]
        pltpu.make_async_remote_copy(
            src_ref=self.piece(origin_mask, color),
            dst_ref=self.full.at[flips(self.me, origin_mask), rows, cols],
            send_sem=self.send.at[send_index], recv_sem=self.recv.at[sem_index],
            device_id=(flip(self.me, bit),), device_id_type=MESH).start()

    def masks(self, color, stage):
        d1, d2, d3 = COLOR_ORDERS[color]
        return ((0,), (0, d1), (0, d1, d2, d1 | d2))[stage]

    def start(self, stage):
        for color in range(3):
            for mask in self.masks(color, stage):
                self.push(mask, color, COLOR_ORDERS[color][stage], 3 * color + stage, 0)

    def wait(self, stage):
        for color in range(3):
            rows, cols = self.pieces[color]
            landed = self.full.at[pl.ds(0, 2 ** stage), rows, cols]
            pltpu.make_async_copy(landed, landed, self.recv.at[3 * color + stage]).wait()

    def share(self, stage):
        for color in range(3):
            if stage < 0:
                self.push(0, color, CORE, 9, 1)
            else:
                bit = COLOR_ORDERS[color][stage]
                for mask in self.masks(color, stage):
                    self.push(mask | bit, color, CORE, 9, 1)

    def own_load(self):
        pltpu.make_async_copy(self.shard, self.own_vmem, self.own_sem).start()

    def own_store(self):
        pltpu.make_async_copy(self.shard, self.own_vmem, self.own_sem).wait()
        pltpu.make_async_copy(self.own_vmem, self.full.at[self.me], self.own_sem).start()

    def blocks(self, count, sem):
        span = self.full.at[pl.ds(0, count)]
        pltpu.make_async_copy(span, span, sem).wait()

    def shared(self, count):
        self.blocks(count, self.recv.at[9])

    def finish(self, sent, shared):
        self.blocks(sent, self.send.at[0])
        self.blocks(shared, self.send.at[1])
        if self.shard is not None:
            pltpu.make_async_copy(self.own_vmem, self.full.at[self.me], self.own_sem).wait()


GATHER_SEMS = [pltpu.SemaphoreType.DMA((10,)), pltpu.SemaphoreType.DMA((2,))]


def gather_scratch(shard):
    return GATHER_SEMS + [pltpu.VMEM(shard.shape, BF), pltpu.SemaphoreType.DMA]


def pieces_in(full):
    cols = full.shape[2]
    a = LANES * ((cols // LANES + 2) // 3)
    every = slice(None)
    return [(every, pl.ds(0, a)), (every, pl.ds(a, a)), (every, pl.ds(2 * a, cols - 2 * a))]


def pieces_out(full):
    rows = full.shape[1]
    b = 16 * (rows // 48)
    every = slice(None)
    return [(pl.ds(0, b), every), (pl.ds(b, b), every), (pl.ds(2 * b, rows - 2 * b), every)]


def gather_in(shard, full, scratch):
    recv, send, vmem, sem = scratch
    return Gather(full, pieces_in(full), (recv, send), shard, vmem, sem)


def gather_out(shard, full, scratch):
    recv, send, vmem, sem = scratch
    return Gather(full, pieces_out(full), (recv, send), shard, vmem, sem)


def full_shape(shard):
    return jax.ShapeDtypeStruct((DEVICES,) + shard.shape, BF)


def gather_kernel(with_tokens, *refs):
    if with_tokens:
        shard_in, shard_out, x_hbm, full_in, full_out, pair, *scratch = refs
        *scratch, x_vmem, x_sems = scratch
    else:
        shard_in, shard_out, full_in, full_out, *scratch = refs
    g_in, g_out = gather_in(shard_in, full_in, scratch[:4]), gather_out(shard_out, full_out, scratch[4:])
    me = lax.axis_index('data')
    greet_neighbours(*((ANTIPODE,) if with_tokens else ()))
    g_in.start(0)
    g_out.start(0)
    if with_tokens:
        trade = pltpu.make_async_remote_copy(src_ref=x_hbm, dst_ref=pair.at[1], send_sem=x_sems.at[0], recv_sem=x_sems.at[1],
                                             device_id=(flips(me, ANTIPODE),), device_id_type=MESH)
        load = pltpu.make_async_copy(x_hbm, x_vmem, x_sems.at[2])
        store = pltpu.make_async_copy(x_vmem, pair.at[0], x_sems.at[2])
        trade.start()
        load.start()
    for g in (g_in, g_out):
        g.own_load()
    for g in (g_in, g_out):
        g.share(-1)
    for g in (g_in, g_out):
        g.own_store()
    if with_tokens:
        load.wait()
        store.start()
    g_in.wait(0)
    g_in.start(1)
    g_in.share(0)
    g_out.wait(0)
    g_out.start(1)
    g_out.share(0)
    g_in.wait(1)
    g_in.start(2)
    g_in.share(1)
    g_in.wait(2)
    g_in.share(2)
    g_out.wait(1)
    g_in.shared(8)
    g_out.shared(2)
    g_in.finish(7, 8)
    g_out.finish(3, 2)
    if with_tokens:
        trade.wait()
        store.wait()


def gather_layer(shard_in, shard_out, x=None):
    with_tokens = x is not None
    out_shape = [full_shape(shard_in), full_shape(shard_out)]
    scratch = gather_scratch(shard_in) + gather_scratch(shard_out)
    args = [shard_in, shard_out]
    if with_tokens:
        args += [x]
        out_shape += [jax.ShapeDtypeStruct((2,) + x.shape, BF)]
        scratch += [pltpu.VMEM(x.shape, BF), pltpu.SemaphoreType.DMA((3,))]
    return pl.pallas_call(
        functools.partial(gather_kernel, with_tokens), out_shape=out_shape,
        in_specs=[ANY] * len(args), out_specs=[ANY] * len(out_shape), scratch_shapes=scratch,
        compiler_params=pltpu.CompilerParams(collective_id=6 if with_tokens else 0, has_side_effects=True, vmem_limit_bytes=VMEM_LIMIT),
        name='gather_with_tokens' if with_tokens else 'gather_first')(*args)


HB = 512
MT = 512


def gelu_and_slope(z):
    w = z * SQRT_HALF
    phi = 0.5 + 0.5 * lax.erf(w)
    density = jnp.exp2(LOG_DENSITY - w * w * LOG2_E)
    return z * phi, phi + z * density


def forward_kernel(last, trading, n_up, n_down, *refs):
    if not last:
        (h_ref, wi_ref, _, next_in, next_out, wo_full, a_hbm, d_ref, hn_ref, full_in, full_out,
         a_vmem, wo_vmem, a_sem, wo_sem, recv, send, *scratch) = refs
        nxt_in, nxt_out = gather_in(next_in, full_in, scratch[:4]), gather_out(next_out, full_out, scratch[4:])
    else:
        if trading:
            h_ref, wi_ref, _, y_hbm, wo_full, a_hbm, d_ref, r_ref, rb_ref, loss_ref, y_other, *scratch = refs
        else:
            h_ref, wi_ref, _, y_hbm, y_other, wo_full, a_hbm, d_ref, r_ref, rb_ref, loss_ref, *scratch = refs
        a_vmem, wo_vmem, a_sem, wo_sem, recv, send, y_vmem, late, y_sems = scratch
    w_out = Gather(wo_full, pieces_out(wo_full), (recv, send))
    step = pl.program_id(0)
    me = lax.axis_index('data')
    unit = wo_full.shape[1]
    own_blocks = n_down // 2

    def at(s, fn):
        pl.when(step == s)(fn)

    def wo_loads():
        for dev in range(DEVICES):
            yield pltpu.make_async_copy(wo_full.at[dev], wo_vmem.at[pl.ds(dev * unit, unit)], wo_sem)

    def trade_y():
        return pltpu.make_async_remote_copy(src_ref=y_hbm, dst_ref=y_other, send_sem=y_sems.at[0], recv_sem=y_sems.at[1],
                                            device_id=(flips(me, ANTIPODE),), device_id_type=MESH)

    def load_y(which):
        own = which == 0
        return pltpu.make_async_copy(y_hbm if own else y_other, y_vmem.at[which], y_sems.at[2 + which])

    def begin():
        greet_neighbours(*((ANTIPODE,) if trading else ()))
        if not last:
            nxt_in.start(0)
        w_out.start(2)
        w_out.share(1)
        if not last:
            for g in (nxt_in, nxt_out):
                g.own_load()
            for g in (nxt_in, nxt_out):
                g.share(-1)
        else:
            loss_ref[...] = jnp.zeros_like(loss_ref)
            load_y(0).start()
            if not trading:
                load_y(1).start()

    def pass_on():
        w_out.wait(2)
        w_out.share(2)
        if trading:
            trade_y().start()

    def bring_w_out():
        w_out.shared(6)
        for copy in wo_loads():
            copy.start()

    def advance_in(stage):
        nxt_in.wait(stage)
        nxt_in.start(stage + 1)
        nxt_in.share(stage)

    def advance_out():
        nxt_out.wait(0)
        nxt_out.share(0)

    at(0, begin)
    if last:
        at(n_up - 4, pass_on)
        at(n_up - 2, bring_w_out)
    else:
        def stores():
            nxt_in.own_store()
            nxt_out.own_store()

        def second():
            advance_in(0)
            nxt_out.start(0)

        def arrive_in():
            nxt_in.wait(2)
            nxt_in.share(2)
        at(1, stores)
        at(2, second)
        at(n_up - 2, pass_on)
        at(n_up - 1, functools.partial(advance_in, 1))
        at(n_up - 1, bring_w_out)
        at(n_up, advance_out)
        at(n_up + 1, lambda: nxt_out.start(1))
        at(n_up + n_down - 1, arrive_in)

    @pl.when(step < n_up)
    def _():
        base = pl.multiple_of(jnp.minimum(step, n_up - 1) * HB, HB)
        for m in range(h_ref.shape[0] // MT):
            rows = span(m, MT)
            z = jnp.dot(h_ref[rows, :], wi_ref[...], preferred_element_type=F32)
            act, slope = gelu_and_slope(z.astype(BF).astype(F32))
            a_vmem[rows, pl.ds(base, HB)] = act.astype(BF)
            d_ref[rows, :] = slope
        pltpu.make_async_copy(a_vmem.at[:, pl.ds(base, HB)], a_hbm.at[:, pl.ds(base, HB)], a_sem).start()

    def residual(h_next, which, block):
        rows = pl.ds(pl.multiple_of(block * MT, MT), MT)
        error = h_next.astype(F32) - y_vmem[which, rows, :].astype(F32)
        r = error / (own_blocks * MT)
        r_ref[...] = r
        rb_ref[...] = r.astype(BF)
        return error

    @pl.when((step >= n_up) & (step < n_up + n_down))
    def _():
        @pl.when(step == n_up)
        def _():
            pltpu.make_async_copy(wo_vmem, wo_vmem, wo_sem).wait()
            if last:
                load_y(0).wait()
                if not trading:
                    load_y(1).wait()
        block = jnp.clip(step - n_up, 0, n_down - 1)
        base = pl.multiple_of(block * MT, MT)
        branch = jnp.dot(a_vmem[pl.ds(base, MT), :], wo_vmem[...], preferred_element_type=F32)
        h_next = (h_ref[pl.ds(base, MT), :].astype(F32) + branch).astype(BF)
        if not last:
            hn_ref[...] = h_next
        else:
            if trading:
                late[pl.ds(pl.multiple_of((block % own_blocks) * MT, MT), MT), :] = h_next

            @pl.when(step < n_up + own_blocks)
            def _():
                error = residual(h_next, 0, block)
                loss_ref[...] += fold_squares(error)
            if not trading:
                @pl.when(step >= n_up + own_blocks)
                def _():
                    residual(h_next, 1, block - own_blocks)

    final = n_up + n_down - 1
    if trading:
        final += own_blocks

        @pl.when(step == n_up + n_down)
        def _():
            trade_y().wait()
            load_y(1).start()
            load_y(1).wait()

        @pl.when(step >= n_up + n_down)
        def _():
            block = jnp.clip(step - n_up - n_down, 0, own_blocks - 1)
            residual(late[pl.ds(pl.multiple_of(block * MT, MT), MT), :], 1, block)

    def end():
        pltpu.make_async_copy(a_vmem, a_hbm, a_sem).wait()
        w_out.finish(4, 6)
        if not last:
            nxt_out.wait(1)
            nxt_in.shared(8)
            nxt_out.shared(2)
            nxt_in.finish(7, 8)
            nxt_out.finish(3, 2)
    at(final, end)


def forward_layer(h, w_in_full, w_out_part, next_shards=None, y=None, y_other=None):
    tokens, width = h.shape
    hidden = w_in_full.shape[1]
    n_up, n_down = hidden // HB, tokens // MT
    last = next_shards is None
    trading = last and y_other is None
    half = n_down // 2
    up = lambda s: jnp.minimum(s, n_up - 1)
    down = lambda s: jnp.maximum(s - n_up, 0)
    if trading:
        down = lambda s: jnp.where(s < n_up + n_down, jnp.clip(s - n_up, 0, half - 1), s - n_up - half)
    row_block = pl.BlockSpec((MT, width), lambda s: (down(s), 0))
    in_specs = [pl.BlockSpec((tokens, width), lambda s: (0, 0), pipeline_mode=pl.Buffered(1)),
                pl.BlockSpec((width, HB), lambda s: (0, up(s))), ANY]
    out_specs = [ANY, ANY, pl.BlockSpec((tokens, HB), lambda s: (0, up(s)))]
    out_shape = [jax.ShapeDtypeStruct(w_out_part.shape, BF), jax.ShapeDtypeStruct((tokens, hidden), BF), jax.ShapeDtypeStruct((tokens, hidden), F32)]
    scratch = [pltpu.VMEM((tokens, hidden), BF), pltpu.VMEM((hidden, width), BF),
               pltpu.SemaphoreType.DMA, pltpu.SemaphoreType.DMA] + GATHER_SEMS
    args = [h, w_in_full, w_out_part]
    if not last:
        args += list(next_shards)
        in_specs += [ANY, ANY]
        out_specs += [row_block, ANY, ANY]
        out_shape += [jax.ShapeDtypeStruct((tokens, width), BF)] + [full_shape(sh) for sh in next_shards]
        for sh in next_shards:
            scratch += gather_scratch(sh)
    else:
        args += [y] if trading else [y, y_other]
        in_specs += [ANY] if trading else [ANY, ANY]
        out_specs += [row_block, row_block, pl.BlockSpec(SUM_TILE, lambda s: (0, 0))]
        out_shape += [jax.ShapeDtypeStruct((tokens, width), F32), jax.ShapeDtypeStruct((tokens, width), BF), jax.ShapeDtypeStruct(SUM_TILE, F32)]
        if trading:
            out_specs += [ANY]
            out_shape += [jax.ShapeDtypeStruct(y.shape, BF)]
        scratch += [pltpu.VMEM((2,) + y.shape, BF), pltpu.VMEM(y.shape, BF), pltpu.SemaphoreType.DMA((4,))]
    return pl.pallas_call(
        functools.partial(forward_kernel, last, trading, n_up, n_down), grid=(n_up + n_down + (half if trading else 0),),
        in_specs=in_specs, out_specs=out_specs, out_shape=out_shape, scratch_shapes=scratch,
        input_output_aliases={2: 0},
        compiler_params=pltpu.CompilerParams(collective_id=7 if trading else 8 if last else 1, has_side_effects=True, vmem_limit_bytes=VMEM_LIMIT),
        cost_estimate=pl.CostEstimate(flops=4 * tokens * width * hidden, bytes_accessed=70 * 2 ** 20, transcendentals=0),
        name='forward_trade' if trading else 'forward_last' if last else 'forward_gather')(*args)


NB = 512
TILE = 256
OWNERS = (1, 2, 4, 0)
TURNS = 8
TAIL = 8
LEAD = 4


def chip_at(turn):
    chip = lax.shift_right_logical(lax.axis_index('data'), 1)
    near = chip ^ (lax.shift_left(1, turn & 3) & 7)
    return jnp.where(turn < 4, near, 7 - near)


def rounded_sum(lhs_t, rhs, half):
    first = jnp.dot(lhs_t[:, :half], rhs[:half, :], preferred_element_type=F32).astype(BF).astype(F32)
    second = jnp.dot(lhs_t[:, half:], rhs[half:, :], preferred_element_type=F32).astype(BF).astype(F32)
    return first + second


def backward_kernel(with_input_grad, rb_ref, wo_ref, a_ref, d_ref, h_hbm, *refs):
    if with_input_grad:
        wi_ref, r_ref, rn_ref, rbn_ref, gi_out, go_out, *scratch = refs
    else:
        loss_ref, gi_out, go_out, loss_out, *scratch = refs
        *scratch, tiles, tile_send, tile_recv = scratch
    (rbt, ht, e_ref, gi_x, gi_send, gi_recv, go_x, go_recv,
     h_sem, dsend, drecv, gi_sent, go_sent, xrecv, own_sem, credit) = scratch
    step = pl.program_id(0)
    lead = 0 if with_input_grad else LEAD
    me = lax.axis_index('data')
    chip, core = lax.shift_right_logical(me, 1), me & 1
    tokens, width = rb_ref.shape
    half = tokens // 2
    rows_dev = ht.shape[0] // 8
    mine = 4 * rows_dev
    unit = NB // 2
    partner = (flip(me, CORE),)

    def at(s, fn):
        pl.when(step == s)(fn)

    h_base = pl.multiple_of(chip * NB, NB)

    def h_copies():
        for i in range(4):
            source = flip(chip, OWNERS[i]) if OWNERS[i] else chip
            cols = pl.multiple_of(source * 2 * rows_dev, 2 * rows_dev)
            place = pl.multiple_of(h_base + i * 2 * rows_dev, 2 * rows_dev)
            yield pltpu.make_async_copy(h_hbm.at[:, pl.ds(cols, 2 * rows_dev)], e_ref.at[:, pl.ds(place, 2 * rows_dev)], h_sem)

    def begin():
        for copy in h_copies():
            copy.start()
        if lead:
            greet_all()
            tiles[me] = loss_ref[...]
            send_to_all(tiles, tile_send, tile_recv)
        else:
            greet_neighbours()
        if lead:
            for m in range(tokens // MT):
                turn_rb(m)

    def turn_rb(m):
        rbt[:, span(m, MT)] = rb_ref[span(m, MT), :].T

    def turn_h():
        whole = e_ref.at[:, pl.ds(h_base, NB)]
        pltpu.make_async_copy(whole, whole, h_sem).wait()
        for m in range(tokens // TILE):
            cols = span(m, TILE)
            for i in range(4):
                place = pl.multiple_of(h_base + i * 2 * rows_dev, 2 * rows_dev)
                flipped = e_ref[cols, pl.ds(place, 2 * rows_dev)].T
                ht[pl.ds(pl.multiple_of(i * rows_dev + core * mine, rows_dev), rows_dev), cols] = flipped[:rows_dev]
                ht[pl.ds(pl.multiple_of(i * rows_dev + (1 - core) * mine, rows_dev), rows_dev), cols] = flipped[rows_dev:]

    def core_copy(src, dst, index):
        return pltpu.make_async_remote_copy(src_ref=src, dst_ref=dst, send_sem=dsend.at[index], recv_sem=drecv.at[index],
                                            device_id=partner, device_id_type=MESH)

    def gi_core(turn):
        return core_copy(gi_send.at[turn & 1], gi_recv.at[turn & 1], turn & 1)

    def outbox(turn):
        return 4 + (turn & 1 if lead else 0)

    def go_core(turn):
        return core_copy(go_x.at[outbox(turn)], go_recv, 2 + (outbox(turn) - 4))

    def ship(src, dst, i, sent, arrived, kept):
        if i < 3:
            pltpu.make_async_remote_copy(src_ref=src, dst_ref=dst(1 + i), send_sem=sent, recv_sem=arrived,
                                         device_id=(flip(me, 2 * OWNERS[i]),), device_id_type=MESH).start()
        else:
            pltpu.make_async_copy(src, dst(0), kept).start()

    def go_merge(turn):
        go_core(turn).wait_recv()
        go_x[turn] = go_x[turn] + go_recv[...]
        if turn < 3:
            pl.semaphore_signal(credit, inc=1, device_id=partner, device_id_type=MESH)
        ship(go_x.at[turn], lambda slot: go_out.at[slot], turn, go_sent.at[turn % 3], xrecv.at[3 + turn % 3], own_sem.at[1])

    def gi_merge(turn):
        gi_core(turn).wait_recv()
        gi_x[turn] = gi_x[turn] + gi_recv[turn & 1]
        cols = pl.ds(pl.multiple_of(chip_at(turn) * NB, NB), NB)
        for i in range(4):
            ship(gi_x.at[turn, pl.ds(i * rows_dev, rows_dev)], lambda slot: gi_out.at[slot, :, cols],
                 i, gi_sent.at[i % 3], xrecv.at[i % 3], own_sem.at[0])

    at(0, begin)
    turn = jnp.clip(step - lead, 0, TURNS - 1)
    working = (step >= lead) & (step < lead + TURNS)
    base = pl.multiple_of(chip_at(turn) * NB, NB)

    def slopes(turning):
        for m in range(tokens // MT):
            rows = span(m, MT)
            u = lax.dot_general(rb_ref[rows, :], wo_ref[...], NT, preferred_element_type=F32)
            e_ref[rows, pl.ds(base, NB)] = (d_ref[rows, :] * u).astype(BF)
            if turning:
                turn_rb(m)

    if lead:
        pl.when(working)(lambda: slopes(False))
    else:
        at(0, lambda: slopes(True))
        pl.when(working & (step > 0))(lambda: slopes(False))

    at(lead, turn_h)

    if with_input_grad:
        @pl.when(step >= TURNS)
        def _():
            start = pl.multiple_of((jnp.maximum(step - TURNS, 0) % 2) * half, half)
            for m in range(half // MT):
                rows = span(m, MT)
                u = lax.dot_general(e_ref[pl.ds(start + m * MT, MT), :], wi_ref[...], NT, preferred_element_type=F32) + r_ref[rows, :]
                rn_ref[rows, :] = u
                rbn_ref[rows, :] = u.astype(BF)

    pl.when((step >= lead + 2) & (step < lead + TURNS))(lambda: gi_core(turn).wait_send())

    @pl.when(working)
    def _():
        total = rounded_sum(ht[...], e_ref[:, pl.ds(base, NB)], half)
        gi_x[turn] = total[:mine]
        gi_send[turn & 1] = total[mine:]

    last_merge = TURNS if with_input_grad else lead + TURNS - 1
    pl.when((step >= lead + 1) & (step <= last_merge))(lambda: gi_merge(jnp.clip(step - lead - 1, 0, TURNS - 1)))

    @pl.when(working)
    def _():
        gi_core(turn).start()

    def out_grad():
        for m in range(width // MT):
            rows = span(m, MT)
            total = rounded_sum(rbt[rows, :], a_ref[...], half)
            for which in range(2):
                go_x[jnp.where(core == which, jnp.minimum(step, 3), outbox(step)), rows, :] = total[:, which * unit:(which + 1) * unit]

    pl.when((step >= 1 + bool(lead)) & (step < 4))(lambda: go_core(step).wait_send())
    pl.when(step < 4)(out_grad)
    for t in range(4):
        at(t + 1, functools.partial(go_merge, t))
    pl.when((step >= 1) & (step < 4))(lambda: pl.semaphore_wait(credit, 1))
    pl.when(step < 4)(lambda: go_core(step).start())

    def end():
        if lead:
            gi_merge(TURNS - 1)
            loss_out[...] = sum_of_all(tiles, tile_send, tile_recv)
        for t in (TURNS - 2, TURNS - 1):
            gi_core(t).wait_send()
        for t in (2, 3) if lead else (3,):
            go_core(t).wait_send()
        for kind, sent, whole in ((0, gi_sent, gi_out.at[0]), (1, go_sent, go_out.at[0])):
            pltpu.make_async_copy(whole, whole, own_sem.at[kind]).wait()
            for i in range(3):
                pltpu.make_async_copy(whole, whole, sent.at[i]).wait()
                pltpu.make_async_copy(whole, whole, xrecv.at[3 * kind + i]).wait()
    at(TURNS + (TAIL if with_input_grad else LEAD) - 1, end)


def backward_layer(rb, r, h, w_in_full, w_out_full, a, d, with_input_grad, squares):
    tokens, width = rb.shape
    hidden = a.shape[1]
    half = tokens // 2
    rows_dev = width // DEVICES
    lead = 0 if with_input_grad else LEAD
    turn = lambda s: jnp.clip(s - lead, 0, TURNS - 1)
    tail = lambda s: jnp.maximum(s - TURNS, 0)
    in_specs = [pl.BlockSpec((tokens, width), lambda s: (0, 0), pipeline_mode=pl.Buffered(1)),
                pl.BlockSpec((NB, width), lambda s: (chip_at(turn(s)), 0)),
                pl.BlockSpec((tokens, NB), lambda s: (0, chip_at(jnp.minimum(s, 3)))),
                pl.BlockSpec((tokens, NB), lambda s: (0, chip_at(turn(s)))),
                ANY]
    args = [rb, w_out_full, a, d, h]
    out_specs, out_shape = [], []
    if with_input_grad:
        block = lambda s: (tail(s) & 1, lax.shift_right_logical(tail(s), 1))
        in_specs += [pl.BlockSpec((TILE, hidden), lambda s: (lax.shift_right_logical(tail(s), 1), 0)), pl.BlockSpec((half, TILE), block)]
        args += [w_in_full, r]
        out_specs += [pl.BlockSpec((half, TILE), block)] * 2
        out_shape += [jax.ShapeDtypeStruct((tokens, width), F32), jax.ShapeDtypeStruct((tokens, width), BF)]
    else:
        in_specs += [pl.BlockSpec(SUM_TILE, lambda s: (0, 0))]
        args += [squares]
    out_specs += [ANY, ANY]
    out_shape += [jax.ShapeDtypeStruct((4, rows_dev, hidden), F32), jax.ShapeDtypeStruct((4, width, hidden // DEVICES), F32)]
    dma = pltpu.SemaphoreType.DMA
    scratch = [pltpu.VMEM((width, tokens), BF), pltpu.VMEM((8 * rows_dev, tokens), BF), pltpu.VMEM((tokens, hidden), BF),
               pltpu.VMEM((TURNS, 4 * rows_dev, NB), F32), pltpu.VMEM((2, 4 * rows_dev, NB), F32), pltpu.VMEM((2, 4 * rows_dev, NB), F32),
               pltpu.VMEM((5 + bool(lead), width, NB // 2), F32), pltpu.VMEM((width, NB // 2), F32),
               dma, dma((4,)), dma((4,)), dma((3,)), dma((3,)), dma((6,)), dma((2,)), pltpu.SemaphoreType.REGULAR]
    if not with_input_grad:
        out_specs += [pl.BlockSpec(SUM_TILE, lambda s: (0, 0))]
        out_shape += [jax.ShapeDtypeStruct(SUM_TILE, F32)]
        scratch += TILE_SCRATCH
    return pl.pallas_call(
        functools.partial(backward_kernel, with_input_grad), grid=(TURNS + (TAIL if with_input_grad else LEAD),),
        in_specs=in_specs, out_specs=out_specs, out_shape=out_shape, scratch_shapes=scratch,
        compiler_params=pltpu.CompilerParams(collective_id=2 if with_input_grad else 3, has_side_effects=True, vmem_limit_bytes=VMEM_LIMIT),
        cost_estimate=pl.CostEstimate(flops=6 * tokens * width * hidden, bytes_accessed=100 * 2 ** 20, transcendentals=0),
        name='backward' if with_input_grad else 'backward_first')(*args)


class Parts:
    def __init__(self, layers, gi, go, w_in, w_out, vgi, vgo, vw_in, vw_out, sems):
        self.layers = layers
        self.copies = []
        for l in range(layers):
            for src, dst in ((gi[l], vgi.at[l]), (go[l], vgo.at[l]), (w_in.at[l], vw_in.at[l]), (w_out.at[l], vw_out.at[l])):
                self.copies.append((l, pltpu.make_async_copy(src, dst, sems.at[len(self.copies)])))
        self.vgi, self.vgo = vgi, vgo

    def start(self):
        for l in reversed(range(self.layers)):
            for layer, copy in self.copies:
                if layer == l:
                    copy.start()

    def wait(self, l):
        for layer, copy in self.copies:
            if layer == l:
                copy.wait()

    def each(self, l, use_in, use_out, carry):
        share = 1.0 / DEVICES

        def in_rows(i, c):
            rows = pl.ds(pl.multiple_of(i * 8, 8), 8)
            total = self.vgi[l, 0, rows, :] + self.vgi[l, 1, rows, :] + self.vgi[l, 2, rows, :] + self.vgi[l, 3, rows, :]
            return use_in(rows, total * share, c)
        carry = lax.fori_loop(0, self.vgi.shape[2] // 8, in_rows, carry)

        def out_cols(i, c):
            rows = pl.ds(pl.multiple_of(i * LANES, LANES), LANES)
            total = self.vgo[l, 0, rows, :] + self.vgo[l, 1, rows, :] + self.vgo[l, 2, rows, :] + self.vgo[l, 3, rows, :]
            return use_out(rows, (total * share).T, c)
        return lax.fori_loop(0, self.vgo.shape[2] // LANES, out_cols, carry)


def fold_squares(values):
    squares = values * values
    part = jnp.sum(squares.reshape(-1, 8, squares.shape[1]), axis=0)
    return sum(part[:, i:i + LANES] for i in range(0, part.shape[1], LANES))


def perturb_kernel(layers, radius, *refs):
    gi, go = refs[:layers], refs[layers:2 * layers]
    w_in, w_out = refs[2 * layers:2 * layers + 2]
    p_in, p_out = refs[2 * layers + 2:3 * layers + 2], refs[3 * layers + 2:4 * layers + 2]
    vgi, vgo, vw_in, vw_out, g_in, g_out, sems, tiles, send, recv = refs[4 * layers + 2:]
    parts = Parts(layers, gi, go, w_in, w_out, vgi, vgo, vw_in, vw_out, sems)
    parts.start()
    greet_all()
    total = jnp.zeros(SUM_TILE, F32)
    for l in reversed(range(layers)):
        parts.wait(l)

        def use_in(rows, mean, carry, l=l):
            g_in[l, rows, :] = mean
            return carry + fold_squares(mean)

        def use_out(rows, mean, carry, l=l):
            g_out[l, :, rows] = mean
            return carry + fold_squares(mean)
        total = parts.each(l, use_in, use_out, total)
    tiles[lax.axis_index('data')] = jnp.full(SUM_TILE, jnp.sum(total), F32)
    send_to_all(tiles, send, recv)
    norm = jnp.sqrt(sum_of_all(tiles, send, recv))
    scale = (radius / norm)[0:1, 0:1]
    for l in range(layers):
        def in_rows(i, carry, l=l):
            rows = pl.ds(pl.multiple_of(i * 16, 16), 16)
            p_in[l][rows, :] = (vw_in[l, rows, :] + scale * g_in[l, rows, :]).astype(BF)
            return carry
        lax.fori_loop(0, p_in[l].shape[0] // 16, in_rows, 0)

        def out_rows(i, carry, l=l):
            rows = pl.ds(pl.multiple_of(i * 64, 64), 64)
            p_out[l][rows, :] = (vw_out[l, rows, :] + scale * g_out[l, rows, :]).astype(BF)
            return carry
        lax.fori_loop(0, p_out[l].shape[0] // 64, out_rows, 0)


def update_kernel(layers, *refs):
    gi, go = refs[:layers], refs[layers:2 * layers]
    w_in, w_out, new_in, new_out, vgi, vgo, vw_in, vw_out, sems, done = refs[2 * layers:]
    parts = Parts(layers, gi, go, w_in, w_out, vgi, vgo, vw_in, vw_out, sems)
    parts.start()
    outs = []
    for l in reversed(range(layers)):
        parts.wait(l)

        def use_in(rows, mean, carry, l=l):
            vw_in[l, rows, :] = vw_in[l, rows, :] - LEARN_RATE * mean
            return carry

        def use_out(rows, mean, carry, l=l):
            vw_out[l, :, rows] = vw_out[l, :, rows] - LEARN_RATE * mean
            return carry
        parts.each(l, use_in, use_out, 0)
        for src, dst in ((vw_in.at[l], new_in.at[l]), (vw_out.at[l], new_out.at[l])):
            outs.append(pltpu.make_async_copy(src, dst, done.at[len(outs)]))
            outs[-1].start()
    for copy in outs:
        copy.wait()


def parts_scratch(gi, go, w_in, w_out):
    layers = len(gi)
    return [pltpu.VMEM((layers,) + gi[0].shape, F32), pltpu.VMEM((layers,) + go[0].shape, F32),
            pltpu.VMEM(w_in.shape, F32), pltpu.VMEM(w_out.shape, F32)]


def perturb(gi, go, w_in, w_out, radius):
    layers = len(gi)
    outs = [jax.ShapeDtypeStruct(w_in.shape[1:], BF)] * layers + [jax.ShapeDtypeStruct(w_out.shape[1:], BF)] * layers
    res = pl.pallas_call(
        functools.partial(perturb_kernel, layers, radius), out_shape=outs,
        in_specs=[ANY] * (2 * layers + 2), out_specs=[pl.BlockSpec(memory_space=pltpu.VMEM)] * (2 * layers),
        scratch_shapes=parts_scratch(gi, go, w_in, w_out) + [
            pltpu.VMEM(w_in.shape, F32), pltpu.VMEM(w_out.shape, F32), pltpu.SemaphoreType.DMA((4 * layers,))] + TILE_SCRATCH,
        compiler_params=pltpu.CompilerParams(collective_id=4, has_side_effects=True, vmem_limit_bytes=VMEM_LIMIT),
        name='perturb')(*gi, *go, w_in, w_out)
    return res[:layers], res[layers:]


def update(gi, go, w_in, w_out):
    layers = len(gi)
    return pl.pallas_call(
        functools.partial(update_kernel, layers),
        out_shape=[jax.ShapeDtypeStruct(w_in.shape, F32), jax.ShapeDtypeStruct(w_out.shape, F32)],
        in_specs=[ANY] * (2 * layers + 2), out_specs=[ANY, ANY],
        scratch_shapes=parts_scratch(gi, go, w_in, w_out) + [
            pltpu.SemaphoreType.DMA((4 * layers,)), pltpu.SemaphoreType.DMA((2 * layers,))],
        compiler_params=pltpu.CompilerParams(vmem_limit_bytes=VMEM_LIMIT), name='update')(*gi, *go, w_in, w_out)


def sam_pass(tokens, targets, shards_in, shards_out):
    layers = len(shards_in)
    if tokens.ndim == 2:
        full_in, full_out, tokens = gather_layer(shards_in[0], shards_out[0], tokens)
    else:
        full_in, full_out = gather_layer(shards_in[0], shards_out[0])
    h_cur = tokens.reshape(-1, tokens.shape[-1])
    saved = []
    for layer in range(layers):
        w_in_full = full_in.reshape(-1, full_in.shape[-1])
        if layer + 1 < layers:
            nxt = (shards_in[layer + 1], shards_out[layer + 1])
            wo, act, slope, h_next, full_in, full_out_next = forward_layer(h_cur, w_in_full, full_out, nxt)
        else:
            wo, act, slope, r, rb, squares, *other = forward_layer(h_cur, w_in_full, full_out, None, *targets)
            if other:
                targets = (targets[0], other[0])
        saved.append((h_cur, act, slope, w_in_full, wo.reshape(-1, wo.shape[-1])))
        if layer + 1 < layers:
            h_cur, full_out = h_next, full_out_next
    g_in = [None] * layers
    g_out = [None] * layers
    for layer in reversed(range(layers)):
        h_prev, act, slope, w_in_full, w_out_full = saved[layer]
        res = backward_layer(rb, r, h_prev, w_in_full, w_out_full, act, slope, layer > 0, squares)
        if layer > 0:
            r, rb, g_in[layer], g_out[layer] = res
        else:
            g_in[layer], g_out[layer], squares = res
    return squares, g_in, g_out, tokens, targets


def solution(mesh):
    groups = mesh.shape['data']

    def device_step(x_blk, y_blk, w_in_sh, w_out_sh):
        layers = w_in_sh.shape[0]
        model_dim = w_out_sh.shape[2]
        radius = RHO_FRAC * math.sqrt(layers * model_dim)
        x_tok = x_blk.reshape(-1, model_dim)
        y_tok = y_blk.reshape(-1, model_dim)
        span = range(layers)
        _, g_in, g_out, x_pair, y_pair = sam_pass(x_tok, (y_tok,), [w_in_sh[l].astype(BF) for l in span], [w_out_sh[l].astype(BF) for l in span])
        pert_in, pert_out = perturb(g_in, g_out, w_in_sh, w_out_sh, radius)
        squares, gp_in, gp_out, _, _ = sam_pass(x_pair, y_pair, pert_in, pert_out)
        mean_loss = jnp.sum(squares) * (0.5 / (x_tok.shape[0] * groups))
        new_in, new_out = update(gp_in, gp_out, w_in_sh, w_out_sh)
        return new_in, new_out, mean_loss

    return jax.shard_map(device_step, mesh=mesh,
                         in_specs=(P('data', None, None), P('data', None, None), P(None, 'data', None), P(None, 'data', None)),
                         out_specs=(P(None, 'data', None), P(None, 'data', None), P()),
                         check_vma=False)
```

time: 2830 us -> 1280 us (0.45)
  waiting for transfers between devices: 1420 us -> 0 us
  Pallas kernels: 0 us -> 1260 us
  matrix products: 1030 us -> 0 us
  blocking collectives: 166 us -> 0 us
  other arithmetic: 122 us -> 4.23 us
  starting transfers between devices: 66.4 us -> 0 us
    pallas_call x0 -> x20, Pallas kernels: none -> 1260 us  [the longest x8 578 us: backward_layer(): pl.pallas_call(functools.partial(backward_kernel, with_input_grad), grid=...]
    all_to_all x16 -> x0, waiting for transfers between devices: 1080 us -> none  [scatter_mean(): lax.all_to_all(grad_full.astype(jnp.bfloat16), 'data', 0, 0, tiled=True)]
    dot_general x44 -> x0, matrix products: 1030 us -> none  [the longest x8 372 us: layer_forward(): jnp.dot(h_prev, w_in_l, preferred_element_type=jnp.float32)]
    all_gather x16 -> x0, waiting for transfers between devices: 326 us -> none  [the longest x8 289 us: sam_pass(): w_in_full.append(lax.all_gather(w_in_sh[layer], 'data', axis=0, tiled=True))]
    psum x2 -> x0, blocking collectives: 166 us -> none  [the longest x1 133 us: device_step(): mean_loss = lax.psum(pert_loss, 'data') / groups]
    reduce_sum x18 -> x1, other arithmetic: 92.4 us -> 1.29 us  [device_step(): mean_loss = jnp.sum(squares) * (0.5 / (x_tok.shape[0] * groups))]
    all_to_all x16 -> x0, starting transfers between devices: 65.4 us -> none  [scatter_mean(): lax.all_to_all(grad_full.astype(jnp.bfloat16), 'data', 0, 0, tiled=True)]
  transfers between devices with their start and end apart: 32 -> 0, of which waited for: 31 -> 0; matrix products, arithmetic and copies ran while one was open for 37% -> 0% of each run, Pallas kernels for 0% -> 0%
where the time goes in v2:
time: 1280 us; the launch traced here: 1270 us
  Pallas kernels  1260 us (98%)
    pallas_call x8, Pallas kernels, backward_layer(): pl.pallas_call(functools.partial(backward_kernel, with_input_grad), grid=...  578 us
    pallas_call x8, Pallas kernels, forward_layer(): pl.pallas_call(functools.partial(forward_kernel, last, trading, n_up, n_d...  505 us
    pallas_call x2, Pallas kernels, gather_layer(): pl.pallas_call(functools.partial(gather_kernel, with_tokens), out_shape=o...  139 us

profile of v2, /device:TPU:0, one launch (start us, length us, event | category | flops | bytes accessed | tf_op | source)
XLA Modules:
  0.0 1271.1 jit_solution(11686603729782052634)
XLA Ops:
  0.6 0.0 copy-start
  0.6 2.6 convert.12
  3.3 1.4 slice_bitcast_fusion.1
  4.7 0.0 copy-done
  4.7 0.3 convert.13
  5.0 1.4 slice_bitcast_fusion
  6.4 93.6 %gather_with_tokens.1 = (bf16[16,64,4096]{2,1,0:T(8,128)(2,1)}, bf16[16,256,1024]{2,1,0:T(8,128)(2,1)}, bf16[2,1024,1024]{2,1,0:T(8,128)(2,1)}) custom-call(bf16[64,4096]{1,0:T(8,128)(2,1)} %get-tuple-element.192.refs_0_, bf16[256,1024]{1,0:T(8,128)(2,1)} %get-tuple-element.188.refs_1_, bf16[1024,1024]{1,0:T(8,128)(2,1)} %bitcast.35), custom_call_target="tpu_custom_call" | custom-call | tf_op jit(solution)/shard_map/gather_with_tokens/pallas_call | solution.py:233
  100.0 62.4 %forward_gather.6 = (bf16[16,256,1024]{2,1,0:T(8,128)(2,1)}, bf16[2048,4096]{1,0:T(8,128)(2,1)}, f32[2048,4096]{1,0:T(8,128)}, bf16[2048,1024]{1,0:T(8,128)(2,1)...) custom-call(bf16[2048,1024]{1,0:T(8,128)(2,1)} %bitcast.40, ...), custom_call_target="tpu_custom_call", output_to_operand_aliasing={{0}: (2, {})} | custom-call | flops 34359738368 | bytes 73400320 | tf_op jit(solution)/shard_map/forward_gather/pallas_call | solution.py:454
  162.4 61.5 %forward_gather.7 = (bf16[16,256,1024]{2,1,0:T(8,128)(2,1)}, bf16[2048,4096]{1,0:T(8,128)(2,1)}, f32[2048,4096]{1,0:T(8,128)}, bf16[2048,1024]{1,0:T(8,128)(2,1)...) custom-call(bf16[2048,1024]{1,0:T(8,128)(2,1)} %get-tuple-element.97.refs_0_.h_hb, ...), custom_call_target="tpu_custom_call", output_to_operand_aliasing={{0}: (2, {})} | custom-call | flops 34359738368 | bytes 73400320 | tf_op jit(solution)/shard_map/forward_gather/pallas_call | solution.py:454
  223.9 61.5 %forward_gather.8 = (bf16[16,256,1024]{2,1,0:T(8,128)(2,1)}, bf16[2048,4096]{1,0:T(8,128)(2,1)}, f32[2048,4096]{1,0:T(8,128)}, bf16[2048,1024]{1,0:T(8,128)(2,1)...) custom-call(bf16[2048,1024]{1,0:T(8,128)(2,1)} %get-tuple-element.100.refs_0_.h_h, ...), custom_call_target="tpu_custom_call", output_to_operand_aliasing={{0}: (2, {})} | custom-call | flops 34359738368 | bytes 73400320 | tf_op jit(solution)/shard_map/forward_gather/pallas_call | solution.py:454
  285.4 74.9 %forward_trade.1 = (bf16[16,256,1024]{2,1,0:T(8,128)(2,1)}, bf16[2048,4096]{1,0:T(8,128)(2,1)}, f32[2048,4096]{1,0:T(8,128)}, f32[2048,1024]{1,0:T(8,128)}, bf16...) custom-call(bf16[2048,1024]{1,0:T(8,128)(2,1)} %get-tuple-element.103, ...), custom_call_target="tpu_custom_call", output_to_operand_aliasing={{0}: (2, {})} | custom-call | flops 34359738368 | bytes 73400320 | tf_op jit(solution)/shard_map/forward_trade/pallas_call | solution.py:454
  360.3 74.7 %backward.6 = (f32[2048,1024]{1,0:T(8,128)}, bf16[2048,1024]{1,0:T(8,128)(2,1)}, f32[4,64,4096]{2,1,0:T(8,128)}, f32[4,1024,256]{2,1,0:T(8,128)}) custom-call(bf16[2048,1024]{1,0:T(8,128)(2,1)} %get-tuple-element.106.rb_ref, bf16[4096,1024]{1,0:T(8,128)(2,1)} %bitcast.62, bf16[2048,4096]{1,0:T(8,128)(2,1)} %get-tuple-element.108.a_ref, ...), custom_call_target="tpu_custom_call" | custom-call | flops 51539607552 | bytes 104857600 | tf_op jit(solution)/shard_map/backward/pallas_call | solution.py:687
  435.0 73.7 %backward.7 = (f32[2048,1024]{1,0:T(8,128)}, bf16[2048,1024]{1,0:T(8,128)(2,1)}, f32[4,64,4096]{2,1,0:T(8,128)}, f32[4,1024,256]{2,1,0:T(8,128)}) custom-call(bf16[2048,1024]{1,0:T(8,128)(2,1)} %get-tuple-element.111.rb_ref, bf16[4096,1024]{1,0:T(8,128)(2,1)} %bitcast.60, bf16[2048,4096]{1,0:T(8,128)(2,1)} %get-tuple-element.113.a_ref, ...), custom_call_target="tpu_custom_call" | custom-call | flops 51539607552 | bytes 104857600 | tf_op jit(solution)/shard_map/backward/pallas_call | solution.py:687
  508.8 73.7 %backward.8 = (f32[2048,1024]{1,0:T(8,128)}, bf16[2048,1024]{1,0:T(8,128)(2,1)}, f32[4,64,4096]{2,1,0:T(8,128)}, f32[4,1024,256]{2,1,0:T(8,128)}) custom-call(bf16[2048,1024]{1,0:T(8,128)(2,1)} %get-tuple-element.116.rb_ref, bf16[4096,1024]{1,0:T(8,128)(2,1)} %bitcast.58, bf16[2048,4096]{1,0:T(8,128)(2,1)} %get-tuple-element.118.a_ref, ...), custom_call_target="tpu_custom_call" | custom-call | flops 51539607552 | bytes 104857600 | tf_op jit(solution)/shard_map/backward/pallas_call | solution.py:687
  582.5 67.2 %backward_first.2 = (f32[4,64,4096]{2,1,0:T(8,128)}, f32[4,1024,256]{2,1,0:T(8,128)}, f32[8,128]{1,0:T(8,128)}) custom-call(bf16[2048,1024]{1,0:T(8,128)(2,1)} %get-tuple-element.121.rb_ref, bf16[4096,1024]{1,0:T(8,128)(2,1)} %bitcast.37, bf16[2048,4096]{1,0:T(8,128)(2,1)} %get-tuple-element.123.a_ref, f32[2048,4096]{1,0:T(8,128)} %get-tuple-element.124.d_ref, ...), custom_call_target="tpu_custom_call" | custom-call | flops 51539607552 | bytes 104857600 | tf_op jit(solution)/shard_map/backward_first/pallas_call | solution.py:687
  649.7 21.0 %perturb.1 = (bf16[64,4096]{1,0:T(8,128)(2,1)}, bf16[64,4096]{1,0:T(8,128)(2,1)}, bf16[64,4096]{1,0:T(8,128)(2,1)}, bf16[64,4096]{1,0:T(8,128)(2,1)}, bf16[256,1...) custom-call(f32[4,64,4096]{2,1,0:T(8,128)} %get-tuple-element.126.refs_0_, ...), custom_call_target="tpu_custom_call" | custom-call | tf_op jit(solution)/shard_map/perturb/pallas_call | solution.py:808
  670.7 45.1 %gather_first.1 = (bf16[16,64,4096]{2,1,0:T(8,128)(2,1)}, bf16[16,256,1024]{2,1,0:T(8,128)(2,1)}) custom-call(bf16[64,4096]{1,0:T(8,128)(2,1)} %get-tuple-element.134.refs_0_, bf16[256,1024]{1,0:T(8,128)(2,1)} %get-tuple-element.135.refs_1_), custom_call_target="tpu_custom_call" | custom-call | tf_op jit(solution)/shard_map/gather_first/pallas_call | solution.py:233
  715.8 62.4 %forward_gather.9 = (bf16[16,256,1024]{2,1,0:T(8,128)(2,1)}, bf16[2048,4096]{1,0:T(8,128)(2,1)}, f32[2048,4096]{1,0:T(8,128)}, bf16[2048,1024]{1,0:T(8,128)(2,1)...) custom-call(bf16[2048,1024]{1,0:T(8,128)(2,1)} %bitcast.42, ...), custom_call_target="tpu_custom_call", output_to_operand_aliasing={{0}: (2, {})} | custom-call | flops 34359738368 | bytes 73400320 | tf_op jit(solution)/shard_map/forward_gather/pallas_call | solution.py:454
  778.2 61.4 %forward_gather.10 = (bf16[16,256,1024]{2,1,0:T(8,128)(2,1)}, bf16[2048,4096]{1,0:T(8,128)(2,1)}, f32[2048,4096]{1,0:T(8,128)}, bf16[2048,1024]{1,0:T(8,128)(2,1...) custom-call(bf16[2048,1024]{1,0:T(8,128)(2,1)} %get-tuple-element.140.refs_0_.h_, ...), custom_call_target="tpu_custom_call", output_to_operand_aliasing={{0}: (2, {})} | custom-call | flops 34359738368 | bytes 73400320 | tf_op jit(solution)/shard_map/forward_gather/pallas_call | solution.py:454
  839.6 61.4 %forward_gather.11 = (bf16[16,256,1024]{2,1,0:T(8,128)(2,1)}, bf16[2048,4096]{1,0:T(8,128)(2,1)}, f32[2048,4096]{1,0:T(8,128)}, bf16[2048,1024]{1,0:T(8,128)(2,1...) custom-call(bf16[2048,1024]{1,0:T(8,128)(2,1)} %get-tuple-element.145.refs_0_.h_, ...), custom_call_target="tpu_custom_call", output_to_operand_aliasing={{0}: (2, {})} | custom-call | flops 34359738368 | bytes 73400320 | tf_op jit(solution)/shard_map/forward_gather/pallas_call | solution.py:454
  901.0 59.9 %forward_last.1 = (bf16[16,256,1024]{2,1,0:T(8,128)(2,1)}, bf16[2048,4096]{1,0:T(8,128)(2,1)}, f32[2048,4096]{1,0:T(8,128)}, f32[2048,1024]{1,0:T(8,128)}, bf16[2048,1024]{1,0:T(8,128)(2,1)}, /*index=5*/f32[8,128]{1,0:T(8,128)}) custom-call(bf16[2048,1024]{1,0:T(8,128)(2,1)} %get-tuple-element.150.refs_0_.h_hbm, ...), custom_call_target="tpu_custom_call", output_to_operand_aliasing={{0}: (2, {})} | custom-call | flops 34359738368 | bytes 73400320 | tf_op jit(solution)/shard_map/forward_last/pallas_call | solution.py:454
  960.9 74.0 %backward.9 = (f32[2048,1024]{1,0:T(8,128)}, bf16[2048,1024]{1,0:T(8,128)(2,1)}, f32[4,64,4096]{2,1,0:T(8,128)}, f32[4,1024,256]{2,1,0:T(8,128)}) custom-call(bf16[2048,1024]{1,0:T(8,128)(2,1)} %get-tuple-element.154.rb_ref, bf16[4096,1024]{1,0:T(8,128)(2,1)} %bitcast.63, bf16[2048,4096]{1,0:T(8,128)(2,1)} %get-tuple-element.156.a_ref, ...), custom_call_target="tpu_custom_call" | custom-call | flops 51539607552 | bytes 104857600 | tf_op jit(solution)/shard_map/backward/pallas_call | solution.py:687
  1034.9 73.8 %backward.10 = (f32[2048,1024]{1,0:T(8,128)}, bf16[2048,1024]{1,0:T(8,128)(2,1)}, f32[4,64,4096]{2,1,0:T(8,128)}, f32[4,1024,256]{2,1,0:T(8,128)}) custom-call(bf16[2048,1024]{1,0:T(8,128)(2,1)} %get-tuple-element.159.rb_ref, bf16[4096,1024]{1,0:T(8,128)(2,1)} %bitcast.61, bf16[2048,4096]{1,0:T(8,128)(2,1)} %get-tuple-element.161.a_ref, ...), custom_call_target="tpu_custom_call" | custom-call | flops 51539607552 | bytes 104857600 | tf_op jit(solution)/shard_map/backward/pallas_call | solution.py:687
  1108.7 73.8 %backward.11 = (f32[2048,1024]{1,0:T(8,128)}, bf16[2048,1024]{1,0:T(8,128)(2,1)}, f32[4,64,4096]{2,1,0:T(8,128)}, f32[4,1024,256]{2,1,0:T(8,128)}) custom-call(bf16[2048,1024]{1,0:T(8,128)(2,1)} %get-tuple-element.164.rb_ref, bf16[4096,1024]{1,0:T(8,128)(2,1)} %bitcast.59, bf16[2048,4096]{1,0:T(8,128)(2,1)} %get-tuple-element.166.a_ref, ...), custom_call_target="tpu_custom_call" | custom-call | flops 51539607552 | bytes 104857600 | tf_op jit(solution)/shard_map/backward/pallas_call | solution.py:687
  1182.5 67.3 %backward_first.3 = (f32[4,64,4096]{2,1,0:T(8,128)}, f32[4,1024,256]{2,1,0:T(8,128)}, f32[8,128]{1,0:T(8,128)}) custom-call(bf16[2048,1024]{1,0:T(8,128)(2,1)} %get-tuple-element.169.rb_ref, bf16[4096,1024]{1,0:T(8,128)(2,1)} %bitcast.39, bf16[2048,4096]{1,0:T(8,128)(2,1)} %get-tuple-element.171.a_ref, f32[2048,4096]{1,0:T(8,128)} %get-tuple-element.172.d_ref, ...), custom_call_target="tpu_custom_call" | custom-call | flops 51539607552 | bytes 104857600 | tf_op jit(solution)/shard_map/backward_first/pallas_call | solution.py:687
  1249.8 1.3 reduce_sum.9
  1251.8 17.8 %update.1 = (f32[4,64,4096]{2,1,0:T(8,128)}, f32[4,256,1024]{2,1,0:T(8,128)}) custom-call(f32[4,64,4096]{2,1,0:T(8,128)} %get-tuple-element.174.refs_0_, f32[4,64,4096]{2,1,0:T(8,128)} %get-tuple-element.175.refs_1_, f32[4,64,4096]{2,1,0:T(8,128)} %get-tuple-element.176.refs_2_, f32[4,64,4096]{2,1,0:T(8,128)} %get-tuple-element.177.refs_3_, ...), custom_call_target="tpu_custom_call" | custom-call | tf_op jit(solution)/shard_map/update/pallas_call | solution.py:820
Async XLA Ops:
  0.6 4.0 copy-start

commit v3 on v2

--- a/solution.py
+++ b/solution.py
@@ -24,6 +24,10 @@
 ANTIPODE = AX_X | AX_Y | AX_Z
 COLOR_ORDERS = ((AX_X, AX_Y, AX_Z), (AX_Y, AX_Z, AX_X), (AX_Z, AX_X, AX_Y))
 ANY = pl.BlockSpec(memory_space=pl.ANY)
+
+
+def origin(step):
+    return 0, 0
 
 
 def span(index, size):
@@ -428,7 +432,7 @@
     if trading:
         down = lambda s: jnp.where(s < n_up + n_down, jnp.clip(s - n_up, 0, half - 1), s - n_up - half)
     row_block = pl.BlockSpec((MT, width), lambda s: (down(s), 0))
-    in_specs = [pl.BlockSpec((tokens, width), lambda s: (0, 0), pipeline_mode=pl.Buffered(1)),
+    in_specs = [pl.BlockSpec((tokens, width), origin, pipeline_mode=pl.Buffered(1)),
                 pl.BlockSpec((width, HB), lambda s: (0, up(s))), ANY]
     out_specs = [ANY, ANY, pl.BlockSpec((tokens, HB), lambda s: (0, up(s)))]
     out_shape = [jax.ShapeDtypeStruct(w_out_part.shape, BF), jax.ShapeDtypeStruct((tokens, hidden), BF), jax.ShapeDtypeStruct((tokens, hidden), F32)]
@@ -445,7 +449,7 @@
     else:
         args += [y] if trading else [y, y_other]
         in_specs += [ANY] if trading else [ANY, ANY]
-        out_specs += [row_block, row_block, pl.BlockSpec(SUM_TILE, lambda s: (0, 0))]
+        out_specs += [row_block, row_block, pl.BlockSpec(SUM_TILE, origin)]
         out_shape += [jax.ShapeDtypeStruct((tokens, width), F32), jax.ShapeDtypeStruct((tokens, width), BF), jax.ShapeDtypeStruct(SUM_TILE, F32)]
         if trading:
             out_specs += [ANY]
@@ -465,7 +469,7 @@
 OWNERS = (1, 2, 4, 0)
 TURNS = 8
 TAIL = 8
-LEAD = 4
+LEAD = 8
 
 
 def chip_at(turn):
@@ -480,14 +484,15 @@
     return first + second
 
 
-def backward_kernel(with_input_grad, rb_ref, wo_ref, a_ref, d_ref, h_hbm, *refs):
+def backward_kernel(with_input_grad, rb_ref, wo_hbm, a_hbm, d_hbm, h_hbm, *refs):
     if with_input_grad:
-        wi_ref, r_ref, rn_ref, rbn_ref, gi_out, go_out, *scratch = refs
+        wi_hbm, r_hbm, rn_ref, rbn_ref, gi_out, go_out, *scratch = refs
+        *scratch, wi_buf, r_buf, wi_sem, r_sem = scratch
     else:
         loss_ref, gi_out, go_out, loss_out, *scratch = refs
         *scratch, tiles, tile_send, tile_recv = scratch
-    (rbt, ht, e_ref, gi_x, gi_send, gi_recv, go_x, go_recv,
-     h_sem, dsend, drecv, gi_sent, go_sent, xrecv, own_sem, credit) = scratch
+    (rbt, ht, e_ref, wo_buf, a_buf, d_buf, gi_x, gi_send, gi_recv, go_x, go_send, go_recv,
+     h_sem, wo_sem, a_sem, d_sem, gi_dsend, gi_drecv, go_dsend, go_drecv, gi_sent, go_sent, xrecv, own_sem) = scratch
     step = pl.program_id(0)
     lead = 0 if with_input_grad else LEAD
     me = lax.axis_index('data')
@@ -498,9 +503,32 @@
     mine = 4 * rows_dev
     unit = NB // 2
     partner = (flip(me, CORE),)
+    a_slots = a_buf.shape[0]
 
     def at(s, fn):
         pl.when(step == s)(fn)
+
+    def hidden_cols(turn):
+        return pl.ds(pl.multiple_of(chip_at(turn) * NB, NB), NB)
+
+    def wo_copy(turn):
+        return pltpu.make_async_copy(wo_hbm.at[hidden_cols(turn)], wo_buf.at[turn & 1], wo_sem.at[turn & 1])
+
+    def d_copy(turn):
+        return pltpu.make_async_copy(d_hbm.at[:, hidden_cols(turn)], d_buf.at[turn & 1], d_sem.at[turn & 1])
+
+    def a_copy(owner):
+        slot = owner & (a_slots - 1)
+        return pltpu.make_async_copy(a_hbm.at[:, hidden_cols(owner)], a_buf.at[slot], a_sem.at[slot])
+
+    def wi_copy(block):
+        rows = pl.ds(pl.multiple_of(block * TILE, TILE), TILE)
+        return pltpu.make_async_copy(wi_hbm.at[rows], wi_buf.at[block & 1], wi_sem.at[block & 1])
+
+    def r_copy(index):
+        rows = pl.ds(pl.multiple_of((index & 1) * half, half), half)
+        cols = pl.ds(pl.multiple_of(lax.shift_right_logical(index, 1) * TILE, TILE), TILE)
+        return pltpu.make_async_copy(r_hbm.at[rows, cols], r_buf.at[index & 1], r_sem.at[index & 1])
 
     h_base = pl.multiple_of(chip * NB, NB)
 
@@ -512,17 +540,23 @@
             yield pltpu.make_async_copy(h_hbm.at[:, pl.ds(cols, 2 * rows_dev)], e_ref.at[:, pl.ds(place, 2 * rows_dev)], h_sem)
 
     def begin():
+        first = jnp.int32(0)
+        pair = (first, first + 1)
+        owners = tuple(first + i for i in range(a_slots))
+        starts = [(wo_copy, pair), (d_copy, pair), (a_copy, owners)]
+        for copy, indices in starts[::-1] if lead else starts:
+            for i in indices:
+                copy(i).start()
         for copy in h_copies():
             copy.start()
         if lead:
             greet_all()
             tiles[me] = loss_ref[...]
             send_to_all(tiles, tile_send, tile_recv)
+            for m in range(tokens // MT):
+                turn_rb(m)
         else:
             greet_neighbours()
-        if lead:
-            for m in range(tokens // MT):
-                turn_rb(m)
 
     def turn_rb(m):
         rbt[:, span(m, MT)] = rb_ref[span(m, MT), :].T
@@ -538,18 +572,19 @@
                 ht[pl.ds(pl.multiple_of(i * rows_dev + core * mine, rows_dev), rows_dev), cols] = flipped[:rows_dev]
                 ht[pl.ds(pl.multiple_of(i * rows_dev + (1 - core) * mine, rows_dev), rows_dev), cols] = flipped[rows_dev:]
 
-    def core_copy(src, dst, index):
-        return pltpu.make_async_remote_copy(src_ref=src, dst_ref=dst, send_sem=dsend.at[index], recv_sem=drecv.at[index],
-                                            device_id=partner, device_id_type=MESH)
+    def core_copy(src, dst, send, recv):
+        return pltpu.make_async_remote_copy(src_ref=src, dst_ref=dst, send_sem=send, recv_sem=recv, device_id=partner, device_id_type=MESH)
 
     def gi_core(turn):
-        return core_copy(gi_send.at[turn & 1], gi_recv.at[turn & 1], turn & 1)
-
-    def outbox(turn):
-        return 4 + (turn & 1 if lead else 0)
-
-    def go_core(turn):
-        return core_copy(go_x.at[outbox(turn)], go_recv, 2 + (outbox(turn) - 4))
+        slot = turn & 1
+        return core_copy(gi_send.at[slot], gi_recv.at[slot], gi_dsend.at[slot], gi_drecv.at[slot])
+
+    def outbox(piece):
+        return piece & (go_send.shape[0] - 1)
+
+    def go_core(piece):
+        out, slot = outbox(piece), piece & 3
+        return core_copy(go_send.at[out], go_recv.at[slot], go_dsend.at[out], go_drecv.at[slot])
 
     def ship(src, dst, i, sent, arrived, kept):
         if i < 3:
@@ -558,17 +593,31 @@
         else:
             pltpu.make_async_copy(src, dst(0), kept).start()
 
-    def go_merge(turn):
-        go_core(turn).wait_recv()
-        go_x[turn] = go_x[turn] + go_recv[...]
-        if turn < 3:
-            pl.semaphore_signal(credit, inc=1, device_id=partner, device_id_type=MESH)
-        ship(go_x.at[turn], lambda slot: go_out.at[slot], turn, go_sent.at[turn % 3], xrecv.at[3 + turn % 3], own_sem.at[1])
+    def go_merge(piece):
+        owner, part = piece & 3, piece >> 2
+        rows = span(part, MT)
+        go_core(piece).wait_recv()
+        go_x[owner, rows, :] = go_x[owner, rows, :] + go_recv[piece & 3]
+        ship(go_x.at[owner, rows], lambda slot: go_out.at[slot, rows], owner, go_sent.at[owner % 3], xrecv.at[3 + owner % 3], own_sem.at[1])
+
+    def out_grad(owner, part, piece):
+        rows = pl.ds(pl.multiple_of(part * MT, MT), MT)
+        total = rounded_sum(rbt[rows, :], a_buf[owner & (a_slots - 1)], half)
+
+        @pl.when(core == 0)
+        def _():
+            go_x[owner, rows, :] = total[:, :unit]
+            go_send[outbox(piece)] = total[:, unit:]
+
+        @pl.when(core == 1)
+        def _():
+            go_x[owner, rows, :] = total[:, unit:]
+            go_send[outbox(piece)] = total[:, :unit]
 
     def gi_merge(turn):
         gi_core(turn).wait_recv()
         gi_x[turn] = gi_x[turn] + gi_recv[turn & 1]
-        cols = pl.ds(pl.multiple_of(chip_at(turn) * NB, NB), NB)
+        cols = hidden_cols(turn)
         for i in range(4):
             ship(gi_x.at[turn, pl.ds(i * rows_dev, rows_dev)], lambda slot: gi_out.at[slot, :, cols],
                  i, gi_sent.at[i % 3], xrecv.at[i % 3], own_sem.at[0])
@@ -578,11 +627,33 @@
     working = (step >= lead) & (step < lead + TURNS)
     base = pl.multiple_of(chip_at(turn) * NB, NB)
 
+    if lead:
+        @pl.when(step < lead)
+        def _():
+            piece = jnp.minimum(step, 7)
+            owner = piece & 3
+            pl.when(piece < 4)(lambda: a_copy(owner).wait())
+            pl.when(piece >= 4)(lambda: go_core(piece).wait_send())
+            out_grad(owner, lax.shift_right_logical(piece, 2), piece)
+        for p in range(8):
+            at(p + 2, functools.partial(go_merge, p))
+        pl.when(step < lead)(lambda: go_core(step).start())
+
+    @pl.when(working)
+    def _():
+        @pl.when((step > lead) & (turn < TURNS - 1))
+        def _():
+            wo_copy(turn + 1).start()
+            d_copy(turn + 1).start()
+        wo_copy(turn).wait()
+        d_copy(turn).wait()
+
     def slopes(turning):
+        slot = turn & 1
         for m in range(tokens // MT):
             rows = span(m, MT)
-            u = lax.dot_general(rb_ref[rows, :], wo_ref[...], NT, preferred_element_type=F32)
-            e_ref[rows, pl.ds(base, NB)] = (d_ref[rows, :] * u).astype(BF)
+            u = lax.dot_general(rb_ref[rows, :], wo_buf[slot], NT, preferred_element_type=F32)
+            e_ref[rows, pl.ds(base, NB)] = (d_buf[slot, rows, :] * u).astype(BF)
             if turning:
                 turn_rb(m)
 
@@ -595,12 +666,31 @@
     at(lead, turn_h)
 
     if with_input_grad:
+        def ahead():
+            for i in range(2):
+                wi_copy(jnp.int32(i)).start()
+                r_copy(jnp.int32(i)).start()
+        at(TURNS - 2, ahead)
+
         @pl.when(step >= TURNS)
         def _():
-            start = pl.multiple_of((jnp.maximum(step - TURNS, 0) % 2) * half, half)
+            index = jnp.maximum(step - TURNS, 0)
+            block = lax.shift_right_logical(index, 1)
+            side = index & 1
+
+            @pl.when((index > 0) & (index < TAIL - 1))
+            def _():
+                r_copy(index + 1).start()
+
+            @pl.when((side == 0) & (index > 0) & (index < TAIL - 2))
+            def _():
+                wi_copy(block + 1).start()
+            pl.when(side == 0)(lambda: wi_copy(block).wait())
+            r_copy(index).wait()
             for m in range(half // MT):
                 rows = span(m, MT)
-                u = lax.dot_general(e_ref[pl.ds(start + m * MT, MT), :], wi_ref[...], NT, preferred_element_type=F32) + r_ref[rows, :]
+                left = e_ref[pl.ds(pl.multiple_of(side * half + m * MT, MT), MT), :]
+                u = lax.dot_general(left, wi_buf[block & 1], NT, preferred_element_type=F32) + r_buf[side, rows, :]
                 rn_ref[rows, :] = u
                 rbn_ref[rows, :] = u.astype(BF)
 
@@ -619,19 +709,23 @@
     def _():
         gi_core(turn).start()
 
-    def out_grad():
-        for m in range(width // MT):
-            rows = span(m, MT)
-            total = rounded_sum(rbt[rows, :], a_ref[...], half)
-            for which in range(2):
-                go_x[jnp.where(core == which, jnp.minimum(step, 3), outbox(step)), rows, :] = total[:, which * unit:(which + 1) * unit]
-
-    pl.when((step >= 1 + bool(lead)) & (step < 4))(lambda: go_core(step).wait_send())
-    pl.when(step < 4)(out_grad)
-    for t in range(4):
-        at(t + 1, functools.partial(go_merge, t))
-    pl.when((step >= 1) & (step < 4))(lambda: pl.semaphore_wait(credit, 1))
-    pl.when(step < 4)(lambda: go_core(step).start())
+    if not lead:
+        @pl.when(step < 4)
+        def _():
+            for i in range(2):
+                piece = 2 * jnp.minimum(step, 3) + i
+                owner = piece & 3
+                a_copy(owner).wait()
+                pl.when(step >= 1)(lambda: go_core(piece).wait_send())
+                out_grad(owner, lax.shift_right_logical(piece, 2), piece)
+                pl.when(step < 3)(lambda: a_copy((owner + 2) & 3).start())
+        for p in range(8):
+            at((p >> 1) + 1, functools.partial(go_merge, p))
+
+        @pl.when(step < 4)
+        def _():
+            for part in range(2):
+                go_core(2 * jnp.minimum(step, 3) + part).start()
 
     def end():
         if lead:
@@ -639,8 +733,8 @@
             loss_out[...] = sum_of_all(tiles, tile_send, tile_recv)
         for t in (TURNS - 2, TURNS - 1):
             gi_core(t).wait_send()
-        for t in (2, 3) if lead else (3,):
-            go_core(t).wait_send()
+        for piece in range(go_send.shape[0]):
+            go_core(piece).wait_send()
         for kind, sent, whole in ((0, gi_sent, gi_out.at[0]), (1, go_sent, go_out.at[0])):
             pltpu.make_async_copy(whole, whole, own_sem.at[kind]).wait()
             for i in range(3):
@@ -654,36 +748,35 @@
     hidden = a.shape[1]
     half = tokens // 2
     rows_dev = width // DEVICES
-    lead = 0 if with_input_grad else LEAD
-    turn = lambda s: jnp.clip(s - lead, 0, TURNS - 1)
     tail = lambda s: jnp.maximum(s - TURNS, 0)
-    in_specs = [pl.BlockSpec((tokens, width), lambda s: (0, 0), pipeline_mode=pl.Buffered(1)),
-                pl.BlockSpec((NB, width), lambda s: (chip_at(turn(s)), 0)),
-                pl.BlockSpec((tokens, NB), lambda s: (0, chip_at(jnp.minimum(s, 3)))),
-                pl.BlockSpec((tokens, NB), lambda s: (0, chip_at(turn(s)))),
-                ANY]
+    in_specs = [pl.BlockSpec((tokens, width), origin, pipeline_mode=pl.Buffered(1))] + [ANY] * 4
     args = [rb, w_out_full, a, d, h]
     out_specs, out_shape = [], []
+    dma = pltpu.SemaphoreType.DMA
+    two, three, four = dma((2,)), dma((3,)), dma((4,))
+    small = (4 * rows_dev, NB)
+    piece = (MT, NB // 2)
+    scratch = [pltpu.VMEM((width, tokens), BF), pltpu.VMEM((8 * rows_dev, tokens), BF), pltpu.VMEM((tokens, hidden), BF),
+               pltpu.VMEM((2, NB, width), BF), pltpu.VMEM((2 if with_input_grad else 4, tokens, NB), BF), pltpu.VMEM((2, tokens, NB), F32),
+               pltpu.VMEM((TURNS,) + small, F32), pltpu.VMEM((2,) + small, F32), pltpu.VMEM((2,) + small, F32),
+               pltpu.VMEM((4, width, NB // 2), F32), pltpu.VMEM((2 if with_input_grad else 4,) + piece, F32), pltpu.VMEM((4,) + piece, F32),
+               dma, two, four, two, two, two, four, four, three, three, dma((6,)), two]
     if with_input_grad:
         block = lambda s: (tail(s) & 1, lax.shift_right_logical(tail(s), 1))
-        in_specs += [pl.BlockSpec((TILE, hidden), lambda s: (lax.shift_right_logical(tail(s), 1), 0)), pl.BlockSpec((half, TILE), block)]
+        in_specs += [ANY, ANY]
         args += [w_in_full, r]
         out_specs += [pl.BlockSpec((half, TILE), block)] * 2
         out_shape += [jax.ShapeDtypeStruct((tokens, width), F32), jax.ShapeDtypeStruct((tokens, width), BF)]
+        scratch += [pltpu.VMEM((2, TILE, hidden), BF), pltpu.VMEM((2, half, TILE), F32), two, two]
     else:
-        in_specs += [pl.BlockSpec(SUM_TILE, lambda s: (0, 0))]
+        in_specs += [pl.BlockSpec(SUM_TILE, origin)]
         args += [squares]
+        scratch += TILE_SCRATCH
     out_specs += [ANY, ANY]
     out_shape += [jax.ShapeDtypeStruct((4, rows_dev, hidden), F32), jax.ShapeDtypeStruct((4, width, hidden // DEVICES), F32)]
-    dma = pltpu.SemaphoreType.DMA
-    scratch = [pltpu.VMEM((width, tokens), BF), pltpu.VMEM((8 * rows_dev, tokens), BF), pltpu.VMEM((tokens, hidden), BF),
-               pltpu.VMEM((TURNS, 4 * rows_dev, NB), F32), pltpu.VMEM((2, 4 * rows_dev, NB), F32), pltpu.VMEM((2, 4 * rows_dev, NB), F32),
-               pltpu.VMEM((5 + bool(lead), width, NB // 2), F32), pltpu.VMEM((width, NB // 2), F32),
-               dma, dma((4,)), dma((4,)), dma((3,)), dma((3,)), dma((6,)), dma((2,)), pltpu.SemaphoreType.REGULAR]
     if not with_input_grad:
-        out_specs += [pl.BlockSpec(SUM_TILE, lambda s: (0, 0))]
+        out_specs += [pl.BlockSpec(SUM_TILE, origin)]
         out_shape += [jax.ShapeDtypeStruct(SUM_TILE, F32)]
-        scratch += TILE_SCRATCH
     return pl.pallas_call(
         functools.partial(backward_kernel, with_input_grad), grid=(TURNS + (TAIL if with_input_grad else LEAD),),
         in_specs=in_specs, out_specs=out_specs, out_shape=out_shape, scratch_shapes=scratch,

time: 1280 us -> 1250 us (0.977)
  Pallas kernels: 1260 us -> 1230 us
    pallas_call x8, Pallas kernels: 578 us -> 544 us  [backward_layer(): pl.pallas_call(functools.partial(backward_kernel, with_input_grad), grid=...]
where the time goes in v3:
time: 1250 us; the launch traced here: 1240 us
  Pallas kernels  1230 us (98%)
    pallas_call x8, Pallas kernels, backward_layer(): pl.pallas_call(functools.partial(backward_kernel, with_input_grad), grid=...  544 us
    pallas_call x8, Pallas kernels, forward_layer(): pl.pallas_call(functools.partial(forward_kernel, last, trading, n_up, n_d...  505 us
    pallas_call x2, Pallas kernels, gather_layer(): pl.pallas_call(functools.partial(gather_kernel, with_tokens), out_shape=o...  139 us

profile of v3, /device:TPU:0, one launch (start us, length us, event | category | flops | bytes accessed | tf_op | source)
XLA Modules:
  0.0 1237.8 jit_solution(9580129849974451647)
XLA Ops:
  0.6 0.0 copy-start
  0.6 2.6 convert.12
  3.3 1.4 slice_bitcast_fusion.1
  4.7 0.0 copy-done
  4.7 0.3 convert.13
  5.0 1.4 slice_bitcast_fusion
  6.4 93.6 %gather_with_tokens.1 = (bf16[16,64,4096]{2,1,0:T(8,128)(2,1)}, bf16[16,256,1024]{2,1,0:T(8,128)(2,1)}, bf16[2,1024,1024]{2,1,0:T(8,128)(2,1)}) custom-call(bf16[64,4096]{1,0:T(8,128)(2,1)} %get-tuple-element.192.refs_0_, bf16[256,1024]{1,0:T(8,128)(2,1)} %get-tuple-element.188.refs_1_, bf16[1024,1024]{1,0:T(8,128)(2,1)} %bitcast.35), custom_call_target="tpu_custom_call" | custom-call | tf_op jit(solution)/shard_map/gather_with_tokens/pallas_call | solution.py:237
  100.0 62.4 %forward_gather.6 = (bf16[16,256,1024]{2,1,0:T(8,128)(2,1)}, bf16[2048,4096]{1,0:T(8,128)(2,1)}, f32[2048,4096]{1,0:T(8,128)}, bf16[2048,1024]{1,0:T(8,128)(2,1)...) custom-call(bf16[2048,1024]{1,0:T(8,128)(2,1)} %bitcast.40, ...), custom_call_target="tpu_custom_call", output_to_operand_aliasing={{0}: (2, {})} | custom-call | flops 34359738368 | bytes 73400320 | tf_op jit(solution)/shard_map/forward_gather/pallas_call | solution.py:458
  162.4 61.5 %forward_gather.7 = (bf16[16,256,1024]{2,1,0:T(8,128)(2,1)}, bf16[2048,4096]{1,0:T(8,128)(2,1)}, f32[2048,4096]{1,0:T(8,128)}, bf16[2048,1024]{1,0:T(8,128)(2,1)...) custom-call(bf16[2048,1024]{1,0:T(8,128)(2,1)} %get-tuple-element.97.refs_0_.h_hb, ...), custom_call_target="tpu_custom_call", output_to_operand_aliasing={{0}: (2, {})} | custom-call | flops 34359738368 | bytes 73400320 | tf_op jit(solution)/shard_map/forward_gather/pallas_call | solution.py:458
  223.9 61.5 %forward_gather.8 = (bf16[16,256,1024]{2,1,0:T(8,128)(2,1)}, bf16[2048,4096]{1,0:T(8,128)(2,1)}, f32[2048,4096]{1,0:T(8,128)}, bf16[2048,1024]{1,0:T(8,128)(2,1)...) custom-call(bf16[2048,1024]{1,0:T(8,128)(2,1)} %get-tuple-element.100.refs_0_.h_h, ...), custom_call_target="tpu_custom_call", output_to_operand_aliasing={{0}: (2, {})} | custom-call | flops 34359738368 | bytes 73400320 | tf_op jit(solution)/shard_map/forward_gather/pallas_call | solution.py:458
  285.4 74.9 %forward_trade.1 = (bf16[16,256,1024]{2,1,0:T(8,128)(2,1)}, bf16[2048,4096]{1,0:T(8,128)(2,1)}, f32[2048,4096]{1,0:T(8,128)}, f32[2048,1024]{1,0:T(8,128)}, bf16...) custom-call(bf16[2048,1024]{1,0:T(8,128)(2,1)} %get-tuple-element.103, ...), custom_call_target="tpu_custom_call", output_to_operand_aliasing={{0}: (2, {})} | custom-call | flops 34359738368 | bytes 73400320 | tf_op jit(solution)/shard_map/forward_trade/pallas_call | solution.py:458
  360.3 70.5 %backward.6 = (f32[2048,1024]{1,0:T(8,128)}, bf16[2048,1024]{1,0:T(8,128)(2,1)}, f32[4,64,4096]{2,1,0:T(8,128)}, f32[4,1024,256]{2,1,0:T(8,128)}) custom-call(bf16[2048,1024]{1,0:T(8,128)(2,1)} %get-tuple-element.106.rb_ref, bf16[4096,1024]{1,0:T(8,128)(2,1)} %bitcast.62, bf16[2048,4096]{1,0:T(8,128)(2,1)} %get-tuple-element.108.a_hbm, ...), custom_call_target="tpu_custom_call" | custom-call | flops 51539607552 | bytes 104857600 | tf_op jit(solution)/shard_map/backward/pallas_call | solution.py:780
  430.8 70.2 %backward.7 = (f32[2048,1024]{1,0:T(8,128)}, bf16[2048,1024]{1,0:T(8,128)(2,1)}, f32[4,64,4096]{2,1,0:T(8,128)}, f32[4,1024,256]{2,1,0:T(8,128)}) custom-call(bf16[2048,1024]{1,0:T(8,128)(2,1)} %get-tuple-element.111.rb_ref, bf16[4096,1024]{1,0:T(8,128)(2,1)} %bitcast.60, bf16[2048,4096]{1,0:T(8,128)(2,1)} %get-tuple-element.113.a_hbm, ...), custom_call_target="tpu_custom_call" | custom-call | flops 51539607552 | bytes 104857600 | tf_op jit(solution)/shard_map/backward/pallas_call | solution.py:780
  501.0 70.2 %backward.8 = (f32[2048,1024]{1,0:T(8,128)}, bf16[2048,1024]{1,0:T(8,128)(2,1)}, f32[4,64,4096]{2,1,0:T(8,128)}, f32[4,1024,256]{2,1,0:T(8,128)}) custom-call(bf16[2048,1024]{1,0:T(8,128)(2,1)} %get-tuple-element.116.rb_ref, bf16[4096,1024]{1,0:T(8,128)(2,1)} %bitcast.58, bf16[2048,4096]{1,0:T(8,128)(2,1)} %get-tuple-element.118.a_hbm, ...), custom_call_target="tpu_custom_call" | custom-call | flops 51539607552 | bytes 104857600 | tf_op jit(solution)/shard_map/backward/pallas_call | solution.py:780
  571.2 61.1 %backward_first.2 = (f32[4,64,4096]{2,1,0:T(8,128)}, f32[4,1024,256]{2,1,0:T(8,128)}, f32[8,128]{1,0:T(8,128)}) custom-call(bf16[2048,1024]{1,0:T(8,128)(2,1)} %get-tuple-element.121.rb_ref, bf16[4096,1024]{1,0:T(8,128)(2,1)} %bitcast.37, bf16[2048,4096]{1,0:T(8,128)(2,1)} %get-tuple-element.123.a_hbm, f32[2048,4096]{1,0:T(8,128)} %get-tuple-element.124.d_hbm, ...), custom_call_target="tpu_custom_call" | custom-call | flops 51539607552 | bytes 104857600 | tf_op jit(solution)/shard_map/backward_first/pallas_call | solution.py:780
  632.3 21.5 %perturb.1 = (bf16[64,4096]{1,0:T(8,128)(2,1)}, bf16[64,4096]{1,0:T(8,128)(2,1)}, bf16[64,4096]{1,0:T(8,128)(2,1)}, bf16[64,4096]{1,0:T(8,128)(2,1)}, bf16[256,1...) custom-call(f32[4,64,4096]{2,1,0:T(8,128)} %get-tuple-element.126.refs_0_, ...), custom_call_target="tpu_custom_call" | custom-call | tf_op jit(solution)/shard_map/perturb/pallas_call | solution.py:901
  653.9 45.2 %gather_first.1 = (bf16[16,64,4096]{2,1,0:T(8,128)(2,1)}, bf16[16,256,1024]{2,1,0:T(8,128)(2,1)}) custom-call(bf16[64,4096]{1,0:T(8,128)(2,1)} %get-tuple-element.134.refs_0_, bf16[256,1024]{1,0:T(8,128)(2,1)} %get-tuple-element.135.refs_1_), custom_call_target="tpu_custom_call" | custom-call | tf_op jit(solution)/shard_map/gather_first/pallas_call | solution.py:237
  699.1 62.4 %forward_gather.9 = (bf16[16,256,1024]{2,1,0:T(8,128)(2,1)}, bf16[2048,4096]{1,0:T(8,128)(2,1)}, f32[2048,4096]{1,0:T(8,128)}, bf16[2048,1024]{1,0:T(8,128)(2,1)...) custom-call(bf16[2048,1024]{1,0:T(8,128)(2,1)} %bitcast.42, ...), custom_call_target="tpu_custom_call", output_to_operand_aliasing={{0}: (2, {})} | custom-call | flops 34359738368 | bytes 73400320 | tf_op jit(solution)/shard_map/forward_gather/pallas_call | solution.py:458
  761.5 61.4 %forward_gather.10 = (bf16[16,256,1024]{2,1,0:T(8,128)(2,1)}, bf16[2048,4096]{1,0:T(8,128)(2,1)}, f32[2048,4096]{1,0:T(8,128)}, bf16[2048,1024]{1,0:T(8,128)(2,1...) custom-call(bf16[2048,1024]{1,0:T(8,128)(2,1)} %get-tuple-element.140.refs_0_.h_, ...), custom_call_target="tpu_custom_call", output_to_operand_aliasing={{0}: (2, {})} | custom-call | flops 34359738368 | bytes 73400320 | tf_op jit(solution)/shard_map/forward_gather/pallas_call | solution.py:458
  822.9 61.4 %forward_gather.11 = (bf16[16,256,1024]{2,1,0:T(8,128)(2,1)}, bf16[2048,4096]{1,0:T(8,128)(2,1)}, f32[2048,4096]{1,0:T(8,128)}, bf16[2048,1024]{1,0:T(8,128)(2,1...) custom-call(bf16[2048,1024]{1,0:T(8,128)(2,1)} %get-tuple-element.145.refs_0_.h_, ...), custom_call_target="tpu_custom_call", output_to_operand_aliasing={{0}: (2, {})} | custom-call | flops 34359738368 | bytes 73400320 | tf_op jit(solution)/shard_map/forward_gather/pallas_call | solution.py:458
  884.3 59.9 %forward_last.1 = (bf16[16,256,1024]{2,1,0:T(8,128)(2,1)}, bf16[2048,4096]{1,0:T(8,128)(2,1)}, f32[2048,4096]{1,0:T(8,128)}, f32[2048,1024]{1,0:T(8,128)}, bf16[2048,1024]{1,0:T(8,128)(2,1)}, /*index=5*/f32[8,128]{1,0:T(8,128)}) custom-call(bf16[2048,1024]{1,0:T(8,128)(2,1)} %get-tuple-element.150.refs_0_.h_hbm, ...), custom_call_target="tpu_custom_call", output_to_operand_aliasing={{0}: (2, {})} | custom-call | flops 34359738368 | bytes 73400320 | tf_op jit(solution)/shard_map/forward_last/pallas_call | solution.py:458
  944.2 70.5 %backward.9 = (f32[2048,1024]{1,0:T(8,128)}, bf16[2048,1024]{1,0:T(8,128)(2,1)}, f32[4,64,4096]{2,1,0:T(8,128)}, f32[4,1024,256]{2,1,0:T(8,128)}) custom-call(bf16[2048,1024]{1,0:T(8,128)(2,1)} %get-tuple-element.154.rb_ref, bf16[4096,1024]{1,0:T(8,128)(2,1)} %bitcast.63, bf16[2048,4096]{1,0:T(8,128)(2,1)} %get-tuple-element.156.a_hbm, ...), custom_call_target="tpu_custom_call" | custom-call | flops 51539607552 | bytes 104857600 | tf_op jit(solution)/shard_map/backward/pallas_call | solution.py:780
  1014.7 70.2 %backward.10 = (f32[2048,1024]{1,0:T(8,128)}, bf16[2048,1024]{1,0:T(8,128)(2,1)}, f32[4,64,4096]{2,1,0:T(8,128)}, f32[4,1024,256]{2,1,0:T(8,128)}) custom-call(bf16[2048,1024]{1,0:T(8,128)(2,1)} %get-tuple-element.159.rb_ref, bf16[4096,1024]{1,0:T(8,128)(2,1)} %bitcast.61, bf16[2048,4096]{1,0:T(8,128)(2,1)} %get-tuple-element.161.a_hbm, ...), custom_call_target="tpu_custom_call" | custom-call | flops 51539607552 | bytes 104857600 | tf_op jit(solution)/shard_map/backward/pallas_call | solution.py:780
  1084.9 70.3 %backward.11 = (f32[2048,1024]{1,0:T(8,128)}, bf16[2048,1024]{1,0:T(8,128)(2,1)}, f32[4,64,4096]{2,1,0:T(8,128)}, f32[4,1024,256]{2,1,0:T(8,128)}) custom-call(bf16[2048,1024]{1,0:T(8,128)(2,1)} %get-tuple-element.164.rb_ref, bf16[4096,1024]{1,0:T(8,128)(2,1)} %bitcast.59, bf16[2048,4096]{1,0:T(8,128)(2,1)} %get-tuple-element.166.a_hbm, ...), custom_call_target="tpu_custom_call" | custom-call | flops 51539607552 | bytes 104857600 | tf_op jit(solution)/shard_map/backward/pallas_call | solution.py:780
  1155.2 61.3 %backward_first.3 = (f32[4,64,4096]{2,1,0:T(8,128)}, f32[4,1024,256]{2,1,0:T(8,128)}, f32[8,128]{1,0:T(8,128)}) custom-call(bf16[2048,1024]{1,0:T(8,128)(2,1)} %get-tuple-element.169.rb_ref, bf16[4096,1024]{1,0:T(8,128)(2,1)} %bitcast.39, bf16[2048,4096]{1,0:T(8,128)(2,1)} %get-tuple-element.171.a_hbm, f32[2048,4096]{1,0:T(8,128)} %get-tuple-element.172.d_hbm, ...), custom_call_target="tpu_custom_call" | custom-call | flops 51539607552 | bytes 104857600 | tf_op jit(solution)/shard_map/backward_first/pallas_call | solution.py:780
  1216.5 1.3 reduce_sum.9
  1218.5 17.8 %update.1 = (f32[4,64,4096]{2,1,0:T(8,128)}, f32[4,256,1024]{2,1,0:T(8,128)}) custom-call(f32[4,64,4096]{2,1,0:T(8,128)} %get-tuple-element.174.refs_0_, f32[4,64,4096]{2,1,0:T(8,128)} %get-tuple-element.175.refs_1_, f32[4,64,4096]{2,1,0:T(8,128)} %get-tuple-element.176.refs_2_, f32[4,64,4096]{2,1,0:T(8,128)} %get-tuple-element.177.refs_3_, ...), custom_call_target="tpu_custom_call" | custom-call | tf_op jit(solution)/shard_map/update/pallas_call | solution.py:913
Async XLA Ops:
  0.6 4.0 copy-start

commit v4 on v3

--- a/solution.py
+++ b/solution.py
@@ -34,6 +34,18 @@
     return pl.ds(index * size, size)
 
 
+def aligned(index, size):
+    return pl.ds(pl.multiple_of(index * size, size), size)
+
+
+def halve(index):
+    return lax.shift_right_logical(index, 1)
+
+
+def parity(index):
+    return index & 1
+
+
 def flip(dev, bit):
     return dev ^ bit
 
@@ -124,8 +136,11 @@
     def own_load(self):
         pltpu.make_async_copy(self.shard, self.own_vmem, self.own_sem).start()
 
-    def own_store(self):
-        pltpu.make_async_copy(self.shard, self.own_vmem, self.own_sem).wait()
+    def own_store(self, in_vmem=False):
+        if in_vmem:
+            self.own_vmem = self.shard
+        else:
+            pltpu.make_async_copy(self.shard, self.own_vmem, self.own_sem).wait()
         pltpu.make_async_copy(self.own_vmem, self.full.at[self.me], self.own_sem).start()
 
     def blocks(self, count, sem):
@@ -178,13 +193,27 @@
 
 
 def gather_kernel(with_tokens, *refs):
+    me = lax.axis_index('data')
     if with_tokens:
-        shard_in, shard_out, x_hbm, full_in, full_out, pair, *scratch = refs
-        *scratch, x_vmem, x_sems = scratch
+        masters, (x_hbm, full_in, full_out, pair), refs = refs[:2], refs[2:6], refs[6:]
+        layers = masters[0].shape[0]
+        casts, refs = (refs[:layers], refs[layers:2 * layers]), refs[2 * layers:]
+        scratch, (x_vmem, x_sems), wide, narrow, (load_sems, cast_sems) = refs[:8], refs[8:10], refs[10:12], refs[12:14], refs[14:]
+        loads = [[pltpu.make_async_copy(masters[k].at[l], wide[k].at[l], load_sems.at[k, l]) for l in range(layers)] for k in range(2)]
+        stores = [pltpu.make_async_copy(narrow[k].at[l], casts[k][l], cast_sems.at[k, l]) for l in range(layers) for k in range(2)]
+        for l in range(layers):
+            for k in range(2):
+                loads[k][l].start()
+
+        def cast(l):
+            for k in range(2):
+                loads[k][l].wait()
+                narrow[k][l] = wide[k][l].astype(BF)
+        cast(0)
+        shard_in, shard_out = narrow[0].at[0], narrow[1].at[0]
     else:
         shard_in, shard_out, full_in, full_out, *scratch = refs
     g_in, g_out = gather_in(shard_in, full_in, scratch[:4]), gather_out(shard_out, full_out, scratch[4:])
-    me = lax.axis_index('data')
     greet_neighbours(*((ANTIPODE,) if with_tokens else ()))
     g_in.start(0)
     g_out.start(0)
@@ -195,15 +224,21 @@
         store = pltpu.make_async_copy(x_vmem, pair.at[0], x_sems.at[2])
         trade.start()
         load.start()
-    for g in (g_in, g_out):
-        g.own_load()
-    for g in (g_in, g_out):
+    both = (g_in, g_out)
+    if not with_tokens:
+        for g in both:
+            g.own_load()
+    for g in both:
         g.share(-1)
-    for g in (g_in, g_out):
-        g.own_store()
+    for g in both:
+        g.own_store(with_tokens)
     if with_tokens:
         load.wait()
         store.start()
+        for l in range(1, layers):
+            cast(l)
+        for copy in stores:
+            copy.start()
     g_in.wait(0)
     g_in.start(1)
     g_in.share(0)
@@ -223,17 +258,24 @@
     if with_tokens:
         trade.wait()
         store.wait()
+        for copy in stores:
+            copy.wait()
 
 
 def gather_layer(shard_in, shard_out, x=None):
     with_tokens = x is not None
-    out_shape = [full_shape(shard_in), full_shape(shard_out)]
-    scratch = gather_scratch(shard_in) + gather_scratch(shard_out)
     args = [shard_in, shard_out]
+    dma = pltpu.SemaphoreType.DMA
     if with_tokens:
+        layers = shard_in.shape[0]
+        rows = [jax.ShapeDtypeStruct(sh.shape[1:], BF) for sh in args]
+        out_shape = [full_shape(sh) for sh in rows] + [jax.ShapeDtypeStruct((2,) + x.shape, BF)] + rows[:1] * layers + rows[1:] * layers
+        scratch = sum((gather_scratch(sh) for sh in rows), []) + [pltpu.VMEM(x.shape, BF), dma((3,))]
+        scratch += [pltpu.VMEM(sh.shape, kind) for kind in (F32, BF) for sh in args] + [dma((2, layers))] * 2
         args += [x]
-        out_shape += [jax.ShapeDtypeStruct((2,) + x.shape, BF)]
-        scratch += [pltpu.VMEM(x.shape, BF), pltpu.SemaphoreType.DMA((3,))]
+    else:
+        out_shape = [full_shape(sh) for sh in args]
+        scratch = sum((gather_scratch(sh) for sh in args), [])
     return pl.pallas_call(
         functools.partial(gather_kernel, with_tokens), out_shape=out_shape,
         in_specs=[ANY] * len(args), out_specs=[ANY] * len(out_shape), scratch_shapes=scratch,
@@ -254,15 +296,15 @@
 
 def forward_kernel(last, trading, n_up, n_down, *refs):
     if not last:
-        (h_ref, wi_ref, _, next_in, next_out, wo_full, a_hbm, d_ref, hn_ref, full_in, full_out,
-         a_vmem, wo_vmem, a_sem, wo_sem, recv, send, *scratch) = refs
+        (h_hbm, wi_ref, _, next_in, next_out, wo_full, a_hbm, d_ref, hn_ref, full_in, full_out,
+         h_ref, a_vmem, wo_vmem, h_sem, a_sem, wo_sem, recv, send, *scratch) = refs
         nxt_in, nxt_out = gather_in(next_in, full_in, scratch[:4]), gather_out(next_out, full_out, scratch[4:])
     else:
         if trading:
-            h_ref, wi_ref, _, y_hbm, wo_full, a_hbm, d_ref, r_ref, rb_ref, loss_ref, y_other, *scratch = refs
+            h_hbm, wi_ref, _, y_hbm, wo_full, a_hbm, d_ref, r_ref, rb_ref, loss_ref, y_other, *scratch = refs
         else:
-            h_ref, wi_ref, _, y_hbm, y_other, wo_full, a_hbm, d_ref, r_ref, rb_ref, loss_ref, *scratch = refs
-        a_vmem, wo_vmem, a_sem, wo_sem, recv, send, y_vmem, late, y_sems = scratch
+            h_hbm, wi_ref, _, y_hbm, y_other, wo_full, a_hbm, d_ref, r_ref, rb_ref, loss_ref, *scratch = refs
+        h_ref, a_vmem, wo_vmem, h_sem, a_sem, wo_sem, recv, send, y_vmem, late, y_sems = scratch
     w_out = Gather(wo_full, pieces_out(wo_full), (recv, send))
     step = pl.program_id(0)
     me = lax.axis_index('data')
@@ -285,6 +327,8 @@
         return pltpu.make_async_copy(y_hbm if own else y_other, y_vmem.at[which], y_sems.at[2 + which])
 
     def begin():
+        h_load = pltpu.make_async_copy(h_hbm, h_ref, h_sem)
+        h_load.start()
         greet_neighbours(*((ANTIPODE,) if trading else ()))
         if not last:
             nxt_in.start(0)
@@ -300,6 +344,7 @@
             load_y(0).start()
             if not trading:
                 load_y(1).start()
+        h_load.wait()
 
     def pass_on():
         w_out.wait(2)
@@ -358,7 +403,7 @@
         pltpu.make_async_copy(a_vmem.at[:, pl.ds(base, HB)], a_hbm.at[:, pl.ds(base, HB)], a_sem).start()
 
     def residual(h_next, which, block):
-        rows = pl.ds(pl.multiple_of(block * MT, MT), MT)
+        rows = aligned(block, MT)
         error = h_next.astype(F32) - y_vmem[which, rows, :].astype(F32)
         r = error / (own_blocks * MT)
         r_ref[...] = r
@@ -382,7 +427,7 @@
             hn_ref[...] = h_next
         else:
             if trading:
-                late[pl.ds(pl.multiple_of((block % own_blocks) * MT, MT), MT), :] = h_next
+                late[aligned((block % own_blocks), MT), :] = h_next
 
             @pl.when(step < n_up + own_blocks)
             def _():
@@ -406,7 +451,7 @@
         @pl.when(step >= n_up + n_down)
         def _():
             block = jnp.clip(step - n_up - n_down, 0, own_blocks - 1)
-            residual(late[pl.ds(pl.multiple_of(block * MT, MT), MT), :], 1, block)
+            residual(late[aligned(block, MT), :], 1, block)
 
     def end():
         pltpu.make_async_copy(a_vmem, a_hbm, a_sem).wait()
@@ -432,12 +477,11 @@
     if trading:
         down = lambda s: jnp.where(s < n_up + n_down, jnp.clip(s - n_up, 0, half - 1), s - n_up - half)
     row_block = pl.BlockSpec((MT, width), lambda s: (down(s), 0))
-    in_specs = [pl.BlockSpec((tokens, width), origin, pipeline_mode=pl.Buffered(1)),
-                pl.BlockSpec((width, HB), lambda s: (0, up(s))), ANY]
+    in_specs = [ANY, pl.BlockSpec((width, HB), lambda s: (0, up(s))), ANY]
     out_specs = [ANY, ANY, pl.BlockSpec((tokens, HB), lambda s: (0, up(s)))]
     out_shape = [jax.ShapeDtypeStruct(w_out_part.shape, BF), jax.ShapeDtypeStruct((tokens, hidden), BF), jax.ShapeDtypeStruct((tokens, hidden), F32)]
-    scratch = [pltpu.VMEM((tokens, hidden), BF), pltpu.VMEM((hidden, width), BF),
-               pltpu.SemaphoreType.DMA, pltpu.SemaphoreType.DMA] + GATHER_SEMS
+    scratch = [pltpu.VMEM((tokens, width), BF), pltpu.VMEM((tokens, hidden), BF), pltpu.VMEM((hidden, width), BF),
+               pltpu.SemaphoreType.DMA, pltpu.SemaphoreType.DMA, pltpu.SemaphoreType.DMA] + GATHER_SEMS
     args = [h, w_in_full, w_out_part]
     if not last:
         args += list(next_shards)
@@ -473,7 +517,7 @@
 
 
 def chip_at(turn):
-    chip = lax.shift_right_logical(lax.axis_index('data'), 1)
+    chip = halve(lax.axis_index('data'))
     near = chip ^ (lax.shift_left(1, turn & 3) & 7)
     return jnp.where(turn < 4, near, 7 - near)
 
@@ -496,7 +540,7 @@
     step = pl.program_id(0)
     lead = 0 if with_input_grad else LEAD
     me = lax.axis_index('data')
-    chip, core = lax.shift_right_logical(me, 1), me & 1
+    chip, core = halve(me), parity(me)
     tokens, width = rb_ref.shape
     half = tokens // 2
     rows_dev = ht.shape[0] // 8
@@ -509,26 +553,26 @@
         pl.when(step == s)(fn)
 
     def hidden_cols(turn):
-        return pl.ds(pl.multiple_of(chip_at(turn) * NB, NB), NB)
+        return aligned(chip_at(turn), NB)
 
     def wo_copy(turn):
-        return pltpu.make_async_copy(wo_hbm.at[hidden_cols(turn)], wo_buf.at[turn & 1], wo_sem.at[turn & 1])
+        return pltpu.make_async_copy(wo_hbm.at[hidden_cols(turn)], wo_buf.at[parity(turn)], wo_sem.at[parity(turn)])
 
     def d_copy(turn):
-        return pltpu.make_async_copy(d_hbm.at[:, hidden_cols(turn)], d_buf.at[turn & 1], d_sem.at[turn & 1])
+        return pltpu.make_async_copy(d_hbm.at[:, hidden_cols(turn)], d_buf.at[parity(turn)], d_sem.at[parity(turn)])
 
     def a_copy(owner):
         slot = owner & (a_slots - 1)
         return pltpu.make_async_copy(a_hbm.at[:, hidden_cols(owner)], a_buf.at[slot], a_sem.at[slot])
 
     def wi_copy(block):
-        rows = pl.ds(pl.multiple_of(block * TILE, TILE), TILE)
-        return pltpu.make_async_copy(wi_hbm.at[rows], wi_buf.at[block & 1], wi_sem.at[block & 1])
+        rows = aligned(block, TILE)
+        return pltpu.make_async_copy(wi_hbm.at[rows], wi_buf.at[parity(block)], wi_sem.at[parity(block)])
 
     def r_copy(index):
-        rows = pl.ds(pl.multiple_of((index & 1) * half, half), half)
-        cols = pl.ds(pl.multiple_of(lax.shift_right_logical(index, 1) * TILE, TILE), TILE)
-        return pltpu.make_async_copy(r_hbm.at[rows, cols], r_buf.at[index & 1], r_sem.at[index & 1])
+        rows = aligned(parity(index), half)
+        cols = aligned(halve(index), TILE)
+        return pltpu.make_async_copy(r_hbm.at[rows, cols], r_buf.at[parity(index)], r_sem.at[parity(index)])
 
     h_base = pl.multiple_of(chip * NB, NB)
 
@@ -576,7 +620,7 @@
         return pltpu.make_async_remote_copy(src_ref=src, dst_ref=dst, send_sem=send, recv_sem=recv, device_id=partner, device_id_type=MESH)
 
     def gi_core(turn):
-        slot = turn & 1
+        slot = parity(turn)
         return core_copy(gi_send.at[slot], gi_recv.at[slot], gi_dsend.at[slot], gi_drecv.at[slot])
 
     def outbox(piece):
@@ -601,7 +645,7 @@
         ship(go_x.at[owner, rows], lambda slot: go_out.at[slot, rows], owner, go_sent.at[owner % 3], xrecv.at[3 + owner % 3], own_sem.at[1])
 
     def out_grad(owner, part, piece):
-        rows = pl.ds(pl.multiple_of(part * MT, MT), MT)
+        rows = aligned(part, MT)
         total = rounded_sum(rbt[rows, :], a_buf[owner & (a_slots - 1)], half)
 
         @pl.when(core == 0)
@@ -616,7 +660,7 @@
 
     def gi_merge(turn):
         gi_core(turn).wait_recv()
-        gi_x[turn] = gi_x[turn] + gi_recv[turn & 1]
+        gi_x[turn] = gi_x[turn] + gi_recv[parity(turn)]
         cols = hidden_cols(turn)
         for i in range(4):
             ship(gi_x.at[turn, pl.ds(i * rows_dev, rows_dev)], lambda slot: gi_out.at[slot, :, cols],
@@ -649,7 +693,7 @@
         d_copy(turn).wait()
 
     def slopes(turning):
-        slot = turn & 1
+        slot = parity(turn)
         for m in range(tokens // MT):
             rows = span(m, MT)
             u = lax.dot_general(rb_ref[rows, :], wo_buf[slot], NT, preferred_element_type=F32)
@@ -675,8 +719,8 @@
         @pl.when(step >= TURNS)
         def _():
             index = jnp.maximum(step - TURNS, 0)
-            block = lax.shift_right_logical(index, 1)
-            side = index & 1
+            block = halve(index)
+            side = parity(index)
 
             @pl.when((index > 0) & (index < TAIL - 1))
             def _():
@@ -690,7 +734,7 @@
             for m in range(half // MT):
                 rows = span(m, MT)
                 left = e_ref[pl.ds(pl.multiple_of(side * half + m * MT, MT), MT), :]
-                u = lax.dot_general(left, wi_buf[block & 1], NT, preferred_element_type=F32) + r_buf[side, rows, :]
+                u = lax.dot_general(left, wi_buf[parity(block)], NT, preferred_element_type=F32) + r_buf[side, rows, :]
                 rn_ref[rows, :] = u
                 rbn_ref[rows, :] = u.astype(BF)
 
@@ -700,7 +744,7 @@
     def _():
         total = rounded_sum(ht[...], e_ref[:, pl.ds(base, NB)], half)
         gi_x[turn] = total[:mine]
-        gi_send[turn & 1] = total[mine:]
+        gi_send[parity(turn)] = total[mine:]
 
     last_merge = TURNS if with_input_grad else lead + TURNS - 1
     pl.when((step >= lead + 1) & (step <= last_merge))(lambda: gi_merge(jnp.clip(step - lead - 1, 0, TURNS - 1)))
@@ -762,7 +806,7 @@
                pltpu.VMEM((4, width, NB // 2), F32), pltpu.VMEM((2 if with_input_grad else 4,) + piece, F32), pltpu.VMEM((4,) + piece, F32),
                dma, two, four, two, two, two, four, four, three, three, dma((6,)), two]
     if with_input_grad:
-        block = lambda s: (tail(s) & 1, lax.shift_right_logical(tail(s), 1))
+        block = lambda s: (tail(s) & 1, halve(tail(s)))
         in_specs += [ANY, ANY]
         args += [w_in_full, r]
         out_specs += [pl.BlockSpec((half, TILE), block)] * 2
@@ -809,13 +853,13 @@
         share = 1.0 / DEVICES
 
         def in_rows(i, c):
-            rows = pl.ds(pl.multiple_of(i * 8, 8), 8)
+            rows = aligned(i, 8)
             total = self.vgi[l, 0, rows, :] + self.vgi[l, 1, rows, :] + self.vgi[l, 2, rows, :] + self.vgi[l, 3, rows, :]
             return use_in(rows, total * share, c)
         carry = lax.fori_loop(0, self.vgi.shape[2] // 8, in_rows, carry)
 
         def out_cols(i, c):
-            rows = pl.ds(pl.multiple_of(i * LANES, LANES), LANES)
+            rows = aligned(i, LANES)
             total = self.vgo[l, 0, rows, :] + self.vgo[l, 1, rows, :] + self.vgo[l, 2, rows, :] + self.vgo[l, 3, rows, :]
             return use_out(rows, (total * share).T, c)
         return lax.fori_loop(0, self.vgo.shape[2] // LANES, out_cols, carry)
@@ -853,13 +897,13 @@
     scale = (radius / norm)[0:1, 0:1]
     for l in range(layers):
         def in_rows(i, carry, l=l):
-            rows = pl.ds(pl.multiple_of(i * 16, 16), 16)
+            rows = aligned(i, 16)
             p_in[l][rows, :] = (vw_in[l, rows, :] + scale * g_in[l, rows, :]).astype(BF)
             return carry
         lax.fori_loop(0, p_in[l].shape[0] // 16, in_rows, 0)
 
         def out_rows(i, carry, l=l):
-            rows = pl.ds(pl.multiple_of(i * 64, 64), 64)
+            rows = aligned(i, 64)
             p_out[l][rows, :] = (vw_out[l, rows, :] + scale * g_out[l, rows, :]).astype(BF)
             return carry
         lax.fori_loop(0, p_out[l].shape[0] // 64, out_rows, 0)
@@ -920,9 +964,10 @@
 
 
 def sam_pass(tokens, targets, shards_in, shards_out):
-    layers = len(shards_in)
+    layers = len(shards_in) if isinstance(shards_in, (list, tuple)) else shards_in.shape[0]
     if tokens.ndim == 2:
-        full_in, full_out, tokens = gather_layer(shards_in[0], shards_out[0], tokens)
+        full_in, full_out, tokens, *casts = gather_layer(shards_in, shards_out, tokens)
+        shards_in, shards_out = casts[:layers], casts[layers:]
     else:
         full_in, full_out = gather_layer(shards_in[0], shards_out[0])
     h_cur = tokens.reshape(-1, tokens.shape[-1])
@@ -953,6 +998,7 @@
 
 def solution(mesh):
     groups = mesh.shape['data']
+    batch, rows = P('data', None, None), P(None, 'data', None)
 
     def device_step(x_blk, y_blk, w_in_sh, w_out_sh):
         layers = w_in_sh.shape[0]
@@ -960,8 +1006,7 @@
         radius = RHO_FRAC * math.sqrt(layers * model_dim)
         x_tok = x_blk.reshape(-1, model_dim)
         y_tok = y_blk.reshape(-1, model_dim)
-        span = range(layers)
-        _, g_in, g_out, x_pair, y_pair = sam_pass(x_tok, (y_tok,), [w_in_sh[l].astype(BF) for l in span], [w_out_sh[l].astype(BF) for l in span])
+        _, g_in, g_out, x_pair, y_pair = sam_pass(x_tok, (y_tok,), w_in_sh, w_out_sh)
         pert_in, pert_out = perturb(g_in, g_out, w_in_sh, w_out_sh, radius)
         squares, gp_in, gp_out, _, _ = sam_pass(x_pair, y_pair, pert_in, pert_out)
         mean_loss = jnp.sum(squares) * (0.5 / (x_tok.shape[0] * groups))
@@ -969,6 +1014,5 @@
         return new_in, new_out, mean_loss
 
     return jax.shard_map(device_step, mesh=mesh,
-                         in_specs=(P('data', None, None), P('data', None, None), P(None, 'data', None), P(None, 'data', None)),
-                         out_specs=(P(None, 'data', None), P(None, 'data', None), P()),
+                         in_specs=(batch, batch, rows, rows), out_specs=(rows, rows, P()),
                          check_vma=False)

time: 1250 us -> 1230 us (0.984)
  no operation moved by 1% of the time
where the time goes in v4:
time: 1230 us; the launch traced here: 1220 us
  Pallas kernels  1220 us (99%)
    pallas_call x8, Pallas kernels, backward_layer(): pl.pallas_call(functools.partial(backward_kernel, with_input_grad), grid=...  544 us
    pallas_call x8, Pallas kernels, forward_layer(): pl.pallas_call(functools.partial(forward_kernel, last, trading, n_up, n_d...  495 us
    pallas_call x2, Pallas kernels, gather_layer(): pl.pallas_call(functools.partial(gather_kernel, with_tokens), out_shape=o...  141 us

profile of v4, /device:TPU:0, one launch (start us, length us, event | category | flops | bytes accessed | tf_op | source)
XLA Modules:
  0.0 1223.5 jit_solution(16921787807740496772)
XLA Ops:
  0.6 95.3 %gather_with_tokens.1 = (bf16[16,64,4096]{2,1,0:T(8,128)(2,1)}, bf16[16,256,1024]{2,1,0:T(8,128)(2,1)}, bf16[2,1024,1024]{2,1,0:T(8,128)(2,1)}, bf16[64,4096]{1,...) custom-call(f32[4,64,4096]{2,1,0:T(8,128)} %refs_8_.3, ...), custom_call_target="tpu_custom_call" | custom-call | tf_op jit(solution)/shard_map/gather_with_tokens/pallas_call | solution.py:279
  96.0 61.1 %forward_gather.6 = (bf16[16,256,1024]{2,1,0:T(8,128)(2,1)}, bf16[2048,4096]{1,0:T(8,128)(2,1)}, f32[2048,4096]{1,0:T(8,128)}, bf16[2048,1024]{1,0:T(8,128)(2,1)...) custom-call(bf16[2048,1024]{1,0:T(8,128)(2,1)} %bitcast.24, ...), custom_call_target="tpu_custom_call", output_to_operand_aliasing={{0}: (2, {})} | custom-call | flops 34359738368 | bytes 73400320 | tf_op jit(solution)/shard_map/forward_gather/pallas_call | solution.py:502
  157.1 60.2 %forward_gather.7 = (bf16[16,256,1024]{2,1,0:T(8,128)(2,1)}, bf16[2048,4096]{1,0:T(8,128)(2,1)}, f32[2048,4096]{1,0:T(8,128)}, bf16[2048,1024]{1,0:T(8,128)(2,1)...) custom-call(bf16[2048,1024]{1,0:T(8,128)(2,1)} %get-tuple-element.105.refs_0_.h_h, ...), custom_call_target="tpu_custom_call", output_to_operand_aliasing={{0}: (2, {})} | custom-call | flops 34359738368 | bytes 73400320 | tf_op jit(solution)/shard_map/forward_gather/pallas_call | solution.py:502
  217.4 60.2 %forward_gather.8 = (bf16[16,256,1024]{2,1,0:T(8,128)(2,1)}, bf16[2048,4096]{1,0:T(8,128)(2,1)}, f32[2048,4096]{1,0:T(8,128)}, bf16[2048,1024]{1,0:T(8,128)(2,1)...) custom-call(bf16[2048,1024]{1,0:T(8,128)(2,1)} %get-tuple-element.110.refs_0_.h_h, ...), custom_call_target="tpu_custom_call", output_to_operand_aliasing={{0}: (2, {})} | custom-call | flops 34359738368 | bytes 73400320 | tf_op jit(solution)/shard_map/forward_gather/pallas_call | solution.py:502
  277.6 73.7 %forward_trade.1 = (bf16[16,256,1024]{2,1,0:T(8,128)(2,1)}, bf16[2048,4096]{1,0:T(8,128)(2,1)}, f32[2048,4096]{1,0:T(8,128)}, f32[2048,1024]{1,0:T(8,128)}, bf16...) custom-call(bf16[2048,1024]{1,0:T(8,128)(2,1)} %get-tuple-element.115, ...), custom_call_target="tpu_custom_call", output_to_operand_aliasing={{0}: (2, {})} | custom-call | flops 34359738368 | bytes 73400320 | tf_op jit(solution)/shard_map/forward_trade/pallas_call | solution.py:502
  351.3 70.5 %backward.6 = (f32[2048,1024]{1,0:T(8,128)}, bf16[2048,1024]{1,0:T(8,128)(2,1)}, f32[4,64,4096]{2,1,0:T(8,128)}, f32[4,1024,256]{2,1,0:T(8,128)}) custom-call(bf16[2048,1024]{1,0:T(8,128)(2,1)} %get-tuple-element.118.rb_ref, bf16[4096,1024]{1,0:T(8,128)(2,1)} %bitcast.46, bf16[2048,4096]{1,0:T(8,128)(2,1)} %get-tuple-element.120.a_hbm, ...), custom_call_target="tpu_custom_call" | custom-call | flops 51539607552 | bytes 104857600 | tf_op jit(solution)/shard_map/backward/pallas_call | solution.py:824
  421.8 70.2 %backward.7 = (f32[2048,1024]{1,0:T(8,128)}, bf16[2048,1024]{1,0:T(8,128)(2,1)}, f32[4,64,4096]{2,1,0:T(8,128)}, f32[4,1024,256]{2,1,0:T(8,128)}) custom-call(bf16[2048,1024]{1,0:T(8,128)(2,1)} %get-tuple-element.123.rb_ref, bf16[4096,1024]{1,0:T(8,128)(2,1)} %bitcast.44, bf16[2048,4096]{1,0:T(8,128)(2,1)} %get-tuple-element.125.a_hbm, ...), custom_call_target="tpu_custom_call" | custom-call | flops 51539607552 | bytes 104857600 | tf_op jit(solution)/shard_map/backward/pallas_call | solution.py:824
  491.9 70.2 %backward.8 = (f32[2048,1024]{1,0:T(8,128)}, bf16[2048,1024]{1,0:T(8,128)(2,1)}, f32[4,64,4096]{2,1,0:T(8,128)}, f32[4,1024,256]{2,1,0:T(8,128)}) custom-call(bf16[2048,1024]{1,0:T(8,128)(2,1)} %get-tuple-element.128.rb_ref, bf16[4096,1024]{1,0:T(8,128)(2,1)} %bitcast.42, bf16[2048,4096]{1,0:T(8,128)(2,1)} %get-tuple-element.130.a_hbm, ...), custom_call_target="tpu_custom_call" | custom-call | flops 51539607552 | bytes 104857600 | tf_op jit(solution)/shard_map/backward/pallas_call | solution.py:824
  562.2 61.1 %backward_first.2 = (f32[4,64,4096]{2,1,0:T(8,128)}, f32[4,1024,256]{2,1,0:T(8,128)}, f32[8,128]{1,0:T(8,128)}) custom-call(bf16[2048,1024]{1,0:T(8,128)(2,1)} %get-tuple-element.133.rb_ref, bf16[4096,1024]{1,0:T(8,128)(2,1)} %bitcast.21, bf16[2048,4096]{1,0:T(8,128)(2,1)} %get-tuple-element.135.a_hbm, f32[2048,4096]{1,0:T(8,128)} %get-tuple-element.136.d_hbm, ...), custom_call_target="tpu_custom_call" | custom-call | flops 51539607552 | bytes 104857600 | tf_op jit(solution)/shard_map/backward_first/pallas_call | solution.py:824
  623.3 21.5 %perturb.1 = (bf16[64,4096]{1,0:T(8,128)(2,1)}, bf16[64,4096]{1,0:T(8,128)(2,1)}, bf16[64,4096]{1,0:T(8,128)(2,1)}, bf16[64,4096]{1,0:T(8,128)(2,1)}, bf16[256,1...) custom-call(f32[4,64,4096]{2,1,0:T(8,128)} %get-tuple-element.138.refs_0_, ...), custom_call_target="tpu_custom_call" | custom-call | tf_op jit(solution)/shard_map/perturb/pallas_call | solution.py:945
  644.8 45.2 %gather_first.1 = (bf16[16,64,4096]{2,1,0:T(8,128)(2,1)}, bf16[16,256,1024]{2,1,0:T(8,128)(2,1)}) custom-call(bf16[64,4096]{1,0:T(8,128)(2,1)} %get-tuple-element.146.refs_0_, bf16[256,1024]{1,0:T(8,128)(2,1)} %get-tuple-element.147.refs_1_), custom_call_target="tpu_custom_call" | custom-call | tf_op jit(solution)/shard_map/gather_first/pallas_call | solution.py:279
  690.0 61.2 %forward_gather.9 = (bf16[16,256,1024]{2,1,0:T(8,128)(2,1)}, bf16[2048,4096]{1,0:T(8,128)(2,1)}, f32[2048,4096]{1,0:T(8,128)}, bf16[2048,1024]{1,0:T(8,128)(2,1)...) custom-call(bf16[2048,1024]{1,0:T(8,128)(2,1)} %bitcast.26, ...), custom_call_target="tpu_custom_call", output_to_operand_aliasing={{0}: (2, {})} | custom-call | flops 34359738368 | bytes 73400320 | tf_op jit(solution)/shard_map/forward_gather/pallas_call | solution.py:502
  751.2 60.1 %forward_gather.10 = (bf16[16,256,1024]{2,1,0:T(8,128)(2,1)}, bf16[2048,4096]{1,0:T(8,128)(2,1)}, f32[2048,4096]{1,0:T(8,128)}, bf16[2048,1024]{1,0:T(8,128)(2,1...) custom-call(bf16[2048,1024]{1,0:T(8,128)(2,1)} %get-tuple-element.152.refs_0_.h_, ...), custom_call_target="tpu_custom_call", output_to_operand_aliasing={{0}: (2, {})} | custom-call | flops 34359738368 | bytes 73400320 | tf_op jit(solution)/shard_map/forward_gather/pallas_call | solution.py:502
  811.3 60.1 %forward_gather.11 = (bf16[16,256,1024]{2,1,0:T(8,128)(2,1)}, bf16[2048,4096]{1,0:T(8,128)(2,1)}, f32[2048,4096]{1,0:T(8,128)}, bf16[2048,1024]{1,0:T(8,128)(2,1...) custom-call(bf16[2048,1024]{1,0:T(8,128)(2,1)} %get-tuple-element.157.refs_0_.h_, ...), custom_call_target="tpu_custom_call", output_to_operand_aliasing={{0}: (2, {})} | custom-call | flops 34359738368 | bytes 73400320 | tf_op jit(solution)/shard_map/forward_gather/pallas_call | solution.py:502
  871.4 58.7 %forward_last.1 = (bf16[16,256,1024]{2,1,0:T(8,128)(2,1)}, bf16[2048,4096]{1,0:T(8,128)(2,1)}, f32[2048,4096]{1,0:T(8,128)}, f32[2048,1024]{1,0:T(8,128)}, bf16[2048,1024]{1,0:T(8,128)(2,1)}, /*index=5*/f32[8,128]{1,0:T(8,128)}) custom-call(bf16[2048,1024]{1,0:T(8,128)(2,1)} %get-tuple-element.162.refs_0_.h_hbm, ...), custom_call_target="tpu_custom_call", output_to_operand_aliasing={{0}: (2, {})} | custom-call | flops 34359738368 | bytes 73400320 | tf_op jit(solution)/shard_map/forward_last/pallas_call | solution.py:502
  930.1 70.5 %backward.9 = (f32[2048,1024]{1,0:T(8,128)}, bf16[2048,1024]{1,0:T(8,128)(2,1)}, f32[4,64,4096]{2,1,0:T(8,128)}, f32[4,1024,256]{2,1,0:T(8,128)}) custom-call(bf16[2048,1024]{1,0:T(8,128)(2,1)} %get-tuple-element.166.rb_ref, bf16[4096,1024]{1,0:T(8,128)(2,1)} %bitcast.47, bf16[2048,4096]{1,0:T(8,128)(2,1)} %get-tuple-element.168.a_hbm, ...), custom_call_target="tpu_custom_call" | custom-call | flops 51539607552 | bytes 104857600 | tf_op jit(solution)/shard_map/backward/pallas_call | solution.py:824
  1000.6 70.2 %backward.10 = (f32[2048,1024]{1,0:T(8,128)}, bf16[2048,1024]{1,0:T(8,128)(2,1)}, f32[4,64,4096]{2,1,0:T(8,128)}, f32[4,1024,256]{2,1,0:T(8,128)}) custom-call(bf16[2048,1024]{1,0:T(8,128)(2,1)} %get-tuple-element.171.rb_ref, bf16[4096,1024]{1,0:T(8,128)(2,1)} %bitcast.45, bf16[2048,4096]{1,0:T(8,128)(2,1)} %get-tuple-element.173.a_hbm, ...), custom_call_target="tpu_custom_call" | custom-call | flops 51539607552 | bytes 104857600 | tf_op jit(solution)/shard_map/backward/pallas_call | solution.py:824
  1070.8 70.2 %backward.11 = (f32[2048,1024]{1,0:T(8,128)}, bf16[2048,1024]{1,0:T(8,128)(2,1)}, f32[4,64,4096]{2,1,0:T(8,128)}, f32[4,1024,256]{2,1,0:T(8,128)}) custom-call(bf16[2048,1024]{1,0:T(8,128)(2,1)} %get-tuple-element.176.rb_ref, bf16[4096,1024]{1,0:T(8,128)(2,1)} %bitcast.43, bf16[2048,4096]{1,0:T(8,128)(2,1)} %get-tuple-element.178.a_hbm, ...), custom_call_target="tpu_custom_call" | custom-call | flops 51539607552 | bytes 104857600 | tf_op jit(solution)/shard_map/backward/pallas_call | solution.py:824
  1141.1 61.2 %backward_first.3 = (f32[4,64,4096]{2,1,0:T(8,128)}, f32[4,1024,256]{2,1,0:T(8,128)}, f32[8,128]{1,0:T(8,128)}) custom-call(bf16[2048,1024]{1,0:T(8,128)(2,1)} %get-tuple-element.181.rb_ref, bf16[4096,1024]{1,0:T(8,128)(2,1)} %bitcast.23, bf16[2048,4096]{1,0:T(8,128)(2,1)} %get-tuple-element.183.a_hbm, f32[2048,4096]{1,0:T(8,128)} %get-tuple-element.184.d_hbm, ...), custom_call_target="tpu_custom_call" | custom-call | flops 51539607552 | bytes 104857600 | tf_op jit(solution)/shard_map/backward_first/pallas_call | solution.py:824
  1202.3 1.3 reduce_sum.9
  1204.2 17.8 %update.1 = (f32[4,64,4096]{2,1,0:T(8,128)}, f32[4,256,1024]{2,1,0:T(8,128)}) custom-call(f32[4,64,4096]{2,1,0:T(8,128)} %get-tuple-element.186.refs_0_, f32[4,64,4096]{2,1,0:T(8,128)} %get-tuple-element.187.refs_1_, f32[4,64,4096]{2,1,0:T(8,128)} %get-tuple-element.188.refs_2_, f32[4,64,4096]{2,1,0:T(8,128)} %get-tuple-element.189.refs_3_, ...), custom_call_target="tpu_custom_call" | custom-call | tf_op jit(solution)/shard_map/update/pallas_call | solution.py:957
